TPU v7x, 128 devices: a whole 4x4x4 slice. The times are simulated.
128 devices in a mesh: chain: 32 (over x_hi, y, z), group: 4 (over x_lo, core).
Axes of the slice: x: 4 (x_hi: 2, x_lo: 2; x = x_hi * 2 + x_lo), y: 4, z: 4, core: 2. Of those that a mesh axis runs over, the one named last changes fastest.
Arguments:
- site_tensors: bfloat16 [4, 32, 16, 256, 2, 256], P('group', 'chain')
- bond_weights: float32 [4, 32, 16, 256], P('group', 'chain'), may hold values from 0.5 to 1.5
- sector_sizes: int32 [4, 32, 16], P('group', 'chain'), may hold values from 192 to 256, as said below
- kept_ranks: int32 [4, 32, 16], P('group', 'chain'), may hold values from 128 to 256, as said below
- sketches: bfloat16 [16, 512, 256], replicated, may hold values from -6 to 6
- gate_ends: float32 [2], replicated, may hold values from 0.5 to 1.5
- gate_pair: float32 [3], replicated, may hold values from -0.4 to 0.4
Outputs:
- updated_sites: bfloat16 [4, 32, 16, 256, 2, 256], P('group', 'chain')
Inputs may be any that keep to these rules, and one draw needn't show every extreme that they name: `sector_sizes`: every bond has one charge sector, the same for all bonds of a draw, of size 256. `kept_ranks`: A kept rank of sector q of bond n is at most the size of sector q of bonds n - 1, n and n + 1 (bonds outside the MPS count as 256); in the sector of size 256 it equals 256.
All inputs are finite; a program needn't handle non-finite values.
Results may differ from a plain program's by a relative error of at most 0.0088.
Values may be sent and summed in bfloat16 or wider, within the bound.
No kernel may reach another device: no remote copies, remote signals or barrier semaphores. Data moves between devices by JAX's collectives and lax.ppermute only.
A program may use at most 192 MiB of HBM per device.

v0:
```python
import functools

import jax
import jax.numpy as jnp
from jax import lax
from jax.experimental import pallas as pl
from jax.experimental.pallas import tpu as pltpu
from jax.sharding import PartitionSpec as P

f32 = jnp.float32
bf16 = jnp.bfloat16


BATCH = 4
LEAF = 32
PANELS = 8
LANES = 128
SIZE = 256


def split(x):
    high = x.astype(bf16)
    return high, (x - high.astype(f32)).astype(bf16)


def invert_leaf(d):
    lane = lax.broadcasted_iota(jnp.int32, (8, LANES), 1)
    sub = lax.broadcasted_iota(jnp.int32, (8, LANES), 0)
    segment = (lane // LEAF) * LEAF
    tiles = LEAF // 8
    rows = [d[8 * t : 8 * t + 8, :] for t in range(tiles)]
    cols = [
        [
            jnp.take_along_axis(rows[t], segment + j, axis=1) if t >= j // 8 else None
            for t in range(tiles)
        ]
        for j in range(LEAF)
    ]
    inverse = [((lane - segment) == (sub + 8 * t)).astype(f32) for t in range(tiles)]
    pivots = [jnp.ones((8, LANES), f32) for _ in range(tiles)]

    def row(v, r):
        return jnp.broadcast_to(v[r : r + 1, :], (8, LANES))

    for j in range(LEAF):
        top, r = j // 8, j % 8
        pivot = row(cols[j][top], r)
        reciprocal = 1.0 / pivot
        pivots[top] = jnp.where(sub == r, pivot, pivots[top])
        scaled = {t: cols[j][t] * reciprocal for t in range(top, tiles)}
        for i in range(j + 1, LEAF):
            factor = row(scaled[i // 8], i % 8)
            for t in range(i // 8, tiles):
                cols[i][t] = cols[i][t] - factor * cols[j][t]
        source = row(inverse[top], r)
        for t in range(top, tiles):
            factor = jnp.where(sub > r, scaled[t], 0.0) if t == top else scaled[t]
            inverse[t] = inverse[t] - factor * source
    return jnp.concatenate([inverse[t] * lax.rsqrt(pivots[t]) for t in range(tiles)], axis=0)


def block_weights(high, low, masks):
    high = jnp.concatenate([high * mask for mask in masks], axis=0)
    low = jnp.concatenate([low * mask for mask in masks], axis=0)
    upper = jnp.concatenate([high, high], axis=1)
    lower = jnp.concatenate([low, jnp.zeros_like(low)], axis=1)
    return jnp.concatenate([upper, lower], axis=0)


def times_transposed(x, weights):
    out = lax.dot_general(x, weights, (((1,), (1,)), ((), ())), preferred_element_type=f32)
    return out[:, :LANES] + out[:, LANES:]


def invert_factor(a_ref, x_ref):
    lane = lax.broadcasted_iota(jnp.int32, (LEAF, LANES), 1)
    sub = lax.broadcasted_iota(jnp.int32, (LEAF, LANES), 0)
    eye = ((lane % LEAF) == sub).astype(f32)
    masks = [((lane // LEAF) == b).astype(f32).astype(bf16) for b in range(BATCH)]

    def weights_of(rows, ks):
        return jnp.concatenate(
            [
                block_weights(
                    x_ref[rows, k * SIZE : k * SIZE + LANES],
                    x_ref[rows, k * SIZE + LANES : (k + 1) * SIZE],
                    masks,
                )
                for k in ks
            ],
            axis=1,
        )

    partial = None
    for j in range(PANELS):
        start = j * LEAF
        block = slice(start, start + LEAF)
        col = a_ref[j]
        if j:
            last = slice((j - 1) * SIZE, j * SIZE)
            if partial is not None:
                col = col - partial
            col = col - times_transposed(x_ref[:, last], weights_of(block, [j - 1]))
            x_ref[block, : j * SIZE] = jnp.zeros((LEAF, j * SIZE), bf16)
            if j < PANELS - 1:
                following = slice(start + LEAF, start + 2 * LEAF)
                partial = times_transposed(
                    x_ref[:, : j * SIZE], weights_of(following, range(j))
                )
        inverse = invert_leaf(col[block])
        col = jnp.concatenate(
            [part for part in (col[:start], eye, col[start + LEAF :]) if part.shape[0]], axis=0
        )
        col = times_transposed(
            jnp.concatenate(split(col), axis=1), block_weights(*split(inverse), masks)
        )
        x_ref[:, j * SIZE : (j + 1) * SIZE] = jnp.concatenate(split(col), axis=1)


UPPER, LOWER = slice(0, SIZE), slice(SIZE, 2 * SIZE)
CONTRACT_ROWS = (((0,), (0,)), ((), ()))


def dot(a, b):
    return jnp.dot(a, b, preferred_element_type=f32)


def lines_of(lane_block, s):
    return pl.ds(2 * lane_block + s, SIZE, stride=4)


def lanes_of(lane_block):
    return slice(lane_block * LANES, (lane_block + 1) * LANES)


def column_of(line):
    return jnp.transpose(jnp.broadcast_to(line, (LANES, SIZE)))


def weigh(t, role, own, got, scale, left, right, wide):
    is_right = role[0] == 1
    q = role[1] - 1 + t
    own_wide = own[jnp.clip(q, 0, 15) - role[2]].astype(f32)
    got_wide = got[...].astype(f32)
    wide[0] = jnp.where(is_right, got_wide, own_wide)
    wide[1] = jnp.where(is_right, own_wide, got_wide)
    left_rows = column_of(scale[0, q + 1])
    right_rows = column_of(scale[1, q + 1])
    for s in range(2):
        col = scale[2, q + s + 1]
        for jb in range(2):
            lines, lanes = lines_of(jb, s), lanes_of(jb)
            left[s, :, lanes] = (wide[0, lines, :] * left_rows).astype(bf16)
            right[s, :, lanes] = ((wide[1, lines, :] * right_rows) * col[:, lanes]).astype(bf16)


def sample(gates, kept, sketch, left, before, right, right_before, right_after, mixed, samp, gram):
    g0, g1, p0, p1, p2 = [gates[i] for i in range(5)]
    mixed[UPPER, UPPER] = (g0 * dot(left[0], right[0])).astype(bf16)
    mixed[UPPER, LOWER] = (p0 * dot(left[0], right[1]) + p2 * dot(left[1], right_after)).astype(bf16)
    mixed[LOWER, UPPER] = (
        p2 * dot(before[0], right_before) + p1 * dot(before[1], right[0])
    ).astype(bf16)
    mixed[LOWER, LOWER] = (g1 * dot(before[1], right[1])).astype(bf16)
    keep = lax.broadcasted_iota(jnp.int32, (1, SIZE), 1) < kept
    sampled = jnp.where(keep, dot(mixed[...], sketch), 0.0)
    high, low = split(sampled)
    samp[0] = high
    samp[1] = low
    shift = 0.01 * jnp.sum(sampled * sampled) / SIZE
    hh = lax.dot_general(high, high, CONTRACT_ROWS, preferred_element_type=f32)
    hl = lax.dot_general(high, low, CONTRACT_ROWS, preferred_element_type=f32)
    rows = lax.broadcasted_iota(jnp.int32, (SIZE, SIZE), 0)
    eye = rows == lax.broadcasted_iota(jnp.int32, (SIZE, SIZE), 1)
    added = jnp.where(keep, 0.0, 1.0) + shift
    gram[...] = (hh + (hl + jnp.transpose(hl))) + jnp.where(eye, added, 0.0)


def rolled(value, segments):
    shift = (segments * LEAF) % LANES
    return pltpu.roll(value, shift, axis=1) if shift else value


def gather_lanes(pieces):
    segment = lax.broadcasted_iota(jnp.int32, (1, LANES), 1) // LEAF
    out = pieces[0]
    for i in range(1, BATCH):
        out = jnp.where(segment == i, pieces[i], out)
    return out


def solve(gram, samp, scaled, a_ref, x_ref):
    for k in range(PANELS):
        rows = slice(k * LEAF, SIZE)
        lanes = lanes_of(k // 4)
        a_ref[k, rows, :] = gather_lanes(
            [rolled(gram[b][rows, lanes], b - k % 4) for b in range(BATCH)]
        )
        if k:
            a_ref[k, : k * LEAF, :] = jnp.zeros((k * LEAF, LANES), f32)

    invert_factor(a_ref, x_ref)

    def factor(b, offset):
        halves = []
        for g in range(2):
            panels = [
                rolled(x_ref[:, k * SIZE + offset : k * SIZE + offset + LANES], k % 4 - b)
                for k in range(4 * g, 4 * g + 4)
            ]
            halves.append(gather_lanes(panels))
        return jnp.concatenate(halves, axis=1)

    for b in range(BATCH):
        high, low = factor(b, 0), factor(b, LANES)
        solved = dot(samp[b][0], high) + (dot(samp[b][0], low) + dot(samp[b][1], high))
        scaled[b] = (solved * 16.0).astype(bf16)


def deliver(role, scaled, mixed, wide, ready, msg, out, sems):
    is_right = role[0] == 1
    copies = []
    for b in range(BATCH):
        right_part = lax.dot_general(
            scaled[b], mixed[b][...], CONTRACT_ROWS, preferred_element_type=f32
        ) * (1.0 / SIZE)
        left_wide, right_wide = wide.at[2 * (b % 2)], wide.at[2 * (b % 2) + 1]
        for s in range(2):
            half = scaled[b, UPPER, :] if s == 0 else scaled[b + 1, LOWER, :]
            for jb in range(2):
                lines = lines_of(jb, s)
                left_wide[lines, :] = half[:, lanes_of(jb)].astype(f32)
                right_wide[lines, :] = right_part[:, lanes_of(2 * s + jb)]
        left_site = left_wide[...]
        right_site = right_wide[...]
        msg[b] = jnp.where(is_right, left_site, right_site).astype(bf16)
        ready[b] = jnp.where(is_right, right_site, left_site).astype(bf16)
        copies.append(pltpu.make_async_copy(ready.at[b], out.at[role[1] + b], sems.at[b]))
        copies[-1].start()
    return copies


def early_kernel(role, gates, kept, own, got_0, got, scale, sketch, *refs):
    mixed, samp, gram, edge, left_w, right_w, wide = refs

    def step(t, loop):
        at = jnp.minimum(t - 2, 2)
        weigh(t, role, own, got.at[at], scale, left_w.at[t], right_w.at[t], wide)
        return loop

    weigh(1, role, own, got_0.at[0], scale, left_w.at[1], right_w.at[1], wide)
    lax.fori_loop(2, 6, step, 0)
    for s in range(2):
        edge[s] = left_w[1, s]
        edge[2 + s] = right_w[1, s]
    edge[4] = right_w[2, 0]
    below = role[1] - 5
    wide[0] = got[2].astype(f32)
    rows = column_of(scale[1, below + 1])
    col = scale[2, below + 2]
    for jb in range(2):
        lanes = lanes_of(jb)
        edge[5, :, lanes] = ((wide[0, lines_of(jb, 1), :] * rows) * col[:, lanes]).astype(bf16)
    for b in range(1, BATCH):
        t = b + 1
        sample(
            gates,
            kept[role[1] + b],
            sketch[b],
            (left_w[t, 0], left_w[t, 1]),
            (left_w[t - 1, 0], left_w[t - 1, 1]),
            (right_w[t, 0], right_w[t, 1]),
            right_w[t - 1, 1],
            right_w[t + 1, 0],
            mixed.at[b - 1],
            samp.at[b - 1],
            gram.at[b - 1],
        )


def first_kernel(role, gates, kept, own, got, scale, sketch, *refs):
    (mixed_e, samp_e, gram_e, edge, msg, out, carry), refs = refs[:7], refs[7:]
    mixed, samp, gram, scaled, a_ref, x_ref, wide, ready, sems = refs
    left, right = carry.at[pl.ds(1, 2)], carry.at[pl.ds(3, 2)]
    weigh(0, role, own, got.at[0], scale, left, right, wide)
    sample(
        gates,
        kept[role[1]],
        sketch[0],
        (edge[0], edge[1]),
        (left[0], left[1]),
        (edge[2], edge[3]),
        right[1],
        edge[4],
        mixed,
        samp,
        gram,
    )
    mixed = [mixed] + [mixed_e.at[b] for b in range(BATCH - 1)]
    samp = [samp] + [samp_e.at[b] for b in range(BATCH - 1)]
    gram = [gram] + [gram_e.at[b] for b in range(BATCH - 1)]
    solve(gram, samp, scaled, a_ref, x_ref)
    scaled[BATCH, LOWER, :] = jnp.zeros((SIZE, SIZE), bf16)
    carry[0] = scaled[0, LOWER, :]
    for copy in deliver(role, scaled, mixed, wide, ready, msg, out, sems):
        copy.wait()


def second_kernel(role, gates, kept, own, got, scale, sketch, *refs):
    (edge, carry, _, msg, out, merge), refs = refs[:6], refs[6:]
    left_w, right_w, mixed, samp, gram, scaled, a_ref, x_ref, wide = refs[:9]
    ready, sems = refs[9:]

    def step(t, loop):
        at = jnp.maximum(t - 1, 0)
        weigh(t, role, own, got.at[at], scale, left_w.at[t], right_w.at[t], wide)
        return loop

    lax.fori_loop(0, 4, step, 0)
    right_w[0, 1] = edge[5]
    for s in range(2):
        left_w[4, s] = carry[1 + s]
        right_w[4, s] = carry[3 + s]
    right_w[5, 0] = edge[2]
    for b in range(BATCH):
        t = b + 1
        sample(
            gates,
            kept[role[1] + b],
            sketch[b],
            (left_w[t, 0], left_w[t, 1]),
            (left_w[b, 0], left_w[b, 1]),
            (right_w[t, 0], right_w[t, 1]),
            right_w[b, 1],
            right_w[t + 1, 0],
            mixed.at[b],
            samp.at[b],
            gram.at[b],
        )
    every = range(BATCH)
    solve([gram.at[b] for b in every], [samp.at[b] for b in every], scaled, a_ref, x_ref)
    scaled[BATCH, LOWER, :] = carry[0]
    copies = deliver(
        role, scaled, [mixed.at[b] for b in every], wide, ready, msg, out, sems
    )
    used = jnp.where(role[0] == 1, 0.0, 1.0)
    for jb in range(2):
        value = scaled[0, LOWER, lanes_of(jb)].astype(f32)
        wide[0, lines_of(jb, 0), :] = jnp.zeros((SIZE, LANES), f32)
        wide[0, lines_of(jb, 1), :] = value * used
    merge[...] = wide[0].astype(bf16)
    for copy in copies:
        copy.wait()


def in_hbm(x):
    return pltpu.with_memory_space_constraint(x, pltpu.HBM)


def shaped(*shape, dtype=bf16):
    return jax.ShapeDtypeStruct(shape, dtype)


def run(kernel, operands, specs, outs, out_specs, scratch, aliases=None, mib=20):
    return pl.pallas_call(
        kernel,
        out_shape=outs,
        in_specs=specs,
        out_specs=out_specs,
        scratch_shapes=scratch,
        input_output_aliases=aliases or {},
        compiler_params=pltpu.CompilerParams(vmem_limit_bytes=mib * 2**20),
        cost_estimate=pl.CostEstimate(
            flops=mib * 500_000_000, bytes_accessed=8_000_000, transcendentals=0
        ),
    )(*operands)


SMEM = pl.BlockSpec(memory_space=pltpu.SMEM)
VMEM = pl.BlockSpec(memory_space=pltpu.VMEM)
HBM = pl.BlockSpec(memory_space=pltpu.HBM)
SECTOR = (4 * SIZE, LANES)


def factor_scratch():
    return [
        pltpu.VMEM((BATCH + 1, 2 * SIZE, SIZE), bf16),
        pltpu.VMEM((PANELS, SIZE, LANES), f32),
        pltpu.VMEM((SIZE, PANELS * SIZE), bf16),
        pltpu.VMEM((4, *SECTOR), f32),
    ]


def sample_shapes(make, *lead):
    return [
        make((*lead, 2 * SIZE, 2 * SIZE), bf16),
        make((*lead, 2, 2 * SIZE, SIZE), bf16),
        make((*lead, SIZE, SIZE), f32),
    ]


def early(role, gates, kept, own, got_0, got, scale, sketch):
    return run(
        early_kernel,
        (role, gates, kept, own, got_0, got, scale, sketch),
        [SMEM] * 3 + [VMEM] * 5,
        sample_shapes(jax.ShapeDtypeStruct, BATCH - 1) + [shaped(6, SIZE, SIZE)],
        [VMEM] * 4,
        [
            pltpu.VMEM((6, 2, SIZE, SIZE), bf16),
            pltpu.VMEM((6, 2, SIZE, SIZE), bf16),
            pltpu.VMEM((2, *SECTOR), f32),
        ],
    )


def first_half(role, gates, kept, own, got, scale, sketch, parts):
    return run(
        first_kernel,
        (role, gates, kept, own, got, scale, sketch, *parts),
        [SMEM] * 3 + [VMEM] * 8,
        [shaped(BATCH, *SECTOR), pltpu.HBM((16, *SECTOR), bf16), shaped(5, SIZE, SIZE)],
        [VMEM, HBM, VMEM],
        sample_shapes(pltpu.VMEM)
        + factor_scratch()
        + [pltpu.VMEM((BATCH, *SECTOR), bf16), pltpu.SemaphoreType.DMA((BATCH,))],
    )


def second_half(role, gates, kept, own, got, scale, sketch, edge, carry, out):
    return run(
        second_kernel,
        (role, gates, kept, own, got, scale, sketch, edge, carry, out),
        [SMEM] * 3 + [VMEM] * 6 + [HBM],
        [shaped(BATCH, *SECTOR), pltpu.HBM((16, *SECTOR), bf16), shaped(*SECTOR)],
        [VMEM, HBM, VMEM],
        [pltpu.VMEM((6, 2, SIZE, SIZE), bf16), pltpu.VMEM((6, 2, SIZE, SIZE), bf16)]
        + sample_shapes(pltpu.VMEM, BATCH)
        + factor_scratch()
        + [
            pltpu.VMEM((BATCH, *SECTOR), bf16),
            pltpu.SemaphoreType.DMA((BATCH,)),
        ],
        aliases={9: 1},
    )


def fetch_kernel(at, own, out, sem):
    copy = pltpu.make_async_copy(own.at[at[0]], out.at[0], sem)
    copy.start()
    copy.wait()


def fetch(at, own):
    return run(
        fetch_kernel,
        (jnp.reshape(at, (1,)), in_hbm(own)),
        [SMEM, HBM],
        [shaped(1, *SECTOR)],
        [VMEM],
        [pltpu.SemaphoreType.DMA],
        mib=1,
    )[0]


def pack_kernel(role, own, out, low, both, sems):
    flag = role[0]
    copies = [
        pltpu.make_async_copy(own.at[7 + 8 * flag], both.at[0], sems.at[0]),
        pltpu.make_async_copy(own.at[7], both.at[1], sems.at[1]),
        pltpu.make_async_copy(own.at[pl.ds(5 + 8 * flag, 2)], out.at[pl.ds(0, 2)], sems.at[2]),
        pltpu.make_async_copy(own.at[3 + 8 * flag], low.at[0], sems.at[3]),
    ]
    for copy in copies:
        copy.start()
    copies[0].wait()
    copies[1].wait()
    is_odd = lax.broadcasted_iota(jnp.int32, SECTOR, 0) % 2 == 1
    out[2] = jnp.where(is_odd, both[1].astype(f32), both[0].astype(f32)).astype(bf16)
    copies[2].wait()
    copies[3].wait()


def pack(role, own):
    return run(
        pack_kernel,
        (role, in_hbm(own)),
        [SMEM, HBM],
        [shaped(3, *SECTOR), shaped(1, *SECTOR)],
        [VMEM] * 2,
        [pltpu.VMEM((2, *SECTOR), bf16), pltpu.SemaphoreType.DMA((4,))],
        mib=2,
    )


def place_kernel(merged, at, block, *refs):
    if merged:
        merge, _, out, last, sems = refs
    else:
        _, out, sems = refs
    count = block.shape[0]
    copies = []
    for b in range(count):
        source = block.at[b]
        if merged and b == count - 1:
            last[...] = block[b] + merge[...]
            source = last
        copies.append(pltpu.make_async_copy(source, out.at[at[0] + b], sems.at[b]))
        copies[-1].start()
    for copy in copies:
        copy.wait()


def place(out, block, at, merge=None):
    smem = pl.BlockSpec(memory_space=pltpu.SMEM)
    vmem = pl.BlockSpec(memory_space=pltpu.VMEM)
    hbm = pl.BlockSpec(memory_space=pltpu.HBM)
    operands = (jnp.reshape(at, (1,)), block) + (() if merge is None else (merge,)) + (out,)
    scratch = [] if merge is None else [pltpu.VMEM(merge.shape, bf16)]
    return pl.pallas_call(
        functools.partial(place_kernel, merge is not None),
        out_shape=pltpu.HBM(out.shape, out.dtype),
        in_specs=[smem] + [vmem] * (len(operands) - 2) + [hbm],
        out_specs=hbm,
        scratch_shapes=scratch + [pltpu.SemaphoreType.DMA((block.shape[0],))],
        input_output_aliases={len(operands) - 1: 0},
        compiler_params=pltpu.CompilerParams(vmem_limit_bytes=8 * 2**20),
        cost_estimate=pl.CostEstimate(flops=1000000, bytes_accessed=2_000_000, transcendentals=0),
        name="place",
    )(*operands)


def to_lines(x):
    n = x.shape[0]
    return x.reshape(n, SIZE, 2, 2, LANES).transpose(0, 1, 3, 2, 4).reshape(n, 4 * SIZE, LANES)


def from_lines(x):
    n = x.shape[0]
    return x.reshape(n, SIZE, 2, 2, LANES).transpose(0, 1, 3, 2, 4).reshape(n, SIZE, 2, SIZE)


def shards(site_tensors, bond_weights, sector_sizes, kept_ranks, sketches, gate_ends, gate_pair):
    chain = lax.axis_size("chain")
    count = lax.axis_size("group") * chain
    site = lax.axis_index("group") * chain + lax.axis_index("chain")
    is_right = site % 2 == 1

    def swapped(value):
        return lax.ppermute(value, "chain", [(i, i ^ 1) for i in range(chain)])

    def onward(value, by):
        def place(n):
            return n % chain * (count // chain) + n // chain

        pairs = [(place(i), place(i + by)) for i in range(1, count, 2) if i + by < count]
        return lax.ppermute(value, ("chain", "group"), pairs)

    own = to_lines(site_tensors[0, 0])
    sectors = own.shape[0]
    flag = is_right.astype(jnp.int32)

    def window(array, start, size):
        return lax.dynamic_slice_in_dim(array, start, size, 0)

    got_0 = swapped(fetch(4 + 8 * flag, own))
    outgoing, outgoing_low = pack(jnp.reshape(flag, (1,)), own)
    got_a = swapped(outgoing)
    got_low = swapped(outgoing_low)

    column = lax.broadcasted_iota(jnp.int32, (sectors, SIZE), 1)
    lam = bond_weights[0, 0] * (column < sector_sizes[0, 0][:, None]).astype(f32)
    kept_line = jnp.pad(kept_ranks[0, 0].astype(f32)[None, :], ((0, 7), (0, SIZE - sectors)))
    packed = jnp.concatenate([lam, kept_line], axis=0)
    other = swapped(packed)
    before_left = onward(lam, 1)
    before_right = onward(lam, 2)
    got_b = swapped(window(own, 8 * flag, 3))

    lam_prev = jnp.where(is_right, before_right, before_left)
    lam_prev = jnp.where(site < 2, jnp.ones_like(lam), lam_prev)
    lam_mid = jnp.where(is_right, other[:sectors], lam)
    lam_next = jnp.where(is_right, lam, other[:sectors])
    scale = jnp.pad(jnp.stack([lam_prev, lam_mid, lam_next]), ((0, 0), (1, 7), (0, 0)))
    scale = scale[:, :, None, :]
    kept = jnp.where(is_right, other[sectors, :sectors], packed[sectors, :sectors]).astype(jnp.int32)
    gates = jnp.concatenate([gate_ends, 1.0 + gate_pair[:2], gate_pair[2:]])
    first_a = 12 - 8 * flag
    first_b = 8 - 8 * flag
    own_a = 10 - 7 * flag
    own_b = 7 - 7 * flag
    role_a = jnp.stack([flag, first_a, own_a])
    role_b = jnp.stack([flag, first_b, own_b])

    own_win = window(own, own_a, 6)
    sketch_win = window(sketches, first_a, BATCH)
    parts = early(role_a, gates, kept, own_win, got_0, got_a, scale, sketch_win)
    msg_a, out, carry = first_half(
        role_a, gates, kept, own_win, got_low, scale, sketch_win, parts
    )
    back_a = swapped(msg_a)
    own_win = window(own, own_b, BATCH)
    sketch_win = window(sketches, first_b, BATCH)
    msg_b, out, merge = second_half(
        role_b, gates, kept, own_win, got_b, scale, sketch_win, parts[3], carry, out
    )
    back_b = swapped(msg_b)

    back_at = 8 * flag
    out = place(out, back_a, back_at + 4, merge)
    out = place(out, back_b, back_at)
    return from_lines(out)[None, None]


def solution(mesh):
    return jax.shard_map(
        shards,
        mesh=mesh,
        in_specs=(
            P("group", "chain", None, None, None, None),
            P("group", "chain", None, None),
            P("group", "chain", None),
            P("group", "chain", None),
            P(),
            P(),
            P(),
        ),
        out_specs=P("group", "chain", None, None, None, None),
        check_vma=False,
    )
```

profile of v0, /device:TPU:1, one launch (start us, length us, event | category | flops | bytes accessed | tf_op | source)
XLA Modules:
  0.0 102.1 jit_solution(8492968457669474118)
XLA Ops:
  0.0 0.8 bitcast_select_fusion
  0.8 0.7 collective-permute-start.2
  1.4 1.3 %collective-permute-start.3 = (f32[16,256]{1,0:T(8,128)S(1)}, f32[16,256]{1,0:T(8,128)S(1)}, u32[]{:S(2)}, u32[]{:S(2)}) collective-permute-start(f32[16,256]{1,0:T(8,128)S(1)} %bitcast_select_fusion), channel_id=1, source_target_pairs={{4,8},{12,16},{20,24},{28,32},{36,40},{44,48},{52,56},{60,64},{68,... | collective-permute-start | bytes 49160 | tf_op jit(solution)/shard_map/ppermute | solution.py:557
  2.8 0.0 copy-start.6
  2.8 0.0 copy-start.7
  2.8 2.2 %shard_map.74 = (bf16[3,1024,128]{2,1,0:T(8,128)(2,1)}, bf16[1,1024,128]{2,1,0:T(8,128)(2,1)S(1)}) custom-call(s32[1]{0:T(128)} %bitcast.1.role, bf16[16,1024,128]{2,1,0:T(8,128)(2,1)} %bitcast.36), custom_call_target="tpu_custom_call" | custom-call | flops 1000000000 | bytes 8000000 | tf_op jit(solution)/shard_map/pallas_call | solution.py:365
  5.0 6.5 %collective-permute-start.5 = (bf16[3,1024,128]{2,1,0:T(8,128)(2,1)}, bf16[3,1024,128]{2,1,0:T(8,128)(2,1)}, u32[]{:S(2)}, u32[]{:S(2)}) collective-permute-start(bf16[3,1024,128]{2,1,0:T(8,128)(2,1)} %get-tuple-element.17), channel_id=1, source_target_pairs={{0,4},{4,0},{8,12},{12,8},{16,20},{20,16},{24,28},{28,24},{32,36},... | collective-permute-start | bytes 2359304 | tf_op jit(solution)/shard_map/ppermute | solution.py:550
  11.5 1.0 shard_map.73
  12.5 0.1 collective-permute-start.4
  12.6 0.0 copy-done.6
  12.6 1.5 %collective-permute-start = (f32[24,256]{1,0:T(8,128)S(1)}, f32[24,256]{1,0:T(8,128)S(1)}, u32[]{:S(2)}, u32[]{:S(2)}) collective-permute-start(f32[24,256]{1,0:T(8,128)S(1)} %select_maximum_fusion.2), channel_id=1, source_target_pairs={{0,4},{4,0},{8,12},{12,8},{16,20},{20,16},{24,28},{28,24},{32,36},... | collective-permute-start | bytes 73736 | tf_op jit(solution)/shard_map/ppermute | solution.py:550
  14.1 0.0 copy-done.7
  14.1 0.6 slice.15
  14.7 2.1 %constant_dynamic-slice_fusion.3 = bf16[3,1024,128]{2,1,0:T(8,128)(2,1)} fusion(bf16[16,1024,128]{2,1,0:T(8,128)(2,1)} %bitcast.38, s32[]{:T(128)} %mul.18), kind=kLoop, calls=%fused_computation.15 | loop fusion | bytes 1572868 | tf_op jit(solution)/shard_map/dynamic_slice | solution.py:564
  16.8 0.0 copy-start.5
  16.8 0.0 copy-start.3
  16.8 0.0 copy-start.4
  16.8 1.6 %constant_dynamic-slice_fusion.1.own = bf16[6,1024,128]{2,1,0:T(8,128)(2,1)S(1)} fusion(bf16[16,1024,128]{2,1,0:T(8,128)(2,1)} %bitcast.39, s32[]{:T(128)S(6)} %select_n.61), kind=kLoop, calls=%fused_computation.13 | loop fusion | bytes 3145732 | tf_op jit(solution)/shard_map/dynamic_slice | solution.py:564
  18.3 2.3 %constant_dynamic-slice_fusion.4.own = bf16[4,1024,128]{2,1,0:T(8,128)(2,1)} fusion(bf16[16,1024,128]{2,1,0:T(8,128)(2,1)} %bitcast.40, s32[]{:T(128)S(6)} %select_n.53), kind=kLoop, calls=%fused_computation.16 | loop fusion | bytes 2097156 | tf_op jit(solution)/shard_map/dynamic_slice | solution.py:564
  20.6 0.1 pad_add_fusion.1.role
  20.7 0.1 pad_add_fusion.role
  20.8 2.6 %constant_dynamic-slice_fusion = (bf16[4,512,256]{2,1,0:T(8,128)(2,1)}, bf16[4,512,256]{2,1,0:T(8,128)(2,1)S(1)}) fusion(bf16[16,512,256]{2,1,0:T(8,128)(2,1)} %param.11, s32[]{:T(128)S(6)} %select_n.62, s32[]{:T(128)S(6)} %select_n.60), kind=kLoop, calls=%fused_computation.12 | loop fusion | bytes 4194312 | tf_op jit(solution)/shard_map/dynamic_slice | solution.py:564
  23.4 0.0 copy-done.5
  23.4 0.6 pad_maximum_fusion.gates
  24.1 0.0 collective-permute-done.2
  24.1 0.1 collective-permute-start.6
  24.1 0.0 collective-permute-done.3
  24.2 1.4 %collective-permute-start.1 = (bf16[3,1024,128]{2,1,0:T(8,128)(2,1)}, bf16[3,1024,128]{2,1,0:T(8,128)(2,1)S(1)}, u32[]{:S(2)}, u32[]{:S(2)}) collective-permute-start(bf16[3,1024,128]{2,1,0:T(8,128)(2,1)} %constant_dynamic-slice_fusion.3), channel_id=1, source_target_pairs={{0,4},{4,0},{8,12},{12,8},{16,20},{20,16},{24,28},{28,24},{32,36},... | collective-permute-start | bytes 2359304 | tf_op jit(solution)/shard_map/ppermute | solution.py:550
  25.6 9.2 %collective-permute-done = f32[24,256]{1,0:T(8,128)S(1)} collective-permute-done((f32[24,256]{1,0:T(8,128)S(1)}, f32[24,256]{1,0:T(8,128)S(1)}, u32[]{:S(2)}, u32[]{:S(2)}) %collective-permute-start) | collective-permute-done | bytes 24608 | tf_op jit(solution)/shard_map/ppermute | solution.py:550
  34.8 0.0 copy-done.3
  34.8 0.0 copy-done.4
  34.8 0.1 select_bitcast_fusion.1
  34.9 0.1 broadcast_in_dim.8.scale
  35.0 0.0 collective-permute-done.4.got_0
  35.0 0.0 collective-permute-done.5.got
  35.0 0.0 copy-start
  35.0 1.2 %copy-done = bf16[4,512,256]{2,1,0:T(8,128)(2,1)S(1)} copy-done((bf16[4,512,256]{2,1,0:T(8,128)(2,1)S(1)}, bf16[4,512,256]{2,1,0:T(8,128)(2,1)}, u32[]{:S(2)}) %copy-start) | copy-done | bytes 1048600
  36.2 0.0 copy-start.1
  36.2 5.1 %shard_map.75 = (bf16[3,512,512]{2,1,0:T(8,128)(2,1)S(1)}, bf16[3,2,512,256]{3,2,1,0:T(8,128)(2,1)S(1)}, f32[3,256,256]{2,1,0:T(8,128)S(1)}, bf16[6,256,256]{2,1,0:T(8,128)(2,1)S(1)}) custom-call(s32[3]{0:T(128)S(1)} %pad_add_fusion.1.role, f32[5]{0:T(128)S(1)} %pad_maximum_fusion.gates, s32[16]{0:T(128)S(1)} %fusion.1.kept, ...), custom_call_target="tpu_custom_call" | custom-call | flops 10000000000 | bytes 8000000 | tf_op jit(solution)/shard_map/pallas_call | solution.py:365
  41.4 0.0 collective-permute-done.6.got
  41.4 0.0 copy-done.1
  41.4 0.0 copy-start.2
  41.4 13.6 %shard_map.76 = (bf16[4,1024,128]{2,1,0:T(8,128)(2,1)S(1)}, bf16[16,1024,128]{2,1,0:T(8,128)(2,1)}, bf16[5,256,256]{2,1,0:T(8,128)(2,1)S(1)}) custom-call(s32[3]{0:T(128)S(1)} %pad_add_fusion.1.role, f32[5]{0:T(128)S(1)} %pad_maximum_fusion.gates, s32[16]{0:T(128)S(1)} %fusion.1.kept, bf16[6,1024,128]{2,1,0:T(8,128)(2,1)S(1)} %constant_dynamic-slice_fusion.1.own, ...), custom_call_target="tpu_custom_call" | custom-call | flops 10000000000 | bytes 8000000 | tf_op jit(solution)/shard_map/pallas_call | solution.py:365
  55.0 1.3 %collective-permute-start.8 = (bf16[4,1024,128]{2,1,0:T(8,128)(2,1)S(1)}, bf16[4,1024,128]{2,1,0:T(8,128)(2,1)S(1)}, u32[]{:S(2)}, u32[]{:S(2)}) collective-permute-start(bf16[4,1024,128]{2,1,0:T(8,128)(2,1)S(1)} %get-tuple-element.26), channel_id=1, source_target_pairs={{0,4},{4,0},{8,12},{12,8},{16,20},{20,16},{24,28},{28,24},{32,36},... | collective-permute-start | bytes 3145736 | tf_op jit(solution)/shard_map/ppermute | solution.py:550
  56.2 1.1 %collective-permute-done.1.got = bf16[3,1024,128]{2,1,0:T(8,128)(2,1)S(1)} collective-permute-done((bf16[3,1024,128]{2,1,0:T(8,128)(2,1)}, bf16[3,1024,128]{2,1,0:T(8,128)(2,1)S(1)}, u32[]{:S(2)}, u32[]{:S(2)}) %collective-permute-start.1) | collective-permute-done | bytes 786464 | tf_op jit(solution)/shard_map/ppermute | solution.py:550
  57.3 0.0 copy-done.2
  57.3 16.9 %shard_map.77 = (bf16[4,1024,128]{2,1,0:T(8,128)(2,1)S(1)}, bf16[16,1024,128]{2,1,0:T(8,128)(2,1)}, bf16[1024,128]{1,0:T(8,128)(2,1)S(1)}) custom-call(s32[3]{0:T(128)S(1)} %pad_add_fusion.role, f32[5]{0:T(128)S(1)} %pad_maximum_fusion.gates, s32[16]{0:T(128)S(1)} %fusion.1.kept, ...), custom_call_target="tpu_custom_call", output_to_operand_aliasing={{1}: (9, {})} | custom-call | flops 10000000000 | bytes 8000000 | tf_op jit(solution)/shard_map/pallas_call | solution.py:365
  74.2 1.3 %collective-permute-start.7 = (bf16[4,1024,128]{2,1,0:T(8,128)(2,1)S(1)}, bf16[4,1024,128]{2,1,0:T(8,128)(2,1)S(1)}, u32[]{:S(2)}, u32[]{:S(2)}) collective-permute-start(bf16[4,1024,128]{2,1,0:T(8,128)(2,1)S(1)} %get-tuple-element.25), channel_id=1, source_target_pairs={{0,4},{4,0},{8,12},{12,8},{16,20},{20,16},{24,28},{28,24},{32,36},... | collective-permute-start | bytes 3145736 | tf_op jit(solution)/shard_map/ppermute | solution.py:550
  75.5 2.9 %collective-permute-done.8.block = bf16[4,1024,128]{2,1,0:T(8,128)(2,1)S(1)} collective-permute-done((bf16[4,1024,128]{2,1,0:T(8,128)(2,1)S(1)}, bf16[4,1024,128]{2,1,0:T(8,128)(2,1)S(1)}, u32[]{:S(2)}, u32[]{:S(2)}) %collective-permute-start.8) | collective-permute-done | bytes 1048608 | tf_op jit(solution)/shard_map/ppermute | solution.py:550
  78.4 1.0 place.2.refs_0_
  79.4 21.5 %collective-permute-done.7.block = bf16[4,1024,128]{2,1,0:T(8,128)(2,1)S(1)} collective-permute-done((bf16[4,1024,128]{2,1,0:T(8,128)(2,1)S(1)}, bf16[4,1024,128]{2,1,0:T(8,128)(2,1)S(1)}, u32[]{:S(2)}, u32[]{:S(2)}) %collective-permute-start.7) | collective-permute-done | bytes 1048608 | tf_op jit(solution)/shard_map/ppermute | solution.py:550
  100.9 1.0 place.3
  (6 shorter events, 0.0 us)
Async XLA Ops:
  0.8 23.3 %collective-permute-start.2 = (f32[16,256]{1,0:T(8,128)S(1)}, f32[16,256]{1,0:T(8,128)S(1)}, u32[]{:S(2)}, u32[]{:S(2)}) collective-permute-start(f32[16,256]{1,0:T(8,128)S(1)} %bitcast_select_fusion), channel_id=1, source_target_pairs={{4,12},{12,20},{20,28},{28,36},{36,44},{44,52},{52,60},{60,68},{68... | collective-permute-start | bytes 49160 | tf_op jit(solution)/shard_map/ppermute | solution.py:557
  1.4 22.7 %collective-permute-start.3 = (f32[16,256]{1,0:T(8,128)S(1)}, f32[16,256]{1,0:T(8,128)S(1)}, u32[]{:S(2)}, u32[]{:S(2)}) collective-permute-start(f32[16,256]{1,0:T(8,128)S(1)} %bitcast_select_fusion), channel_id=1, source_target_pairs={{4,8},{12,16},{20,24},{28,32},{36,40},{44,48},{52,56},{60,64},{68,... | collective-permute-start | bytes 49160 | tf_op jit(solution)/shard_map/ppermute | solution.py:557
  2.8 9.8 %copy-start.6 = (s32[1,1,16]{2,1,0:T(1,128)S(1)}, s32[1,1,16]{2,1,0:T(1,128)}, u32[]{:S(2)}) copy-start(s32[1,1,16]{2,1,0:T(1,128)} %param.10) | copy-start | bytes 196
  2.8 11.3 %copy-start.7 = (f32[3]{0:T(128)S(1)}, f32[3]{0:T(128)}, u32[]{:S(2)}) copy-start(f32[3]{0:T(128)} %param.13) | copy-start | bytes 40
  5.0 30.0 %collective-permute-start.5 = (bf16[3,1024,128]{2,1,0:T(8,128)(2,1)}, bf16[3,1024,128]{2,1,0:T(8,128)(2,1)}, u32[]{:S(2)}, u32[]{:S(2)}) collective-permute-start(bf16[3,1024,128]{2,1,0:T(8,128)(2,1)} %get-tuple-element.17), channel_id=1, source_target_pairs={{0,4},{4,0},{8,12},{12,8},{16,20},{20,16},{24,28},{28,24},{32,36},... | collective-permute-start | bytes 2359304 | tf_op jit(solution)/shard_map/ppermute | solution.py:550
  12.5 22.5 %collective-permute-start.4 = (bf16[1,1024,128]{2,1,0:T(8,128)(2,1)S(1)}, bf16[1,1024,128]{2,1,0:T(8,128)(2,1)S(1)}, u32[]{:S(2)}, u32[]{:S(2)}) collective-permute-start(bf16[1,1024,128]{2,1,0:T(8,128)(2,1)S(1)} %shard_map.73), channel_id=1, source_target_pairs={{0,4},{4,0},{8,12},{12,8},{16,20},{20,16},{24,28},{28,24},{32,36},... | collective-permute-start | bytes 786440 | tf_op jit(solution)/shard_map/ppermute | solution.py:550
  12.6 22.2 %collective-permute-start = (f32[24,256]{1,0:T(8,128)S(1)}, f32[24,256]{1,0:T(8,128)S(1)}, u32[]{:S(2)}, u32[]{:S(2)}) collective-permute-start(f32[24,256]{1,0:T(8,128)S(1)} %select_maximum_fusion.2), channel_id=1, source_target_pairs={{0,4},{4,0},{8,12},{12,8},{16,20},{20,16},{24,28},{28,24},{32,36},... | collective-permute-start | bytes 73736 | tf_op jit(solution)/shard_map/ppermute | solution.py:550
  16.8 6.7 %copy-start.5 = (f32[2]{0:T(128)S(1)}, f32[2]{0:T(128)}, u32[]{:S(2)}) copy-start(f32[2]{0:T(128)} %param.12) | copy-start | bytes 28
  16.8 18.1 %copy-start.3 = (f32[1,1,16,256]{3,2,1,0:T(8,128)S(1)}, f32[1,1,16,256]{3,2,1,0:T(8,128)}, u32[]{:S(2)}) copy-start(f32[1,1,16,256]{3,2,1,0:T(8,128)} %param.8) | copy-start | bytes 49156
  16.8 18.1 %copy-start.4 = (s32[1,1,16]{2,1,0:T(1,128)S(1)}, s32[1,1,16]{2,1,0:T(1,128)}, u32[]{:S(2)}) copy-start(s32[1,1,16]{2,1,0:T(1,128)} %param.9) | copy-start | bytes 196
  24.1 17.3 %collective-permute-start.6 = (bf16[1,1024,128]{2,1,0:T(8,128)(2,1)S(1)}, bf16[1,1024,128]{2,1,0:T(8,128)(2,1)S(1)}, u32[]{:S(2)}, u32[]{:S(2)}) collective-permute-start(bf16[1,1024,128]{2,1,0:T(8,128)(2,1)S(1)} %get-tuple-element.19), channel_id=1, source_target_pairs={{0,4},{4,0},{8,12},{12,8},{16,20},{20,16},{24,28},{28,24},{32,36},... | collective-permute-start | bytes 786440 | tf_op jit(solution)/shard_map/ppermute | solution.py:550
  24.2 33.1 %collective-permute-start.1 = (bf16[3,1024,128]{2,1,0:T(8,128)(2,1)}, bf16[3,1024,128]{2,1,0:T(8,128)(2,1)S(1)}, u32[]{:S(2)}, u32[]{:S(2)}) collective-permute-start(bf16[3,1024,128]{2,1,0:T(8,128)(2,1)} %constant_dynamic-slice_fusion.3), channel_id=1, source_target_pairs={{0,4},{4,0},{8,12},{12,8},{16,20},{20,16},{24,28},{28,24},{32,36},... | collective-permute-start | bytes 2359304 | tf_op jit(solution)/shard_map/ppermute | solution.py:550
  35.0 1.2 %copy-start = (bf16[4,512,256]{2,1,0:T(8,128)(2,1)S(1)}, bf16[4,512,256]{2,1,0:T(8,128)(2,1)}, u32[]{:S(2)}) copy-start(bf16[4,512,256]{2,1,0:T(8,128)(2,1)} %get-tuple-element.29.sketch) | copy-start | bytes 3145732
  36.2 5.1 %copy-start.1 = (bf16[4,512,256]{2,1,0:T(8,128)(2,1)S(1)}, bf16[4,512,256]{2,1,0:T(8,128)(2,1)}, u32[]{:S(2)}) copy-start(bf16[4,512,256]{2,1,0:T(8,128)(2,1)} %get-tuple-element.29.sketch) | copy-start | bytes 3145732
  41.4 15.9 %copy-start.2 = (bf16[4,1024,128]{2,1,0:T(8,128)(2,1)S(1)}, bf16[4,1024,128]{2,1,0:T(8,128)(2,1)}, u32[]{:S(2)}) copy-start(bf16[4,1024,128]{2,1,0:T(8,128)(2,1)} %constant_dynamic-slice_fusion.4.own) | copy-start | bytes 3145732
  55.0 23.5 %collective-permute-start.8 = (bf16[4,1024,128]{2,1,0:T(8,128)(2,1)S(1)}, bf16[4,1024,128]{2,1,0:T(8,128)(2,1)S(1)}, u32[]{:S(2)}, u32[]{:S(2)}) collective-permute-start(bf16[4,1024,128]{2,1,0:T(8,128)(2,1)S(1)} %get-tuple-element.26), channel_id=1, source_target_pairs={{0,4},{4,0},{8,12},{12,8},{16,20},{20,16},{24,28},{28,24},{32,36},... | collective-permute-start | bytes 3145736 | tf_op jit(solution)/shard_map/ppermute | solution.py:550
  74.2 26.7 %collective-permute-start.7 = (bf16[4,1024,128]{2,1,0:T(8,128)(2,1)S(1)}, bf16[4,1024,128]{2,1,0:T(8,128)(2,1)S(1)}, u32[]{:S(2)}, u32[]{:S(2)}) collective-permute-start(bf16[4,1024,128]{2,1,0:T(8,128)(2,1)S(1)} %get-tuple-element.25), channel_id=1, source_target_pairs={{0,4},{4,0},{8,12},{12,8},{16,20},{20,16},{24,28},{28,24},{32,36},... | collective-permute-start | bytes 3145736 | tf_op jit(solution)/shard_map/ppermute | solution.py:550
where the time goes:
time: 104 us; the launch traced here: 102 us
  Pallas kernels  40.8 us (39%)
  waiting for transfers between devices  34.7 us (33%)
  starting transfers between devices  14.1 us (14%)
  local copies, waits for them, and re-layouts  10.5 us (10%)
  other arithmetic  1.7 us (2%)
    pallas_call x5, Pallas kernels, run(): pl.pallas_call(kernel, out_shape=outs, in_specs=specs, out_specs=out_spec...  38.8 us
    ppermute x7, waiting for transfers between devices, swapped(): return lax.ppermute(value, 'chain', [(i, i ^ 1) for i in range(chain)])  34.7 us
    ppermute x7, starting transfers between devices, swapped(): return lax.ppermute(value, 'chain', [(i, i ^ 1) for i in range(chain)])  12.1 us
    dynamic_slice x4, local copies, waits for them, and re-layouts, window(): return lax.dynamic_slice_in_dim(array, start, size, 0)  8.57 us
  transfers between devices with their start and end apart: 9, of which 4 were waited for; matrix products, arithmetic and copies ran while one was open for 10% of the time, Pallas kernels for 39%

commit v1 on v0

--- a/solution.py
+++ b/solution.py
@@ -244,18 +244,22 @@
     mixed, samp, gram, edge, left_w, right_w, wide = refs
 
     def step(t, loop):
-        at = jnp.minimum(t - 2, 2)
+        at = jnp.minimum(t - 3, 1)
         weigh(t, role, own, got.at[at], scale, left_w.at[t], right_w.at[t], wide)
         return loop
 
-    weigh(1, role, own, got_0.at[0], scale, left_w.at[1], right_w.at[1], wide)
-    lax.fori_loop(2, 6, step, 0)
+    def step_0(t, loop):
+        weigh(t, role, own, got_0.at[t - 1], scale, left_w.at[t], right_w.at[t], wide)
+        return loop
+
+    lax.fori_loop(1, 3, step_0, 0)
+    lax.fori_loop(3, 6, step, 0)
     for s in range(2):
         edge[s] = left_w[1, s]
         edge[2 + s] = right_w[1, s]
     edge[4] = right_w[2, 0]
     below = role[1] - 5
-    wide[0] = got[2].astype(f32)
+    wide[0] = got[1].astype(f32)
     rows = column_of(scale[1, below + 1])
     col = scale[2, below + 2]
     for jb in range(2):
@@ -446,7 +450,7 @@
 
 
 def fetch_kernel(at, own, out, sem):
-    copy = pltpu.make_async_copy(own.at[at[0]], out.at[0], sem)
+    copy = pltpu.make_async_copy(own.at[pl.ds(at[0], out.shape[0])], out, sem)
     copy.start()
     copy.wait()
 
@@ -456,7 +460,7 @@
         fetch_kernel,
         (jnp.reshape(at, (1,)), in_hbm(own)),
         [SMEM, HBM],
-        [shaped(1, *SECTOR)],
+        [shaped(2, *SECTOR)],
         [VMEM],
         [pltpu.SemaphoreType.DMA],
         mib=1,
@@ -468,7 +472,7 @@
     copies = [
         pltpu.make_async_copy(own.at[7 + 8 * flag], both.at[0], sems.at[0]),
         pltpu.make_async_copy(own.at[7], both.at[1], sems.at[1]),
-        pltpu.make_async_copy(own.at[pl.ds(5 + 8 * flag, 2)], out.at[pl.ds(0, 2)], sems.at[2]),
+        pltpu.make_async_copy(own.at[6 + 8 * flag], out.at[0], sems.at[2]),
         pltpu.make_async_copy(own.at[3 + 8 * flag], low.at[0], sems.at[3]),
     ]
     for copy in copies:
@@ -476,7 +480,7 @@
     copies[0].wait()
     copies[1].wait()
     is_odd = lax.broadcasted_iota(jnp.int32, SECTOR, 0) % 2 == 1
-    out[2] = jnp.where(is_odd, both[1].astype(f32), both[0].astype(f32)).astype(bf16)
+    out[1] = jnp.where(is_odd, both[1].astype(f32), both[0].astype(f32)).astype(bf16)
     copies[2].wait()
     copies[3].wait()
 
@@ -486,7 +490,7 @@
         pack_kernel,
         (role, in_hbm(own)),
         [SMEM, HBM],
-        [shaped(3, *SECTOR), shaped(1, *SECTOR)],
+        [shaped(2, *SECTOR), shaped(1, *SECTOR)],
         [VMEM] * 2,
         [pltpu.VMEM((2, *SECTOR), bf16), pltpu.SemaphoreType.DMA((4,))],
         mib=2,
@@ -549,11 +553,11 @@
     def swapped(value):
         return lax.ppermute(value, "chain", [(i, i ^ 1) for i in range(chain)])
 
-    def onward(value, by):
+    def onward(value):
         def place(n):
             return n % chain * (count // chain) + n // chain
 
-        pairs = [(place(i), place(i + by)) for i in range(1, count, 2) if i + by < count]
+        pairs = [(place(i), place(i + 1)) for i in range(1, count - 1, 2)]
         return lax.ppermute(value, ("chain", "group"), pairs)
 
     own = to_lines(site_tensors[0, 0])
@@ -564,26 +568,25 @@
         return lax.dynamic_slice_in_dim(array, start, size, 0)
 
     got_0 = swapped(fetch(4 + 8 * flag, own))
+    column = lax.broadcasted_iota(jnp.int32, (sectors, SIZE), 1)
+    lam = bond_weights[0, 0] * (column < sector_sizes[0, 0][:, None]).astype(f32)
+    before = onward(lam)
+    before = jnp.where(site < 2, jnp.ones_like(lam), before)
+    kept_line = jnp.pad(kept_ranks[0, 0].astype(f32)[None, :], ((0, 7), (0, SIZE - sectors)))
+    packed = jnp.concatenate([lam, before, kept_line], axis=0)
+    other = swapped(packed)
     outgoing, outgoing_low = pack(jnp.reshape(flag, (1,)), own)
     got_a = swapped(outgoing)
     got_low = swapped(outgoing_low)
-
-    column = lax.broadcasted_iota(jnp.int32, (sectors, SIZE), 1)
-    lam = bond_weights[0, 0] * (column < sector_sizes[0, 0][:, None]).astype(f32)
-    kept_line = jnp.pad(kept_ranks[0, 0].astype(f32)[None, :], ((0, 7), (0, SIZE - sectors)))
-    packed = jnp.concatenate([lam, kept_line], axis=0)
-    other = swapped(packed)
-    before_left = onward(lam, 1)
-    before_right = onward(lam, 2)
-    got_b = swapped(window(own, 8 * flag, 3))
-
-    lam_prev = jnp.where(is_right, before_right, before_left)
-    lam_prev = jnp.where(site < 2, jnp.ones_like(lam), lam_prev)
+    lam_prev = jnp.where(is_right, other[sectors : 2 * sectors], before)
     lam_mid = jnp.where(is_right, other[:sectors], lam)
     lam_next = jnp.where(is_right, lam, other[:sectors])
     scale = jnp.pad(jnp.stack([lam_prev, lam_mid, lam_next]), ((0, 0), (1, 7), (0, 0)))
     scale = scale[:, :, None, :]
-    kept = jnp.where(is_right, other[sectors, :sectors], packed[sectors, :sectors]).astype(jnp.int32)
+    kept = jnp.where(is_right, other[2 * sectors, :sectors], packed[2 * sectors, :sectors])
+    kept = kept.astype(jnp.int32)
+    late = jnp.minimum(kept[0], 0)
+    got_b = swapped(window(own, 8 * flag + late, 3))
     gates = jnp.concatenate([gate_ends, 1.0 + gate_pair[:2], gate_pair[2:]])
     first_a = 12 - 8 * flag
     first_b = 8 - 8 * flag
@@ -592,15 +595,15 @@
     role_a = jnp.stack([flag, first_a, own_a])
     role_b = jnp.stack([flag, first_b, own_b])
 
-    own_win = window(own, own_a, 6)
-    sketch_win = window(sketches, first_a, BATCH)
+    own_win = window(own, own_a + late, 6)
+    sketch_win = window(sketches, first_a + late, BATCH)
     parts = early(role_a, gates, kept, own_win, got_0, got_a, scale, sketch_win)
     msg_a, out, carry = first_half(
         role_a, gates, kept, own_win, got_low, scale, sketch_win, parts
     )
     back_a = swapped(msg_a)
-    own_win = window(own, own_b, BATCH)
-    sketch_win = window(sketches, first_b, BATCH)
+    own_win = window(own, own_b + late, BATCH)
+    sketch_win = window(sketches, first_b + late, BATCH)
     msg_b, out, merge = second_half(
         role_b, gates, kept, own_win, got_b, scale, sketch_win, parts[3], carry, out
     )

time: 104 us -> 110 us (1.058)
  waiting for transfers between devices: 34.7 us -> 50.7 us
  local copies, waits for them, and re-layouts: 10.5 us -> 6.01 us
  starting transfers between devices: 14.1 us -> 10.7 us
  Pallas kernels: 40.8 us -> 38.8 us
    ppermute x7, waiting for transfers between devices: 34.7 us -> 48.8 us  [swapped(): return lax.ppermute(value, 'chain', [(i, i ^ 1) for i in range(chain)])]
    dynamic_slice x4, local copies, waits for them, and re-layouts: 8.57 us -> 5.3 us  [window(): return lax.dynamic_slice_in_dim(array, start, size, 0)]
    ppermute x7, starting transfers between devices: 12.1 us -> 9.44 us  [swapped(): return lax.ppermute(value, 'chain', [(i, i ^ 1) for i in range(chain)])]
    pallas_call x5, Pallas kernels: 38.8 us -> 36.8 us  [run(): pl.pallas_call(kernel, out_shape=outs, in_specs=specs, out_specs=out_spec...]
    ppermute x2 -> x1, waiting for transfers between devices: 0.01 us -> 1.94 us  [onward(): return lax.ppermute(value, ('chain', 'group'), pairs)]
    unnamed x16 -> x12, local copies, waits for them, and re-layouts: 1.25 us -> 0.04 us
  transfers between devices with their start and end apart: 9 -> 8, of which waited for: 4 -> 4; matrix products, arithmetic and copies ran while one was open for 10% -> 6% of each run, Pallas kernels for 39% -> 35%
where the time goes in v1:
time: 110 us; the launch traced here: 109 us
  waiting for transfers between devices  50.7 us (46%)
  Pallas kernels  38.8 us (35%)
  starting transfers between devices  10.7 us (10%)
  local copies, waits for them, and re-layouts  6.01 us (5%)
  other arithmetic  1.76 us (2%)
    ppermute x7, waiting for transfers between devices, swapped(): return lax.ppermute(value, 'chain', [(i, i ^ 1) for i in range(chain)])  48.8 us
    pallas_call x5, Pallas kernels, run(): pl.pallas_call(kernel, out_shape=outs, in_specs=specs, out_specs=out_spec...  36.8 us
    ppermute x7, starting transfers between devices, swapped(): return lax.ppermute(value, 'chain', [(i, i ^ 1) for i in range(chain)])  9.44 us
    dynamic_slice x4, local copies, waits for them, and re-layouts, window(): return lax.dynamic_slice_in_dim(array, start, size, 0)  5.3 us
  transfers between devices with their start and end apart: 8, of which 4 were waited for; matrix products, arithmetic and copies ran while one was open for 6% of the time, Pallas kernels for 35%

profile of v1, /device:TPU:1, one launch (start us, length us, event | category | flops | bytes accessed | tf_op | source)
XLA Modules:
  0.0 108.5 jit_solution(3906285870865279689)
XLA Ops:
  0.0 0.8 bitcast_select_fusion
  0.8 1.3 %collective-permute-start = (f32[16,256]{1,0:T(8,128)S(1)}, f32[16,256]{1,0:T(8,128)S(1)}, u32[]{:S(2)}, u32[]{:S(2)}) collective-permute-start(f32[16,256]{1,0:T(8,128)S(1)} %bitcast_select_fusion), channel_id=1, source_target_pairs={{4,8},{12,16},{20,24},{28,32},{36,40},{44,48},{52,56},{60,64},{68,... | collective-permute-start | bytes 49160 | tf_op jit(solution)/shard_map/ppermute | solution.py:561
  2.1 0.0 copy-start.4
  2.1 0.0 copy-start.5
  2.1 0.0 copy-start.3
  2.1 0.0 copy-start.1
  2.1 0.0 copy-start.2
  2.2 1.2 %shard_map.74 = (bf16[2,1024,128]{2,1,0:T(8,128)(2,1)S(1)}, bf16[1,1024,128]{2,1,0:T(8,128)(2,1)S(1)}) custom-call(s32[1]{0:T(128)} %bitcast.1.role, bf16[16,1024,128]{2,1,0:T(8,128)(2,1)} %bitcast.39), custom_call_target="tpu_custom_call" | custom-call | flops 1000000000 | bytes 8000000 | tf_op jit(solution)/shard_map/pallas_call | solution.py:369
  3.4 4.8 %collective-permute-start.4 = (bf16[2,1024,128]{2,1,0:T(8,128)(2,1)S(1)}, bf16[2,1024,128]{2,1,0:T(8,128)(2,1)S(1)}, u32[]{:S(2)}, u32[]{:S(2)}) collective-permute-start(bf16[2,1024,128]{2,1,0:T(8,128)(2,1)S(1)} %get-tuple-element.17), channel_id=1, source_target_pairs={{0,4},{4,0},{8,12},{12,8},{16,20},{20,16},{24,28},{28,24},{32,36},... | collective-permute-start | bytes 1572872 | tf_op jit(solution)/shard_map/ppermute | solution.py:554
  8.2 1.0 shard_map.73
  9.2 0.1 collective-permute-start.3
  9.4 1.4 %collective-permute-start.5 = (bf16[1,1024,128]{2,1,0:T(8,128)(2,1)S(1)}, bf16[1,1024,128]{2,1,0:T(8,128)(2,1)S(1)}, u32[]{:S(2)}, u32[]{:S(2)}) collective-permute-start(bf16[1,1024,128]{2,1,0:T(8,128)(2,1)S(1)} %get-tuple-element.19), channel_id=1, source_target_pairs={{0,4},{4,0},{8,12},{12,8},{16,20},{20,16},{24,28},{28,24},{32,36},... | collective-permute-start | bytes 786440 | tf_op jit(solution)/shard_map/ppermute | solution.py:554
  10.8 0.0 copy-done.4
  10.8 0.0 copy-done.5
  10.8 0.1 pad_add_fusion.1.role
  10.9 0.1 pad_add_fusion.role
  11.0 0.6 slice.21
  11.6 1.9 %collective-permute-done = f32[16,256]{1,0:T(8,128)S(1)} collective-permute-done((f32[16,256]{1,0:T(8,128)S(1)}, f32[16,256]{1,0:T(8,128)S(1)}, u32[]{:S(2)}, u32[]{:S(2)}) %collective-permute-start) | collective-permute-done | bytes 16416 | tf_op jit(solution)/shard_map/ppermute | solution.py:561
  13.5 0.1 collective-permute-start.1
  13.6 0.0 copy-done.3
  13.6 0.7 pad_maximum_fusion.gates
  14.3 22.9 %collective-permute-done.1 = f32[40,256]{1,0:T(8,128)S(1)} collective-permute-done((f32[40,256]{1,0:T(8,128)S(1)}, f32[40,256]{1,0:T(8,128)S(1)}, u32[]{:S(2)}, u32[]{:S(2)}) %collective-permute-start.1) | collective-permute-done | bytes 40992 | tf_op jit(solution)/shard_map/ppermute | solution.py:554
  37.4 0.0 copy-done.1
  37.4 0.0 copy-done.2
  37.4 0.1 select_bitcast_fusion.1
  37.5 0.1 broadcast_in_dim.8.scale
  37.5 2.1 %constant_dynamic-slice_fusion.3 = bf16[3,1024,128]{2,1,0:T(8,128)(2,1)} fusion(bf16[16,1024,128]{2,1,0:T(8,128)(2,1)} %bitcast.41, s32[]{:T(128)S(6)} %select_n.58), kind=kLoop, calls=%fused_computation.17 | loop fusion | bytes 1572868 | tf_op jit(solution)/shard_map/dynamic_slice | solution.py:568
  39.6 1.2 %collective-permute-start.2 = (bf16[3,1024,128]{2,1,0:T(8,128)(2,1)}, bf16[3,1024,128]{2,1,0:T(8,128)(2,1)S(1)}, u32[]{:S(2)}, u32[]{:S(2)}) collective-permute-start(bf16[3,1024,128]{2,1,0:T(8,128)(2,1)} %constant_dynamic-slice_fusion.3), channel_id=1, source_target_pairs={{0,4},{4,0},{8,12},{12,8},{16,20},{20,16},{24,28},{28,24},{32,36},... | collective-permute-start | bytes 2359304 | tf_op jit(solution)/shard_map/ppermute | solution.py:554
  40.8 0.0 copy-start
  40.8 1.4 %constant_dynamic-slice_fusion.4.own = bf16[4,1024,128]{2,1,0:T(8,128)(2,1)S(1)} fusion(bf16[16,1024,128]{2,1,0:T(8,128)(2,1)} %bitcast.42, s32[]{:T(128)S(6)} %select_n.57), kind=kLoop, calls=%fused_computation.18 | loop fusion | bytes 2097156 | tf_op jit(solution)/shard_map/dynamic_slice | solution.py:568
  42.2 1.6 %constant_dynamic-slice_fusion.1.own = bf16[6,1024,128]{2,1,0:T(8,128)(2,1)S(1)} fusion(bf16[16,1024,128]{2,1,0:T(8,128)(2,1)} %bitcast.43, s32[]{:T(128)S(6)} %select_n.64), kind=kLoop, calls=%fused_computation.15 | loop fusion | bytes 3145732 | tf_op jit(solution)/shard_map/dynamic_slice | solution.py:568
  43.9 0.0 copy-done
  43.9 0.1 constant_dynamic-slice_fusion
  44.0 0.0 collective-permute-done.4.got
  44.1 0.0 collective-permute-done.3.got_0
  44.1 4.4 %shard_map.75 = (bf16[3,512,512]{2,1,0:T(8,128)(2,1)S(1)}, bf16[3,2,512,256]{3,2,1,0:T(8,128)(2,1)S(1)}, f32[3,256,256]{2,1,0:T(8,128)S(1)}, bf16[6,256,256]{2,1,0:T(8,128)(2,1)S(1)}) custom-call(s32[3]{0:T(128)S(1)} %pad_add_fusion.1.role, f32[5]{0:T(128)S(1)} %pad_maximum_fusion.gates, s32[16]{0:T(128)S(1)} %fusion.2.kept, ...), custom_call_target="tpu_custom_call" | custom-call | flops 10000000000 | bytes 8000000 | tf_op jit(solution)/shard_map/pallas_call | solution.py:369
  48.5 0.0 collective-permute-done.5.got
  48.5 13.4 %shard_map.76 = (bf16[4,1024,128]{2,1,0:T(8,128)(2,1)S(1)}, bf16[16,1024,128]{2,1,0:T(8,128)(2,1)}, bf16[5,256,256]{2,1,0:T(8,128)(2,1)S(1)}) custom-call(s32[3]{0:T(128)S(1)} %pad_add_fusion.1.role, f32[5]{0:T(128)S(1)} %pad_maximum_fusion.gates, s32[16]{0:T(128)S(1)} %fusion.2.kept, bf16[6,1024,128]{2,1,0:T(8,128)(2,1)S(1)} %constant_dynamic-slice_fusion.1.own, ...), custom_call_target="tpu_custom_call" | custom-call | flops 10000000000 | bytes 8000000 | tf_op jit(solution)/shard_map/pallas_call | solution.py:369
  62.0 0.6 collective-permute-start.7
  62.5 0.0 collective-permute-done.2.got
  62.5 16.7 %shard_map.77 = (bf16[4,1024,128]{2,1,0:T(8,128)(2,1)S(1)}, bf16[16,1024,128]{2,1,0:T(8,128)(2,1)}, bf16[1024,128]{1,0:T(8,128)(2,1)S(1)}) custom-call(s32[3]{0:T(128)S(1)} %pad_add_fusion.role, f32[5]{0:T(128)S(1)} %pad_maximum_fusion.gates, s32[16]{0:T(128)S(1)} %fusion.2.kept, ...), custom_call_target="tpu_custom_call", output_to_operand_aliasing={{1}: (9, {})} | custom-call | flops 10000000000 | bytes 8000000 | tf_op jit(solution)/shard_map/pallas_call | solution.py:369
  79.2 1.3 %collective-permute-start.6 = (bf16[4,1024,128]{2,1,0:T(8,128)(2,1)S(1)}, bf16[4,1024,128]{2,1,0:T(8,128)(2,1)S(1)}, u32[]{:S(2)}, u32[]{:S(2)}) collective-permute-start(bf16[4,1024,128]{2,1,0:T(8,128)(2,1)S(1)} %get-tuple-element.25), channel_id=1, source_target_pairs={{0,4},{4,0},{8,12},{12,8},{16,20},{20,16},{24,28},{28,24},{32,36},... | collective-permute-start | bytes 3145736 | tf_op jit(solution)/shard_map/ppermute | solution.py:554
  80.5 4.4 %collective-permute-done.7.block = bf16[4,1024,128]{2,1,0:T(8,128)(2,1)S(1)} collective-permute-done((bf16[4,1024,128]{2,1,0:T(8,128)(2,1)S(1)}, bf16[4,1024,128]{2,1,0:T(8,128)(2,1)S(1)}, u32[]{:S(2)}, u32[]{:S(2)}) %collective-permute-start.7) | collective-permute-done | bytes 1048608 | tf_op jit(solution)/shard_map/ppermute | solution.py:554
  84.9 1.0 place.2.refs_0_
  85.9 21.5 %collective-permute-done.6.block = bf16[4,1024,128]{2,1,0:T(8,128)(2,1)S(1)} collective-permute-done((bf16[4,1024,128]{2,1,0:T(8,128)(2,1)S(1)}, bf16[4,1024,128]{2,1,0:T(8,128)(2,1)S(1)}, u32[]{:S(2)}, u32[]{:S(2)}) %collective-permute-start.6) | collective-permute-done | bytes 1048608 | tf_op jit(solution)/shard_map/ppermute | solution.py:554
  107.3 1.0 place.3
  (6 shorter events, 0.0 us)
Async XLA Ops:
  0.8 12.7 %collective-permute-start = (f32[16,256]{1,0:T(8,128)S(1)}, f32[16,256]{1,0:T(8,128)S(1)}, u32[]{:S(2)}, u32[]{:S(2)}) collective-permute-start(f32[16,256]{1,0:T(8,128)S(1)} %bitcast_select_fusion), channel_id=1, source_target_pairs={{4,8},{12,16},{20,24},{28,32},{36,40},{44,48},{52,56},{60,64},{68,... | collective-permute-start | bytes 49160 | tf_op jit(solution)/shard_map/ppermute | solution.py:561
  2.1 8.7 %copy-start.4 = (s32[1,1,16]{2,1,0:T(1,128)S(1)}, s32[1,1,16]{2,1,0:T(1,128)}, u32[]{:S(2)}) copy-start(s32[1,1,16]{2,1,0:T(1,128)} %param.10) | copy-start | bytes 196
  2.1 8.7 %copy-start.5 = (f32[3]{0:T(128)S(1)}, f32[3]{0:T(128)}, u32[]{:S(2)}) copy-start(f32[3]{0:T(128)} %param.13) | copy-start | bytes 40
  2.1 11.5 %copy-start.3 = (f32[2]{0:T(128)S(1)}, f32[2]{0:T(128)}, u32[]{:S(2)}) copy-start(f32[2]{0:T(128)} %param.12) | copy-start | bytes 28
  2.1 35.2 %copy-start.1 = (f32[1,1,16,256]{3,2,1,0:T(8,128)S(1)}, f32[1,1,16,256]{3,2,1,0:T(8,128)}, u32[]{:S(2)}) copy-start(f32[1,1,16,256]{3,2,1,0:T(8,128)} %param.8) | copy-start | bytes 49156
  2.1 35.2 %copy-start.2 = (s32[1,1,16]{2,1,0:T(1,128)S(1)}, s32[1,1,16]{2,1,0:T(1,128)}, u32[]{:S(2)}) copy-start(s32[1,1,16]{2,1,0:T(1,128)} %param.9) | copy-start | bytes 196
  3.4 40.6 %collective-permute-start.4 = (bf16[2,1024,128]{2,1,0:T(8,128)(2,1)S(1)}, bf16[2,1024,128]{2,1,0:T(8,128)(2,1)S(1)}, u32[]{:S(2)}, u32[]{:S(2)}) collective-permute-start(bf16[2,1024,128]{2,1,0:T(8,128)(2,1)S(1)} %get-tuple-element.17), channel_id=1, source_target_pairs={{0,4},{4,0},{8,12},{12,8},{16,20},{20,16},{24,28},{28,24},{32,36},... | collective-permute-start | bytes 1572872 | tf_op jit(solution)/shard_map/ppermute | solution.py:554
  9.2 34.8 %collective-permute-start.3 = (bf16[2,1024,128]{2,1,0:T(8,128)(2,1)S(1)}, bf16[2,1024,128]{2,1,0:T(8,128)(2,1)S(1)}, u32[]{:S(2)}, u32[]{:S(2)}) collective-permute-start(bf16[2,1024,128]{2,1,0:T(8,128)(2,1)S(1)} %shard_map.73), channel_id=1, source_target_pairs={{0,4},{4,0},{8,12},{12,8},{16,20},{20,16},{24,28},{28,24},{32,36},... | collective-permute-start | bytes 1572872 | tf_op jit(solution)/shard_map/ppermute | solution.py:554
  9.4 39.2 %collective-permute-start.5 = (bf16[1,1024,128]{2,1,0:T(8,128)(2,1)S(1)}, bf16[1,1024,128]{2,1,0:T(8,128)(2,1)S(1)}, u32[]{:S(2)}, u32[]{:S(2)}) collective-permute-start(bf16[1,1024,128]{2,1,0:T(8,128)(2,1)S(1)} %get-tuple-element.19), channel_id=1, source_target_pairs={{0,4},{4,0},{8,12},{12,8},{16,20},{20,16},{24,28},{28,24},{32,36},... | collective-permute-start | bytes 786440 | tf_op jit(solution)/shard_map/ppermute | solution.py:554
  13.5 23.7 %collective-permute-start.1 = (f32[40,256]{1,0:T(8,128)S(1)}, f32[40,256]{1,0:T(8,128)S(1)}, u32[]{:S(2)}, u32[]{:S(2)}) collective-permute-start(f32[40,256]{1,0:T(8,128)S(1)} %select_maximum_fusion.2), channel_id=1, source_target_pairs={{0,4},{4,0},{8,12},{12,8},{16,20},{20,16},{24,28},{28,24},{32,36},... | collective-permute-start | bytes 122888 | tf_op jit(solution)/shard_map/ppermute | solution.py:554
  39.6 22.9 %collective-permute-start.2 = (bf16[3,1024,128]{2,1,0:T(8,128)(2,1)}, bf16[3,1024,128]{2,1,0:T(8,128)(2,1)S(1)}, u32[]{:S(2)}, u32[]{:S(2)}) collective-permute-start(bf16[3,1024,128]{2,1,0:T(8,128)(2,1)} %constant_dynamic-slice_fusion.3), channel_id=1, source_target_pairs={{0,4},{4,0},{8,12},{12,8},{16,20},{20,16},{24,28},{28,24},{32,36},... | collective-permute-start | bytes 2359304 | tf_op jit(solution)/shard_map/ppermute | solution.py:554
  40.8 3.1 %copy-start = (bf16[16,512,256]{2,1,0:T(8,128)(2,1)S(1)}, bf16[16,512,256]{2,1,0:T(8,128)(2,1)}, u32[]{:S(2)}) copy-start(bf16[16,512,256]{2,1,0:T(8,128)(2,1)} %param.11) | copy-start | bytes 12582916
  62.0 22.9 %collective-permute-start.7 = (bf16[4,1024,128]{2,1,0:T(8,128)(2,1)S(1)}, bf16[4,1024,128]{2,1,0:T(8,128)(2,1)S(1)}, u32[]{:S(2)}, u32[]{:S(2)}) collective-permute-start(bf16[4,1024,128]{2,1,0:T(8,128)(2,1)S(1)} %get-tuple-element.26), channel_id=1, source_target_pairs={{0,4},{4,0},{8,12},{12,8},{16,20},{20,16},{24,28},{28,24},{32,36},... | collective-permute-start | bytes 3145736 | tf_op jit(solution)/shard_map/ppermute | solution.py:554
  79.2 28.1 %collective-permute-start.6 = (bf16[4,1024,128]{2,1,0:T(8,128)(2,1)S(1)}, bf16[4,1024,128]{2,1,0:T(8,128)(2,1)S(1)}, u32[]{:S(2)}, u32[]{:S(2)}) collective-permute-start(bf16[4,1024,128]{2,1,0:T(8,128)(2,1)S(1)} %get-tuple-element.25), channel_id=1, source_target_pairs={{0,4},{4,0},{8,12},{12,8},{16,20},{20,16},{24,28},{28,24},{32,36},... | collective-permute-start | bytes 3145736 | tf_op jit(solution)/shard_map/ppermute | solution.py:554

commit v2 on v1

--- a/solution.py
+++ b/solution.py
@@ -244,22 +244,21 @@
     mixed, samp, gram, edge, left_w, right_w, wide = refs
 
     def step(t, loop):
-        at = jnp.minimum(t - 3, 1)
-        weigh(t, role, own, got.at[at], scale, left_w.at[t], right_w.at[t], wide)
+        weigh(t, role, own, got.at[0], scale, left_w.at[t], right_w.at[t], wide)
         return loop
 
     def step_0(t, loop):
         weigh(t, role, own, got_0.at[t - 1], scale, left_w.at[t], right_w.at[t], wide)
         return loop
 
-    lax.fori_loop(1, 3, step_0, 0)
-    lax.fori_loop(3, 6, step, 0)
+    lax.fori_loop(1, 4, step_0, 0)
+    lax.fori_loop(4, 6, step, 0)
     for s in range(2):
         edge[s] = left_w[1, s]
         edge[2 + s] = right_w[1, s]
     edge[4] = right_w[2, 0]
     below = role[1] - 5
-    wide[0] = got[1].astype(f32)
+    wide[0] = got[0].astype(f32)
     rows = column_of(scale[1, below + 1])
     col = scale[2, below + 2]
     for jb in range(2):
@@ -460,7 +459,7 @@
         fetch_kernel,
         (jnp.reshape(at, (1,)), in_hbm(own)),
         [SMEM, HBM],
-        [shaped(2, *SECTOR)],
+        [shaped(3, *SECTOR)],
         [VMEM],
         [pltpu.SemaphoreType.DMA],
         mib=1,
@@ -472,17 +471,15 @@
     copies = [
         pltpu.make_async_copy(own.at[7 + 8 * flag], both.at[0], sems.at[0]),
         pltpu.make_async_copy(own.at[7], both.at[1], sems.at[1]),
-        pltpu.make_async_copy(own.at[6 + 8 * flag], out.at[0], sems.at[2]),
-        pltpu.make_async_copy(own.at[3 + 8 * flag], low.at[0], sems.at[3]),
+        pltpu.make_async_copy(own.at[3 + 8 * flag], low.at[0], sems.at[2]),
     ]
     for copy in copies:
         copy.start()
     copies[0].wait()
     copies[1].wait()
     is_odd = lax.broadcasted_iota(jnp.int32, SECTOR, 0) % 2 == 1
-    out[1] = jnp.where(is_odd, both[1].astype(f32), both[0].astype(f32)).astype(bf16)
+    out[0] = jnp.where(is_odd, both[1].astype(f32), both[0].astype(f32)).astype(bf16)
     copies[2].wait()
-    copies[3].wait()
 
 
 def pack(role, own):
@@ -490,9 +487,9 @@
         pack_kernel,
         (role, in_hbm(own)),
         [SMEM, HBM],
-        [shaped(2, *SECTOR), shaped(1, *SECTOR)],
+        [shaped(1, *SECTOR)] * 2,
         [VMEM] * 2,
-        [pltpu.VMEM((2, *SECTOR), bf16), pltpu.SemaphoreType.DMA((4,))],
+        [pltpu.VMEM((2, *SECTOR), bf16), pltpu.SemaphoreType.DMA((3,))],
         mib=2,
     )
 

time: 110 us -> 110 us (level)
  no operation moved by 1% of the time
where the time goes in v2:
time: 110 us; the launch traced here: 108 us
  waiting for transfers between devices  50.6 us (46%)
  Pallas kernels  38.9 us (35%)
  starting transfers between devices  10.7 us (10%)
  local copies, waits for them, and re-layouts  5.95 us (5%)
  other arithmetic  1.76 us (2%)
    ppermute x7, waiting for transfers between devices, swapped(): return lax.ppermute(value, 'chain', [(i, i ^ 1) for i in range(chain)])  48.7 us
    pallas_call x5, Pallas kernels, run(): pl.pallas_call(kernel, out_shape=outs, in_specs=specs, out_specs=out_spec...  36.9 us
    ppermute x7, starting transfers between devices, swapped(): return lax.ppermute(value, 'chain', [(i, i ^ 1) for i in range(chain)])  9.44 us
    dynamic_slice x4, local copies, waits for them, and re-layouts, window(): return lax.dynamic_slice_in_dim(array, start, size, 0)  5.24 us
  transfers between devices with their start and end apart: 8, of which 4 were waited for; matrix products, arithmetic and copies ran while one was open for 6% of the time, Pallas kernels for 35%

profile of v2, /device:TPU:1, one launch (start us, length us, event | category | flops | bytes accessed | tf_op | source)
XLA Modules:
  0.0 108.4 jit_solution(15144921852785594286)
XLA Ops:
  0.0 0.8 bitcast_select_fusion
  0.8 1.3 %collective-permute-start = (f32[16,256]{1,0:T(8,128)S(1)}, f32[16,256]{1,0:T(8,128)S(1)}, u32[]{:S(2)}, u32[]{:S(2)}) collective-permute-start(f32[16,256]{1,0:T(8,128)S(1)} %bitcast_select_fusion), channel_id=1, source_target_pairs={{4,8},{12,16},{20,24},{28,32},{36,40},{44,48},{52,56},{60,64},{68,... | collective-permute-start | bytes 49160 | tf_op jit(solution)/shard_map/ppermute | solution.py:558
  2.1 0.0 copy-start.4
  2.1 0.0 copy-start.5
  2.1 0.0 copy-start.3
  2.1 0.0 copy-start.1
  2.1 0.0 copy-start.2
  2.2 1.2 %shard_map.73 = bf16[3,1024,128]{2,1,0:T(8,128)(2,1)S(1)} custom-call(s32[1]{0:T(128)} %bitcast.20.at, bf16[16,1024,128]{2,1,0:T(8,128)(2,1)} %bitcast.39), custom_call_target="tpu_custom_call" | custom-call | flops 500000000 | bytes 8000000 | tf_op jit(solution)/shard_map/pallas_call | solution.py:368
  3.3 4.8 %collective-permute-start.3 = (bf16[3,1024,128]{2,1,0:T(8,128)(2,1)S(1)}, bf16[3,1024,128]{2,1,0:T(8,128)(2,1)S(1)}, u32[]{:S(2)}, u32[]{:S(2)}) collective-permute-start(bf16[3,1024,128]{2,1,0:T(8,128)(2,1)S(1)} %shard_map.73), channel_id=1, source_target_pairs={{0,4},{4,0},{8,12},{12,8},{16,20},{20,16},{24,28},{28,24},{32,36},... | collective-permute-start | bytes 2359304 | tf_op jit(solution)/shard_map/ppermute | solution.py:551
  8.1 1.2 %shard_map.74 = (bf16[1,1024,128]{2,1,0:T(8,128)(2,1)S(1)}, bf16[1,1024,128]{2,1,0:T(8,128)(2,1)S(1)}) custom-call(s32[1]{0:T(128)} %bitcast.1.role, bf16[16,1024,128]{2,1,0:T(8,128)(2,1)} %bitcast.40), custom_call_target="tpu_custom_call" | custom-call | flops 1000000000 | bytes 8000000 | tf_op jit(solution)/shard_map/pallas_call | solution.py:368
  9.3 0.1 collective-permute-start.4
  9.4 1.4 %collective-permute-start.5 = (bf16[1,1024,128]{2,1,0:T(8,128)(2,1)S(1)}, bf16[1,1024,128]{2,1,0:T(8,128)(2,1)S(1)}, u32[]{:S(2)}, u32[]{:S(2)}) collective-permute-start(bf16[1,1024,128]{2,1,0:T(8,128)(2,1)S(1)} %get-tuple-element.19), channel_id=1, source_target_pairs={{0,4},{4,0},{8,12},{12,8},{16,20},{20,16},{24,28},{28,24},{32,36},... | collective-permute-start | bytes 786440 | tf_op jit(solution)/shard_map/ppermute | solution.py:551
  10.8 0.0 copy-done.4
  10.8 0.0 copy-done.5
  10.9 0.1 pad_add_fusion.1.role
  10.9 0.1 pad_add_fusion.role
  11.0 0.6 slice.21
  11.6 1.9 %collective-permute-done = f32[16,256]{1,0:T(8,128)S(1)} collective-permute-done((f32[16,256]{1,0:T(8,128)S(1)}, f32[16,256]{1,0:T(8,128)S(1)}, u32[]{:S(2)}, u32[]{:S(2)}) %collective-permute-start) | collective-permute-done | bytes 16416 | tf_op jit(solution)/shard_map/ppermute | solution.py:558
  13.5 0.1 collective-permute-start.1
  13.6 0.0 copy-done.3
  13.6 0.7 pad_maximum_fusion.gates
  14.3 22.8 %collective-permute-done.1 = f32[40,256]{1,0:T(8,128)S(1)} collective-permute-done((f32[40,256]{1,0:T(8,128)S(1)}, f32[40,256]{1,0:T(8,128)S(1)}, u32[]{:S(2)}, u32[]{:S(2)}) %collective-permute-start.1) | collective-permute-done | bytes 40992 | tf_op jit(solution)/shard_map/ppermute | solution.py:551
  37.2 0.0 copy-done.1
  37.2 0.0 copy-done.2
  37.2 0.1 select_bitcast_fusion.1
  37.4 0.1 broadcast_in_dim.8.scale
  37.4 2.1 %constant_dynamic-slice_fusion.3 = bf16[3,1024,128]{2,1,0:T(8,128)(2,1)} fusion(bf16[16,1024,128]{2,1,0:T(8,128)(2,1)} %bitcast.41, s32[]{:T(128)S(6)} %select_n.58), kind=kLoop, calls=%fused_computation.17 | loop fusion | bytes 1572868 | tf_op jit(solution)/shard_map/dynamic_slice | solution.py:565
  39.5 1.2 %collective-permute-start.2 = (bf16[3,1024,128]{2,1,0:T(8,128)(2,1)}, bf16[3,1024,128]{2,1,0:T(8,128)(2,1)S(1)}, u32[]{:S(2)}, u32[]{:S(2)}) collective-permute-start(bf16[3,1024,128]{2,1,0:T(8,128)(2,1)} %constant_dynamic-slice_fusion.3), channel_id=1, source_target_pairs={{0,4},{4,0},{8,12},{12,8},{16,20},{20,16},{24,28},{28,24},{32,36},... | collective-permute-start | bytes 2359304 | tf_op jit(solution)/shard_map/ppermute | solution.py:551
  40.7 0.0 copy-start
  40.7 1.7 %constant_dynamic-slice_fusion.1.own = bf16[6,1024,128]{2,1,0:T(8,128)(2,1)S(1)} fusion(bf16[16,1024,128]{2,1,0:T(8,128)(2,1)} %bitcast.42, s32[]{:T(128)S(6)} %select_n.64), kind=kLoop, calls=%fused_computation.15 | loop fusion | bytes 3145732 | tf_op jit(solution)/shard_map/dynamic_slice | solution.py:565
  42.4 1.4 %constant_dynamic-slice_fusion.4.own = bf16[4,1024,128]{2,1,0:T(8,128)(2,1)S(1)} fusion(bf16[16,1024,128]{2,1,0:T(8,128)(2,1)} %bitcast.43, s32[]{:T(128)S(6)} %select_n.57), kind=kLoop, calls=%fused_computation.18 | loop fusion | bytes 2097156 | tf_op jit(solution)/shard_map/dynamic_slice | solution.py:565
  43.7 0.0 copy-done
  43.7 0.1 constant_dynamic-slice_fusion
  43.9 0.0 collective-permute-done.4.got
  43.9 0.0 collective-permute-done.3.got_0
  43.9 4.4 %shard_map.75 = (bf16[3,512,512]{2,1,0:T(8,128)(2,1)S(1)}, bf16[3,2,512,256]{3,2,1,0:T(8,128)(2,1)S(1)}, f32[3,256,256]{2,1,0:T(8,128)S(1)}, bf16[6,256,256]{2,1,0:T(8,128)(2,1)S(1)}) custom-call(s32[3]{0:T(128)S(1)} %pad_add_fusion.1.role, f32[5]{0:T(128)S(1)} %pad_maximum_fusion.gates, s32[16]{0:T(128)S(1)} %fusion.2.kept, ...), custom_call_target="tpu_custom_call" | custom-call | flops 10000000000 | bytes 8000000 | tf_op jit(solution)/shard_map/pallas_call | solution.py:368
  48.4 0.0 collective-permute-done.5.got
  48.4 13.4 %shard_map.76 = (bf16[4,1024,128]{2,1,0:T(8,128)(2,1)S(1)}, bf16[16,1024,128]{2,1,0:T(8,128)(2,1)}, bf16[5,256,256]{2,1,0:T(8,128)(2,1)S(1)}) custom-call(s32[3]{0:T(128)S(1)} %pad_add_fusion.1.role, f32[5]{0:T(128)S(1)} %pad_maximum_fusion.gates, s32[16]{0:T(128)S(1)} %fusion.2.kept, bf16[6,1024,128]{2,1,0:T(8,128)(2,1)S(1)} %constant_dynamic-slice_fusion.1.own, ...), custom_call_target="tpu_custom_call" | custom-call | flops 10000000000 | bytes 8000000 | tf_op jit(solution)/shard_map/pallas_call | solution.py:368
  61.8 0.6 collective-permute-start.7
  62.4 0.0 collective-permute-done.2.got
  62.4 16.7 %shard_map.77 = (bf16[4,1024,128]{2,1,0:T(8,128)(2,1)S(1)}, bf16[16,1024,128]{2,1,0:T(8,128)(2,1)}, bf16[1024,128]{1,0:T(8,128)(2,1)S(1)}) custom-call(s32[3]{0:T(128)S(1)} %pad_add_fusion.role, f32[5]{0:T(128)S(1)} %pad_maximum_fusion.gates, s32[16]{0:T(128)S(1)} %fusion.2.kept, ...), custom_call_target="tpu_custom_call", output_to_operand_aliasing={{1}: (9, {})} | custom-call | flops 10000000000 | bytes 8000000 | tf_op jit(solution)/shard_map/pallas_call | solution.py:368
  79.1 1.3 %collective-permute-start.6 = (bf16[4,1024,128]{2,1,0:T(8,128)(2,1)S(1)}, bf16[4,1024,128]{2,1,0:T(8,128)(2,1)S(1)}, u32[]{:S(2)}, u32[]{:S(2)}) collective-permute-start(bf16[4,1024,128]{2,1,0:T(8,128)(2,1)S(1)} %get-tuple-element.25), channel_id=1, source_target_pairs={{0,4},{4,0},{8,12},{12,8},{16,20},{20,16},{24,28},{28,24},{32,36},... | collective-permute-start | bytes 3145736 | tf_op jit(solution)/shard_map/ppermute | solution.py:551
  80.4 4.4 %collective-permute-done.7.block = bf16[4,1024,128]{2,1,0:T(8,128)(2,1)S(1)} collective-permute-done((bf16[4,1024,128]{2,1,0:T(8,128)(2,1)S(1)}, bf16[4,1024,128]{2,1,0:T(8,128)(2,1)S(1)}, u32[]{:S(2)}, u32[]{:S(2)}) %collective-permute-start.7) | collective-permute-done | bytes 1048608 | tf_op jit(solution)/shard_map/ppermute | solution.py:551
  84.7 1.0 place.2.refs_0_
  85.7 21.5 %collective-permute-done.6.block = bf16[4,1024,128]{2,1,0:T(8,128)(2,1)S(1)} collective-permute-done((bf16[4,1024,128]{2,1,0:T(8,128)(2,1)S(1)}, bf16[4,1024,128]{2,1,0:T(8,128)(2,1)S(1)}, u32[]{:S(2)}, u32[]{:S(2)}) %collective-permute-start.6) | collective-permute-done | bytes 1048608 | tf_op jit(solution)/shard_map/ppermute | solution.py:551
  107.2 1.0 place.3
  (6 shorter events, 0.0 us)
Async XLA Ops:
  0.8 12.7 %collective-permute-start = (f32[16,256]{1,0:T(8,128)S(1)}, f32[16,256]{1,0:T(8,128)S(1)}, u32[]{:S(2)}, u32[]{:S(2)}) collective-permute-start(f32[16,256]{1,0:T(8,128)S(1)} %bitcast_select_fusion), channel_id=1, source_target_pairs={{4,8},{12,16},{20,24},{28,32},{36,40},{44,48},{52,56},{60,64},{68,... | collective-permute-start | bytes 49160 | tf_op jit(solution)/shard_map/ppermute | solution.py:558
  2.1 8.7 %copy-start.4 = (s32[1,1,16]{2,1,0:T(1,128)S(1)}, s32[1,1,16]{2,1,0:T(1,128)}, u32[]{:S(2)}) copy-start(s32[1,1,16]{2,1,0:T(1,128)} %param.10) | copy-start | bytes 196
  2.1 8.7 %copy-start.5 = (f32[3]{0:T(128)S(1)}, f32[3]{0:T(128)}, u32[]{:S(2)}) copy-start(f32[3]{0:T(128)} %param.13) | copy-start | bytes 40
  2.1 11.5 %copy-start.3 = (f32[2]{0:T(128)S(1)}, f32[2]{0:T(128)}, u32[]{:S(2)}) copy-start(f32[2]{0:T(128)} %param.12) | copy-start | bytes 28
  2.1 35.1 %copy-start.1 = (f32[1,1,16,256]{3,2,1,0:T(8,128)S(1)}, f32[1,1,16,256]{3,2,1,0:T(8,128)}, u32[]{:S(2)}) copy-start(f32[1,1,16,256]{3,2,1,0:T(8,128)} %param.8) | copy-start | bytes 49156
  2.1 35.1 %copy-start.2 = (s32[1,1,16]{2,1,0:T(1,128)S(1)}, s32[1,1,16]{2,1,0:T(1,128)}, u32[]{:S(2)}) copy-start(s32[1,1,16]{2,1,0:T(1,128)} %param.9) | copy-start | bytes 196
  3.3 40.6 %collective-permute-start.3 = (bf16[3,1024,128]{2,1,0:T(8,128)(2,1)S(1)}, bf16[3,1024,128]{2,1,0:T(8,128)(2,1)S(1)}, u32[]{:S(2)}, u32[]{:S(2)}) collective-permute-start(bf16[3,1024,128]{2,1,0:T(8,128)(2,1)S(1)} %shard_map.73), channel_id=1, source_target_pairs={{0,4},{4,0},{8,12},{12,8},{16,20},{20,16},{24,28},{28,24},{32,36},... | collective-permute-start | bytes 2359304 | tf_op jit(solution)/shard_map/ppermute | solution.py:551
  9.3 34.6 %collective-permute-start.4 = (bf16[1,1024,128]{2,1,0:T(8,128)(2,1)S(1)}, bf16[1,1024,128]{2,1,0:T(8,128)(2,1)S(1)}, u32[]{:S(2)}, u32[]{:S(2)}) collective-permute-start(bf16[1,1024,128]{2,1,0:T(8,128)(2,1)S(1)} %get-tuple-element.17), channel_id=1, source_target_pairs={{0,4},{4,0},{8,12},{12,8},{16,20},{20,16},{24,28},{28,24},{32,36},... | collective-permute-start | bytes 786440 | tf_op jit(solution)/shard_map/ppermute | solution.py:551
  9.4 39.0 %collective-permute-start.5 = (bf16[1,1024,128]{2,1,0:T(8,128)(2,1)S(1)}, bf16[1,1024,128]{2,1,0:T(8,128)(2,1)S(1)}, u32[]{:S(2)}, u32[]{:S(2)}) collective-permute-start(bf16[1,1024,128]{2,1,0:T(8,128)(2,1)S(1)} %get-tuple-element.19), channel_id=1, source_target_pairs={{0,4},{4,0},{8,12},{12,8},{16,20},{20,16},{24,28},{28,24},{32,36},... | collective-permute-start | bytes 786440 | tf_op jit(solution)/shard_map/ppermute | solution.py:551
  13.5 23.7 %collective-permute-start.1 = (f32[40,256]{1,0:T(8,128)S(1)}, f32[40,256]{1,0:T(8,128)S(1)}, u32[]{:S(2)}, u32[]{:S(2)}) collective-permute-start(f32[40,256]{1,0:T(8,128)S(1)} %select_maximum_fusion.2), channel_id=1, source_target_pairs={{0,4},{4,0},{8,12},{12,8},{16,20},{20,16},{24,28},{28,24},{32,36},... | collective-permute-start | bytes 122888 | tf_op jit(solution)/shard_map/ppermute | solution.py:551
  39.5 22.9 %collective-permute-start.2 = (bf16[3,1024,128]{2,1,0:T(8,128)(2,1)}, bf16[3,1024,128]{2,1,0:T(8,128)(2,1)S(1)}, u32[]{:S(2)}, u32[]{:S(2)}) collective-permute-start(bf16[3,1024,128]{2,1,0:T(8,128)(2,1)} %constant_dynamic-slice_fusion.3), channel_id=1, source_target_pairs={{0,4},{4,0},{8,12},{12,8},{16,20},{20,16},{24,28},{28,24},{32,36},... | collective-permute-start | bytes 2359304 | tf_op jit(solution)/shard_map/ppermute | solution.py:551
  40.7 3.0 %copy-start = (bf16[16,512,256]{2,1,0:T(8,128)(2,1)S(1)}, bf16[16,512,256]{2,1,0:T(8,128)(2,1)}, u32[]{:S(2)}) copy-start(bf16[16,512,256]{2,1,0:T(8,128)(2,1)} %param.11) | copy-start | bytes 12582916
  61.8 22.9 %collective-permute-start.7 = (bf16[4,1024,128]{2,1,0:T(8,128)(2,1)S(1)}, bf16[4,1024,128]{2,1,0:T(8,128)(2,1)S(1)}, u32[]{:S(2)}, u32[]{:S(2)}) collective-permute-start(bf16[4,1024,128]{2,1,0:T(8,128)(2,1)S(1)} %get-tuple-element.26), channel_id=1, source_target_pairs={{0,4},{4,0},{8,12},{12,8},{16,20},{20,16},{24,28},{28,24},{32,36},... | collective-permute-start | bytes 3145736 | tf_op jit(solution)/shard_map/ppermute | solution.py:551
  79.1 28.1 %collective-permute-start.6 = (bf16[4,1024,128]{2,1,0:T(8,128)(2,1)S(1)}, bf16[4,1024,128]{2,1,0:T(8,128)(2,1)S(1)}, u32[]{:S(2)}, u32[]{:S(2)}) collective-permute-start(bf16[4,1024,128]{2,1,0:T(8,128)(2,1)S(1)} %get-tuple-element.25), channel_id=1, source_target_pairs={{0,4},{4,0},{8,12},{12,8},{16,20},{20,16},{24,28},{28,24},{32,36},... | collective-permute-start | bytes 3145736 | tf_op jit(solution)/shard_map/ppermute | solution.py:551

commit v3 on v2

--- a/solution.py
+++ b/solution.py
@@ -140,7 +140,7 @@
 def weigh(t, role, own, got, scale, left, right, wide):
     is_right = role[0] == 1
     q = role[1] - 1 + t
-    own_wide = own[jnp.clip(q, 0, 15) - role[2]].astype(f32)
+    own_wide = own[...].astype(f32)
     got_wide = got[...].astype(f32)
     wide[0] = jnp.where(is_right, got_wide, own_wide)
     wide[1] = jnp.where(is_right, own_wide, got_wide)
@@ -240,15 +240,34 @@
     return copies
 
 
-def early_kernel(role, gates, kept, own, got_0, got, scale, sketch, *refs):
-    mixed, samp, gram, edge, left_w, right_w, wide = refs
+def windows(role, own, sketches, own_win, sketch, sems):
+    count = own_win.shape[0]
+
+    def own_copy(t):
+        at = jnp.clip(role[1] - 1 + t, 0, own.shape[0] - 1)
+        return pltpu.make_async_copy(own.at[at], own_win.at[t], sems.at[t])
+
+    sketch_copy = pltpu.make_async_copy(
+        sketches.at[pl.ds(role[1], BATCH)], sketch, sems.at[count]
+    )
+    return own_copy, sketch_copy
+
+
+def early_kernel(role, gates, kept, own, got_0, got, scale, sketches, *refs):
+    mixed, samp, gram, edge, own_low, left_w, right_w, wide, own_win, sketch, sems = refs
+    own_copy, sketch_copy = windows(role, own, sketches, own_win, sketch, sems)
+    for t in (1, 2, 3, 4, 5, 0):
+        own_copy(t).start()
+    sketch_copy.start()
 
     def step(t, loop):
-        weigh(t, role, own, got.at[0], scale, left_w.at[t], right_w.at[t], wide)
+        own_copy(t).wait()
+        weigh(t, role, own_win.at[t], got.at[0], scale, left_w.at[t], right_w.at[t], wide)
         return loop
 
     def step_0(t, loop):
-        weigh(t, role, own, got_0.at[t - 1], scale, left_w.at[t], right_w.at[t], wide)
+        own_copy(t).wait()
+        weigh(t, role, own_win.at[t], got_0.at[t - 1], scale, left_w.at[t], right_w.at[t], wide)
         return loop
 
     lax.fori_loop(1, 4, step_0, 0)
@@ -264,6 +283,11 @@
     for jb in range(2):
         lanes = lanes_of(jb)
         edge[5, :, lanes] = ((wide[0, lines_of(jb, 1), :] * rows) * col[:, lanes]).astype(bf16)
+    own_copy(0).wait()
+    own_low[...] = own_win[0]
+    sketch_copy.wait()
+    edge[6] = sketch[0, UPPER]
+    edge[7] = sketch[0, LOWER]
     for b in range(1, BATCH):
         t = b + 1
         sample(
@@ -281,15 +305,15 @@
         )
 
 
-def first_kernel(role, gates, kept, own, got, scale, sketch, *refs):
-    (mixed_e, samp_e, gram_e, edge, msg, out, carry), refs = refs[:7], refs[7:]
+def first_kernel(role, gates, kept, got, scale, *refs):
+    (mixed_e, samp_e, gram_e, edge, own, msg, out, carry), refs = refs[:8], refs[8:]
     mixed, samp, gram, scaled, a_ref, x_ref, wide, ready, sems = refs
     left, right = carry.at[pl.ds(1, 2)], carry.at[pl.ds(3, 2)]
     weigh(0, role, own, got.at[0], scale, left, right, wide)
     sample(
         gates,
         kept[role[1]],
-        sketch[0],
+        jnp.concatenate([edge[6], edge[7]], axis=0),
         (edge[0], edge[1]),
         (left[0], left[1]),
         (edge[2], edge[3]),
@@ -309,14 +333,19 @@
         copy.wait()
 
 
-def second_kernel(role, gates, kept, own, got, scale, sketch, *refs):
+def second_kernel(role, gates, kept, own, got, scale, sketches, *refs):
     (edge, carry, _, msg, out, merge), refs = refs[:6], refs[6:]
     left_w, right_w, mixed, samp, gram, scaled, a_ref, x_ref, wide = refs[:9]
-    ready, sems = refs[9:]
+    ready, sems, own_win, sketch, win_sems = refs[9:]
+    own_copy, sketch_copy = windows(role, own, sketches, own_win, sketch, win_sems)
+    for t in range(4):
+        own_copy(t).start()
+    sketch_copy.start()
 
     def step(t, loop):
         at = jnp.maximum(t - 1, 0)
-        weigh(t, role, own, got.at[at], scale, left_w.at[t], right_w.at[t], wide)
+        own_copy(t).wait()
+        weigh(t, role, own_win.at[t], got.at[at], scale, left_w.at[t], right_w.at[t], wide)
         return loop
 
     lax.fori_loop(0, 4, step, 0)
@@ -325,6 +354,7 @@
         left_w[4, s] = carry[1 + s]
         right_w[4, s] = carry[3 + s]
     right_w[5, 0] = edge[2]
+    sketch_copy.wait()
     for b in range(BATCH):
         t = b + 1
         sample(
@@ -402,26 +432,35 @@
     ]
 
 
-def early(role, gates, kept, own, got_0, got, scale, sketch):
+def window_scratch(count):
+    return [
+        pltpu.VMEM((count, *SECTOR), bf16),
+        pltpu.VMEM((BATCH, 2 * SIZE, SIZE), bf16),
+        pltpu.SemaphoreType.DMA((count + 1,)),
+    ]
+
+
+def early(role, gates, kept, own, got_0, got, scale, sketches):
     return run(
         early_kernel,
-        (role, gates, kept, own, got_0, got, scale, sketch),
-        [SMEM] * 3 + [VMEM] * 5,
-        sample_shapes(jax.ShapeDtypeStruct, BATCH - 1) + [shaped(6, SIZE, SIZE)],
-        [VMEM] * 4,
+        (role, gates, kept, in_hbm(own), got_0, got, scale, in_hbm(sketches)),
+        [SMEM] * 3 + [HBM, VMEM, VMEM, VMEM, HBM],
+        sample_shapes(jax.ShapeDtypeStruct, BATCH - 1) + [shaped(8, SIZE, SIZE), shaped(*SECTOR)],
+        [VMEM] * 5,
         [
             pltpu.VMEM((6, 2, SIZE, SIZE), bf16),
             pltpu.VMEM((6, 2, SIZE, SIZE), bf16),
             pltpu.VMEM((2, *SECTOR), f32),
-        ],
-    )
-
-
-def first_half(role, gates, kept, own, got, scale, sketch, parts):
+        ]
+        + window_scratch(6),
+    )
+
+
+def first_half(role, gates, kept, got, scale, parts):
     return run(
         first_kernel,
-        (role, gates, kept, own, got, scale, sketch, *parts),
-        [SMEM] * 3 + [VMEM] * 8,
+        (role, gates, kept, got, scale, *parts),
+        [SMEM] * 3 + [VMEM] * 7,
         [shaped(BATCH, *SECTOR), pltpu.HBM((16, *SECTOR), bf16), shaped(5, SIZE, SIZE)],
         [VMEM, HBM, VMEM],
         sample_shapes(pltpu.VMEM)
@@ -430,11 +469,11 @@
     )
 
 
-def second_half(role, gates, kept, own, got, scale, sketch, edge, carry, out):
+def second_half(role, gates, kept, own, got, scale, sketches, edge, carry, out):
     return run(
         second_kernel,
-        (role, gates, kept, own, got, scale, sketch, edge, carry, out),
-        [SMEM] * 3 + [VMEM] * 6 + [HBM],
+        (role, gates, kept, in_hbm(own), got, scale, in_hbm(sketches), edge, carry, out),
+        [SMEM] * 3 + [HBM, VMEM, VMEM, HBM, VMEM, VMEM, HBM],
         [shaped(BATCH, *SECTOR), pltpu.HBM((16, *SECTOR), bf16), shaped(*SECTOR)],
         [VMEM, HBM, VMEM],
         [pltpu.VMEM((6, 2, SIZE, SIZE), bf16), pltpu.VMEM((6, 2, SIZE, SIZE), bf16)]
@@ -443,7 +482,8 @@
         + [
             pltpu.VMEM((BATCH, *SECTOR), bf16),
             pltpu.SemaphoreType.DMA((BATCH,)),
-        ],
+        ]
+        + window_scratch(4),
         aliases={9: 1},
     )
 
@@ -466,12 +506,13 @@
     )[0]
 
 
-def pack_kernel(role, own, out, low, both, sems):
+def pack_kernel(role, own, out, low, rest, both, sems):
     flag = role[0]
     copies = [
         pltpu.make_async_copy(own.at[7 + 8 * flag], both.at[0], sems.at[0]),
         pltpu.make_async_copy(own.at[7], both.at[1], sems.at[1]),
         pltpu.make_async_copy(own.at[3 + 8 * flag], low.at[0], sems.at[2]),
+        pltpu.make_async_copy(own.at[pl.ds(8 * flag, 3)], rest, sems.at[3]),
     ]
     for copy in copies:
         copy.start()
@@ -480,6 +521,7 @@
     is_odd = lax.broadcasted_iota(jnp.int32, SECTOR, 0) % 2 == 1
     out[0] = jnp.where(is_odd, both[1].astype(f32), both[0].astype(f32)).astype(bf16)
     copies[2].wait()
+    copies[3].wait()
 
 
 def pack(role, own):
@@ -487,9 +529,9 @@
         pack_kernel,
         (role, in_hbm(own)),
         [SMEM, HBM],
-        [shaped(1, *SECTOR)] * 2,
-        [VMEM] * 2,
-        [pltpu.VMEM((2, *SECTOR), bf16), pltpu.SemaphoreType.DMA((3,))],
+        [shaped(1, *SECTOR), shaped(1, *SECTOR), shaped(3, *SECTOR)],
+        [VMEM] * 3,
+        [pltpu.VMEM((2, *SECTOR), bf16), pltpu.SemaphoreType.DMA((4,))],
         mib=2,
     )
 
@@ -561,9 +603,6 @@
     sectors = own.shape[0]
     flag = is_right.astype(jnp.int32)
 
-    def window(array, start, size):
-        return lax.dynamic_slice_in_dim(array, start, size, 0)
-
     got_0 = swapped(fetch(4 + 8 * flag, own))
     column = lax.broadcasted_iota(jnp.int32, (sectors, SIZE), 1)
     lam = bond_weights[0, 0] * (column < sector_sizes[0, 0][:, None]).astype(f32)
@@ -572,7 +611,7 @@
     kept_line = jnp.pad(kept_ranks[0, 0].astype(f32)[None, :], ((0, 7), (0, SIZE - sectors)))
     packed = jnp.concatenate([lam, before, kept_line], axis=0)
     other = swapped(packed)
-    outgoing, outgoing_low = pack(jnp.reshape(flag, (1,)), own)
+    outgoing, outgoing_low, outgoing_b = pack(jnp.reshape(flag, (1,)), own)
     got_a = swapped(outgoing)
     got_low = swapped(outgoing_low)
     lam_prev = jnp.where(is_right, other[sectors : 2 * sectors], before)
@@ -582,27 +621,18 @@
     scale = scale[:, :, None, :]
     kept = jnp.where(is_right, other[2 * sectors, :sectors], packed[2 * sectors, :sectors])
     kept = kept.astype(jnp.int32)
-    late = jnp.minimum(kept[0], 0)
-    got_b = swapped(window(own, 8 * flag + late, 3))
+    got_b = swapped(outgoing_b)
     gates = jnp.concatenate([gate_ends, 1.0 + gate_pair[:2], gate_pair[2:]])
     first_a = 12 - 8 * flag
     first_b = 8 - 8 * flag
-    own_a = 10 - 7 * flag
-    own_b = 7 - 7 * flag
-    role_a = jnp.stack([flag, first_a, own_a])
-    role_b = jnp.stack([flag, first_b, own_b])
-
-    own_win = window(own, own_a + late, 6)
-    sketch_win = window(sketches, first_a + late, BATCH)
-    parts = early(role_a, gates, kept, own_win, got_0, got_a, scale, sketch_win)
-    msg_a, out, carry = first_half(
-        role_a, gates, kept, own_win, got_low, scale, sketch_win, parts
-    )
+    role_a = jnp.stack([flag, first_a])
+    role_b = jnp.stack([flag, first_b])
+
+    parts = early(role_a, gates, kept, own, got_0, got_a, scale, sketches)
+    msg_a, out, carry = first_half(role_a, gates, kept, got_low, scale, parts)
     back_a = swapped(msg_a)
-    own_win = window(own, own_b + late, BATCH)
-    sketch_win = window(sketches, first_b + late, BATCH)
     msg_b, out, merge = second_half(
-        role_b, gates, kept, own_win, got_b, scale, sketch_win, parts[3], carry, out
+        role_b, gates, kept, own, got_b, scale, sketches, parts[3], carry, out
     )
     back_b = swapped(msg_b)
 

time: 110 us -> 122 us (1.11)
  waiting for transfers between devices: 50.6 us -> 65.6 us
  local copies, waits for them, and re-layouts: 5.95 us -> 0.72 us
  Pallas kernels: 38.9 us -> 42.8 us
    ppermute x7, waiting for transfers between devices: 48.7 us -> 64.7 us  [swapped(): return lax.ppermute(value, 'chain', [(i, i ^ 1) for i in range(chain)])]
    dynamic_slice x4 -> x0, local copies, waits for them, and re-layouts: 5.24 us -> none  [window(): return lax.dynamic_slice_in_dim(array, start, size, 0)]
    pallas_call x5, Pallas kernels: 36.9 us -> 40.8 us  [run(): pl.pallas_call(kernel, out_shape=outs, in_specs=specs, out_specs=out_spec...]
  transfers between devices with their start and end apart: 8 -> 8, of which waited for: 4 -> 4; matrix products, arithmetic and copies ran while one was open for 6% -> 1% of each run, Pallas kernels for 35% -> 35%
where the time goes in v3:
time: 122 us; the launch traced here: 121 us
  waiting for transfers between devices  65.6 us (54%)
  Pallas kernels  42.8 us (35%)
  starting transfers between devices  9.87 us (8%)
  other arithmetic  1.68 us (1%)
    ppermute x7, waiting for transfers between devices, swapped(): return lax.ppermute(value, 'chain', [(i, i ^ 1) for i in range(chain)])  64.7 us
    pallas_call x5, Pallas kernels, run(): pl.pallas_call(kernel, out_shape=outs, in_specs=specs, out_specs=out_spec...  40.8 us
    ppermute x7, starting transfers between devices, swapped(): return lax.ppermute(value, 'chain', [(i, i ^ 1) for i in range(chain)])  8.59 us
  transfers between devices with their start and end apart: 8, of which 4 were waited for; matrix products, arithmetic and copies ran while one was open for 1% of the time, Pallas kernels for 35%

profile of v3, /device:TPU:1, one launch (start us, length us, event | category | flops | bytes accessed | tf_op | source)
XLA Modules:
  0.0 121.1 jit_solution(15459340780723211473)
XLA Ops:
  0.0 0.8 bitcast_select_fusion
  0.8 1.3 %collective-permute-start = (f32[16,256]{1,0:T(8,128)S(1)}, f32[16,256]{1,0:T(8,128)S(1)}, u32[]{:S(2)}, u32[]{:S(2)}) collective-permute-start(f32[16,256]{1,0:T(8,128)S(1)} %bitcast_select_fusion), channel_id=1, source_target_pairs={{4,8},{12,16},{20,24},{28,32},{36,40},{44,48},{52,56},{60,64},{68,... | collective-permute-start | bytes 49160 | tf_op jit(solution)/shard_map/ppermute | solution.py:600
  2.1 0.0 copy-start.3
  2.1 0.0 copy-start.4
  2.1 0.0 copy-start.2
  2.1 0.0 copy-start
  2.1 0.0 copy-start.1
  2.2 1.2 shard_map.74
  3.3 4.8 %collective-permute-start.3 = (bf16[3,1024,128]{2,1,0:T(8,128)(2,1)S(1)}, bf16[3,1024,128]{2,1,0:T(8,128)(2,1)S(1)}, u32[]{:S(2)}, u32[]{:S(2)}) collective-permute-start(bf16[3,1024,128]{2,1,0:T(8,128)(2,1)S(1)} %shard_map.74), channel_id=1, source_target_pairs={{0,4},{4,0},{8,12},{12,8},{16,20},{20,16},{24,28},{28,24},{32,36},... | collective-permute-start | bytes 2359304 | tf_op jit(solution)/shard_map/ppermute | solution.py:593
  8.1 2.1 %shard_map.73 = (bf16[1,1024,128]{2,1,0:T(8,128)(2,1)}, bf16[1,1024,128]{2,1,0:T(8,128)(2,1)S(1)}, bf16[3,1024,128]{2,1,0:T(8,128)(2,1)S(1)}) custom-call(s32[1]{0:T(128)} %bitcast.1.role, bf16[16,1024,128]{2,1,0:T(8,128)(2,1)} %bitcast.35), custom_call_target="tpu_custom_call" | custom-call | flops 1000000000 | bytes 8000000 | tf_op jit(solution)/shard_map/pallas_call | solution.py:398
  10.2 0.1 collective-permute-start.4
  10.3 1.4 %collective-permute-start.5 = (bf16[1,1024,128]{2,1,0:T(8,128)(2,1)S(1)}, bf16[1,1024,128]{2,1,0:T(8,128)(2,1)}, u32[]{:S(2)}, u32[]{:S(2)}) collective-permute-start(bf16[1,1024,128]{2,1,0:T(8,128)(2,1)S(1)} %get-tuple-element.22), channel_id=1, source_target_pairs={{0,4},{4,0},{8,12},{12,8},{16,20},{20,16},{24,28},{28,24},{32,36},... | collective-permute-start | bytes 786440 | tf_op jit(solution)/shard_map/ppermute | solution.py:593
  11.8 0.1 collective-permute-start.2
  11.9 0.0 copy-done.3
  11.9 0.0 copy-done.4
  11.9 0.1 pad_add_fusion
  12.0 0.6 slice.18
  12.6 0.9 collective-permute-done
  13.5 0.5 collective-permute-start.1
  14.1 0.0 copy-done.2
  14.1 0.7 pad_maximum_fusion.gates
  14.8 39.3 %collective-permute-done.1 = f32[40,256]{1,0:T(8,128)S(1)} collective-permute-done((f32[40,256]{1,0:T(8,128)S(1)}, f32[40,256]{1,0:T(8,128)S(1)}, u32[]{:S(2)}, u32[]{:S(2)}) %collective-permute-start.1) | collective-permute-done | bytes 40992 | tf_op jit(solution)/shard_map/ppermute | solution.py:593
  54.0 0.0 copy-done
  54.0 0.0 copy-done.1
  54.1 0.1 select_bitcast_fusion.1
  54.1 0.1 broadcast_in_dim.8.scale
  54.2 0.0 collective-permute-done.4.got
  54.2 0.0 collective-permute-done.3.got_0
  54.2 6.0 %shard_map.75 = (bf16[3,512,512]{2,1,0:T(8,128)(2,1)S(1)}, bf16[3,2,512,256]{3,2,1,0:T(8,128)(2,1)S(1)}, f32[3,256,256]{2,1,0:T(8,128)S(1)}, bf16[8,256,256]{2,1,0:T(8,128)(2,1)S(1)}, bf16[1024,128]{1,0:T(8,128)(2,1)S(1)}) custom-call(s32[2]{0:T(128)S(1)} %get-tuple-element.37.role, f32[5]{0:T(128)S(1)} %pad_maximum_fusion.gates, s32[16]{0:T(128)S(1)} %fusion.2.kept, ...), custom_call_target="tpu_custom_call" | custom-call | flops 10000000000 | bytes 8000000 | tf_op jit(solution)/shard_map/pallas_call | solution.py:398
  60.2 0.0 collective-permute-done.5.got
  60.2 13.9 %shard_map.76 = (bf16[4,1024,128]{2,1,0:T(8,128)(2,1)S(1)}, bf16[16,1024,128]{2,1,0:T(8,128)(2,1)}, bf16[5,256,256]{2,1,0:T(8,128)(2,1)S(1)}) custom-call(s32[2]{0:T(128)S(1)} %get-tuple-element.37.role, f32[5]{0:T(128)S(1)} %pad_maximum_fusion.gates, s32[16]{0:T(128)S(1)} %fusion.2.kept, bf16[1,1024,128]{2,1,0:T(8,128)(2,1)} %collective-permute-done.5.got, ...), custom_call_target="tpu_custom_call" | custom-call | flops 10000000000 | bytes 8000000 | tf_op jit(solution)/shard_map/pallas_call | solution.py:398
  74.2 1.3 %collective-permute-start.7 = (bf16[4,1024,128]{2,1,0:T(8,128)(2,1)S(1)}, bf16[4,1024,128]{2,1,0:T(8,128)(2,1)S(1)}, u32[]{:S(2)}, u32[]{:S(2)}) collective-permute-start(bf16[4,1024,128]{2,1,0:T(8,128)(2,1)S(1)} %get-tuple-element.30), channel_id=1, source_target_pairs={{0,4},{4,0},{8,12},{12,8},{16,20},{20,16},{24,28},{28,24},{32,36},... | collective-permute-start | bytes 3145736 | tf_op jit(solution)/shard_map/ppermute | solution.py:593
  75.4 0.0 collective-permute-done.2.got
  75.4 17.7 %shard_map.77 = (bf16[4,1024,128]{2,1,0:T(8,128)(2,1)S(1)}, bf16[16,1024,128]{2,1,0:T(8,128)(2,1)}, bf16[1024,128]{1,0:T(8,128)(2,1)S(1)}) custom-call(s32[2]{0:T(128)S(1)} %get-tuple-element.36.role, f32[5]{0:T(128)S(1)} %pad_maximum_fusion.gates, s32[16]{0:T(128)S(1)} %fusion.2.kept, ...), custom_call_target="tpu_custom_call", output_to_operand_aliasing={{1}: (9, {})} | custom-call | flops 10000000000 | bytes 8000000 | tf_op jit(solution)/shard_map/pallas_call | solution.py:398
  93.1 0.4 collective-permute-start.6
  93.5 4.0 %collective-permute-done.7.block = bf16[4,1024,128]{2,1,0:T(8,128)(2,1)S(1)} collective-permute-done((bf16[4,1024,128]{2,1,0:T(8,128)(2,1)S(1)}, bf16[4,1024,128]{2,1,0:T(8,128)(2,1)S(1)}, u32[]{:S(2)}, u32[]{:S(2)}) %collective-permute-start.7) | collective-permute-done | bytes 1048608 | tf_op jit(solution)/shard_map/ppermute | solution.py:593
  97.4 1.0 place.2.refs_0_
  98.5 21.5 %collective-permute-done.6.block = bf16[4,1024,128]{2,1,0:T(8,128)(2,1)S(1)} collective-permute-done((bf16[4,1024,128]{2,1,0:T(8,128)(2,1)S(1)}, bf16[4,1024,128]{2,1,0:T(8,128)(2,1)S(1)}, u32[]{:S(2)}, u32[]{:S(2)}) %collective-permute-start.6) | collective-permute-done | bytes 1048608 | tf_op jit(solution)/shard_map/ppermute | solution.py:593
  119.9 1.0 place.3
  (6 shorter events, 0.0 us)
Async XLA Ops:
  0.8 12.7 %collective-permute-start = (f32[16,256]{1,0:T(8,128)S(1)}, f32[16,256]{1,0:T(8,128)S(1)}, u32[]{:S(2)}, u32[]{:S(2)}) collective-permute-start(f32[16,256]{1,0:T(8,128)S(1)} %bitcast_select_fusion), channel_id=1, source_target_pairs={{4,8},{12,16},{20,24},{28,32},{36,40},{44,48},{52,56},{60,64},{68,... | collective-permute-start | bytes 49160 | tf_op jit(solution)/shard_map/ppermute | solution.py:600
  2.1 9.8 %copy-start.3 = (s32[1,1,16]{2,1,0:T(1,128)S(1)}, s32[1,1,16]{2,1,0:T(1,128)}, u32[]{:S(2)}) copy-start(s32[1,1,16]{2,1,0:T(1,128)} %param.10) | copy-start | bytes 196
  2.1 9.8 %copy-start.4 = (f32[3]{0:T(128)S(1)}, f32[3]{0:T(128)}, u32[]{:S(2)}) copy-start(f32[3]{0:T(128)} %param.13) | copy-start | bytes 40
  2.1 12.0 %copy-start.2 = (f32[2]{0:T(128)S(1)}, f32[2]{0:T(128)}, u32[]{:S(2)}) copy-start(f32[2]{0:T(128)} %param.12) | copy-start | bytes 28
  2.1 51.9 %copy-start = (f32[1,1,16,256]{3,2,1,0:T(8,128)S(1)}, f32[1,1,16,256]{3,2,1,0:T(8,128)}, u32[]{:S(2)}) copy-start(f32[1,1,16,256]{3,2,1,0:T(8,128)} %param.8) | copy-start | bytes 49156
  2.1 51.9 %copy-start.1 = (s32[1,1,16]{2,1,0:T(1,128)S(1)}, s32[1,1,16]{2,1,0:T(1,128)}, u32[]{:S(2)}) copy-start(s32[1,1,16]{2,1,0:T(1,128)} %param.9) | copy-start | bytes 196
  3.3 50.9 %collective-permute-start.3 = (bf16[3,1024,128]{2,1,0:T(8,128)(2,1)S(1)}, bf16[3,1024,128]{2,1,0:T(8,128)(2,1)S(1)}, u32[]{:S(2)}, u32[]{:S(2)}) collective-permute-start(bf16[3,1024,128]{2,1,0:T(8,128)(2,1)S(1)} %shard_map.74), channel_id=1, source_target_pairs={{0,4},{4,0},{8,12},{12,8},{16,20},{20,16},{24,28},{28,24},{32,36},... | collective-permute-start | bytes 2359304 | tf_op jit(solution)/shard_map/ppermute | solution.py:593
  10.2 44.0 %collective-permute-start.4 = (bf16[1,1024,128]{2,1,0:T(8,128)(2,1)}, bf16[1,1024,128]{2,1,0:T(8,128)(2,1)}, u32[]{:S(2)}, u32[]{:S(2)}) collective-permute-start(bf16[1,1024,128]{2,1,0:T(8,128)(2,1)} %get-tuple-element.20), channel_id=1, source_target_pairs={{0,4},{4,0},{8,12},{12,8},{16,20},{20,16},{24,28},{28,24},{32,36},... | collective-permute-start | bytes 786440 | tf_op jit(solution)/shard_map/ppermute | solution.py:593
  10.3 49.9 %collective-permute-start.5 = (bf16[1,1024,128]{2,1,0:T(8,128)(2,1)S(1)}, bf16[1,1024,128]{2,1,0:T(8,128)(2,1)}, u32[]{:S(2)}, u32[]{:S(2)}) collective-permute-start(bf16[1,1024,128]{2,1,0:T(8,128)(2,1)S(1)} %get-tuple-element.22), channel_id=1, source_target_pairs={{0,4},{4,0},{8,12},{12,8},{16,20},{20,16},{24,28},{28,24},{32,36},... | collective-permute-start | bytes 786440 | tf_op jit(solution)/shard_map/ppermute | solution.py:593
  11.8 63.7 %collective-permute-start.2 = (bf16[3,1024,128]{2,1,0:T(8,128)(2,1)S(1)}, bf16[3,1024,128]{2,1,0:T(8,128)(2,1)S(1)}, u32[]{:S(2)}, u32[]{:S(2)}) collective-permute-start(bf16[3,1024,128]{2,1,0:T(8,128)(2,1)S(1)} %get-tuple-element.19), channel_id=1, source_target_pairs={{0,4},{4,0},{8,12},{12,8},{16,20},{20,16},{24,28},{28,24},{32,36},... | collective-permute-start | bytes 2359304 | tf_op jit(solution)/shard_map/ppermute | solution.py:593
  13.5 40.5 %collective-permute-start.1 = (f32[40,256]{1,0:T(8,128)S(1)}, f32[40,256]{1,0:T(8,128)S(1)}, u32[]{:S(2)}, u32[]{:S(2)}) collective-permute-start(f32[40,256]{1,0:T(8,128)S(1)} %select_maximum_fusion.2), channel_id=1, source_target_pairs={{0,4},{4,0},{8,12},{12,8},{16,20},{20,16},{24,28},{28,24},{32,36},... | collective-permute-start | bytes 122888 | tf_op jit(solution)/shard_map/ppermute | solution.py:593
  74.2 23.3 %collective-permute-start.7 = (bf16[4,1024,128]{2,1,0:T(8,128)(2,1)S(1)}, bf16[4,1024,128]{2,1,0:T(8,128)(2,1)S(1)}, u32[]{:S(2)}, u32[]{:S(2)}) collective-permute-start(bf16[4,1024,128]{2,1,0:T(8,128)(2,1)S(1)} %get-tuple-element.30), channel_id=1, source_target_pairs={{0,4},{4,0},{8,12},{12,8},{16,20},{20,16},{24,28},{28,24},{32,36},... | collective-permute-start | bytes 3145736 | tf_op jit(solution)/shard_map/ppermute | solution.py:593
  93.1 26.8 %collective-permute-start.6 = (bf16[4,1024,128]{2,1,0:T(8,128)(2,1)S(1)}, bf16[4,1024,128]{2,1,0:T(8,128)(2,1)S(1)}, u32[]{:S(2)}, u32[]{:S(2)}) collective-permute-start(bf16[4,1024,128]{2,1,0:T(8,128)(2,1)S(1)} %get-tuple-element.29), channel_id=1, source_target_pairs={{0,4},{4,0},{8,12},{12,8},{16,20},{20,16},{24,28},{28,24},{32,36},... | collective-permute-start | bytes 3145736 | tf_op jit(solution)/shard_map/ppermute | solution.py:593

commit v4 on v3

--- a/solution.py
+++ b/solution.py
@@ -1,5 +1,3 @@
-import functools
-
 import jax
 import jax.numpy as jnp
 from jax import lax
@@ -217,7 +215,7 @@
         scaled[b] = (solved * 16.0).astype(bf16)
 
 
-def deliver(role, scaled, mixed, wide, ready, msg, out, sems):
+def deliver(role, scaled, mixed, wide, ready, msg, out, sems, halved):
     is_right = role[0] == 1
     copies = []
     for b in range(BATCH):
@@ -233,29 +231,36 @@
                 right_wide[lines, :] = right_part[:, lanes_of(2 * s + jb)]
         left_site = left_wide[...]
         right_site = right_wide[...]
-        msg[b] = jnp.where(is_right, left_site, right_site).astype(bf16)
+        if not halved:
+            msg[b] = jnp.where(is_right, left_site, right_site).astype(bf16)
+        elif b + 1 < BATCH:
+            lines = slice(b * 4 * SIZE, (b + 1) * 4 * SIZE)
+            msg[lines, :] = jnp.where(is_right, left_site, right_site).astype(bf16)
+        else:
+            for jb in range(2):
+                lines = slice((12 + jb) * SIZE, (13 + jb) * SIZE)
+                half = scaled[b, UPPER, lanes_of(jb)].astype(f32)
+                msg[lines, :] = jnp.where(is_right, half, right_part[:, lanes_of(jb)]).astype(bf16)
         ready[b] = jnp.where(is_right, right_site, left_site).astype(bf16)
         copies.append(pltpu.make_async_copy(ready.at[b], out.at[role[1] + b], sems.at[b]))
         copies[-1].start()
     return copies
 
 
-def windows(role, own, sketches, own_win, sketch, sems):
+def windows(first, own, sketches, own_win, sketch, sems):
     count = own_win.shape[0]
 
     def own_copy(t):
-        at = jnp.clip(role[1] - 1 + t, 0, own.shape[0] - 1)
+        at = jnp.clip(first - 1 + t, 0, own.shape[0] - 1)
         return pltpu.make_async_copy(own.at[at], own_win.at[t], sems.at[t])
 
-    sketch_copy = pltpu.make_async_copy(
-        sketches.at[pl.ds(role[1], BATCH)], sketch, sems.at[count]
-    )
+    sketch_copy = pltpu.make_async_copy(sketches.at[pl.ds(first, BATCH)], sketch, sems.at[count])
     return own_copy, sketch_copy
 
 
 def early_kernel(role, gates, kept, own, got_0, got, scale, sketches, *refs):
     mixed, samp, gram, edge, own_low, left_w, right_w, wide, own_win, sketch, sems = refs
-    own_copy, sketch_copy = windows(role, own, sketches, own_win, sketch, sems)
+    own_copy, sketch_copy = windows(role[1], own, sketches, own_win, sketch, sems)
     for t in (1, 2, 3, 4, 5, 0):
         own_copy(t).start()
     sketch_copy.start()
@@ -305,9 +310,16 @@
         )
 
 
-def first_kernel(role, gates, kept, got, scale, *refs):
-    (mixed_e, samp_e, gram_e, edge, own, msg, out, carry), refs = refs[:8], refs[8:]
-    mixed, samp, gram, scaled, a_ref, x_ref, wide, ready, sems = refs
+def first_kernel(role, gates, kept, got, scale, all_own, sketches, *refs):
+    (mixed_e, samp_e, gram_e, edge, own), refs = refs[:5], refs[5:]
+    (msg, out, carry, own_next, sketch_next), refs = refs[:5], refs[5:]
+    mixed, samp, gram, scaled, a_ref, x_ref, wide, ready, sems, next_sems = refs
+    own_copy, sketch_copy = windows(
+        role[1] - BATCH, all_own, sketches, own_next, sketch_next, next_sems
+    )
+    for t in range(4):
+        own_copy(t).start()
+    sketch_copy.start()
     left, right = carry.at[pl.ds(1, 2)], carry.at[pl.ds(3, 2)]
     weigh(0, role, own, got.at[0], scale, left, right, wide)
     sample(
@@ -329,23 +341,21 @@
     solve(gram, samp, scaled, a_ref, x_ref)
     scaled[BATCH, LOWER, :] = jnp.zeros((SIZE, SIZE), bf16)
     carry[0] = scaled[0, LOWER, :]
-    for copy in deliver(role, scaled, mixed, wide, ready, msg, out, sems):
+    for copy in deliver(role, scaled, mixed, wide, ready, msg, out, sems, True):
         copy.wait()
-
-
-def second_kernel(role, gates, kept, own, got, scale, sketches, *refs):
+    for t in range(4):
+        own_copy(t).wait()
+    sketch_copy.wait()
+
+
+def second_kernel(role, gates, kept, own, got, scale, sketch, *refs):
     (edge, carry, _, msg, out, merge), refs = refs[:6], refs[6:]
     left_w, right_w, mixed, samp, gram, scaled, a_ref, x_ref, wide = refs[:9]
-    ready, sems, own_win, sketch, win_sems = refs[9:]
-    own_copy, sketch_copy = windows(role, own, sketches, own_win, sketch, win_sems)
-    for t in range(4):
-        own_copy(t).start()
-    sketch_copy.start()
+    ready, sems = refs[9:]
 
     def step(t, loop):
         at = jnp.maximum(t - 1, 0)
-        own_copy(t).wait()
-        weigh(t, role, own_win.at[t], got.at[at], scale, left_w.at[t], right_w.at[t], wide)
+        weigh(t, role, own.at[t], got.at[at], scale, left_w.at[t], right_w.at[t], wide)
         return loop
 
     lax.fori_loop(0, 4, step, 0)
@@ -354,7 +364,6 @@
         left_w[4, s] = carry[1 + s]
         right_w[4, s] = carry[3 + s]
     right_w[5, 0] = edge[2]
-    sketch_copy.wait()
     for b in range(BATCH):
         t = b + 1
         sample(
@@ -374,7 +383,7 @@
     solve([gram.at[b] for b in every], [samp.at[b] for b in every], scaled, a_ref, x_ref)
     scaled[BATCH, LOWER, :] = carry[0]
     copies = deliver(
-        role, scaled, [mixed.at[b] for b in every], wide, ready, msg, out, sems
+        role, scaled, [mixed.at[b] for b in every], wide, ready, msg, out, sems, False
     )
     used = jnp.where(role[0] == 1, 0.0, 1.0)
     for jb in range(2):
@@ -456,24 +465,34 @@
     )
 
 
-def first_half(role, gates, kept, got, scale, parts):
+def first_half(role, gates, kept, got, scale, own, sketches, parts):
     return run(
         first_kernel,
-        (role, gates, kept, got, scale, *parts),
-        [SMEM] * 3 + [VMEM] * 7,
-        [shaped(BATCH, *SECTOR), pltpu.HBM((16, *SECTOR), bf16), shaped(5, SIZE, SIZE)],
-        [VMEM, HBM, VMEM],
+        (role, gates, kept, got, scale, in_hbm(own), in_hbm(sketches), *parts),
+        [SMEM] * 3 + [VMEM, VMEM, HBM, HBM] + [VMEM] * 5,
+        [
+            shaped(14 * SIZE, LANES),
+            pltpu.HBM((16, *SECTOR), bf16),
+            shaped(5, SIZE, SIZE),
+            shaped(4, *SECTOR),
+            shaped(BATCH, 2 * SIZE, SIZE),
+        ],
+        [VMEM, HBM, VMEM, VMEM, VMEM],
         sample_shapes(pltpu.VMEM)
         + factor_scratch()
-        + [pltpu.VMEM((BATCH, *SECTOR), bf16), pltpu.SemaphoreType.DMA((BATCH,))],
-    )
-
-
-def second_half(role, gates, kept, own, got, scale, sketches, edge, carry, out):
+        + [
+            pltpu.VMEM((BATCH, *SECTOR), bf16),
+            pltpu.SemaphoreType.DMA((BATCH,)),
+            pltpu.SemaphoreType.DMA((5,)),
+        ],
+    )
+
+
+def second_half(role, gates, kept, own, got, scale, sketch, edge, carry, out):
     return run(
         second_kernel,
-        (role, gates, kept, in_hbm(own), got, scale, in_hbm(sketches), edge, carry, out),
-        [SMEM] * 3 + [HBM, VMEM, VMEM, HBM, VMEM, VMEM, HBM],
+        (role, gates, kept, own, got, scale, sketch, edge, carry, out),
+        [SMEM] * 3 + [VMEM] * 6 + [HBM],
         [shaped(BATCH, *SECTOR), pltpu.HBM((16, *SECTOR), bf16), shaped(*SECTOR)],
         [VMEM, HBM, VMEM],
         [pltpu.VMEM((6, 2, SIZE, SIZE), bf16), pltpu.VMEM((6, 2, SIZE, SIZE), bf16)]
@@ -482,8 +501,7 @@
         + [
             pltpu.VMEM((BATCH, *SECTOR), bf16),
             pltpu.SemaphoreType.DMA((BATCH,)),
-        ]
-        + window_scratch(4),
+        ],
         aliases={9: 1},
     )
 
@@ -536,41 +554,45 @@
     )
 
 
-def place_kernel(merged, at, block, *refs):
-    if merged:
-        merge, _, out, last, sems = refs
-    else:
-        _, out, sems = refs
-    count = block.shape[0]
+def place_kernel(at, block, _, out, sems):
     copies = []
-    for b in range(count):
-        source = block.at[b]
-        if merged and b == count - 1:
-            last[...] = block[b] + merge[...]
-            source = last
-        copies.append(pltpu.make_async_copy(source, out.at[at[0] + b], sems.at[b]))
+    for b in range(block.shape[0]):
+        copies.append(pltpu.make_async_copy(block.at[b], out.at[at[0] + b], sems.at[b]))
         copies[-1].start()
     for copy in copies:
         copy.wait()
 
 
+def place_halved_kernel(at, block, merge, _, out, last, wide, sems):
+    copies = []
+    for b in range(3):
+        lines = pl.ds(b * 4 * SIZE, 4 * SIZE)
+        copies.append(pltpu.make_async_copy(block.at[lines], out.at[at[0] + b], sems.at[b]))
+        copies[-1].start()
+    for jb in range(2):
+        half = block[(12 + jb) * SIZE : (13 + jb) * SIZE, :]
+        wide[lines_of(jb, 0), :] = half.astype(f32)
+        wide[lines_of(jb, 1), :] = jnp.zeros((SIZE, LANES), f32)
+    last[...] = (wide[...] + merge[...].astype(f32)).astype(bf16)
+    copies.append(pltpu.make_async_copy(last, out.at[at[0] + 3], sems.at[3]))
+    copies[-1].start()
+    for copy in copies:
+        copy.wait()
+
+
 def place(out, block, at, merge=None):
-    smem = pl.BlockSpec(memory_space=pltpu.SMEM)
-    vmem = pl.BlockSpec(memory_space=pltpu.VMEM)
-    hbm = pl.BlockSpec(memory_space=pltpu.HBM)
     operands = (jnp.reshape(at, (1,)), block) + (() if merge is None else (merge,)) + (out,)
-    scratch = [] if merge is None else [pltpu.VMEM(merge.shape, bf16)]
-    return pl.pallas_call(
-        functools.partial(place_kernel, merge is not None),
-        out_shape=pltpu.HBM(out.shape, out.dtype),
-        in_specs=[smem] + [vmem] * (len(operands) - 2) + [hbm],
-        out_specs=hbm,
-        scratch_shapes=scratch + [pltpu.SemaphoreType.DMA((block.shape[0],))],
-        input_output_aliases={len(operands) - 1: 0},
-        compiler_params=pltpu.CompilerParams(vmem_limit_bytes=8 * 2**20),
-        cost_estimate=pl.CostEstimate(flops=1000000, bytes_accessed=2_000_000, transcendentals=0),
-        name="place",
-    )(*operands)
+    scratch = [pltpu.VMEM(SECTOR, bf16), pltpu.VMEM(SECTOR, f32)] if merge is not None else []
+    return run(
+        place_kernel if merge is None else place_halved_kernel,
+        operands,
+        [SMEM] + [VMEM] * (len(operands) - 2) + [HBM],
+        [pltpu.HBM(out.shape, out.dtype)],
+        [HBM],
+        scratch + [pltpu.SemaphoreType.DMA((4,))],
+        aliases={len(operands) - 1: 0},
+        mib=4,
+    )[0]
 
 
 def to_lines(x):
@@ -629,10 +651,12 @@
     role_b = jnp.stack([flag, first_b])
 
     parts = early(role_a, gates, kept, own, got_0, got_a, scale, sketches)
-    msg_a, out, carry = first_half(role_a, gates, kept, got_low, scale, parts)
+    msg_a, out, carry, own_b, sketch_b = first_half(
+        role_a, gates, kept, got_low, scale, own, sketches, parts
+    )
     back_a = swapped(msg_a)
     msg_b, out, merge = second_half(
-        role_b, gates, kept, own, got_b, scale, sketches, parts[3], carry, out
+        role_b, gates, kept, own_b, got_b, scale, sketch_b, parts[3], carry, out
     )
     back_b = swapped(msg_b)
 

time: 122 us -> 120 us (0.984)
  waiting for transfers between devices: 65.6 us -> 63.9 us
    pallas_call x2 -> x0, Pallas kernels: 1.99 us -> none  [place(): pl.pallas_call(functools.partial(place_kernel, merge is not None), out_sh...]
    ppermute x7, waiting for transfers between devices: 64.7 us -> 63.1 us  [swapped(): return lax.ppermute(value, 'chain', [(i, i ^ 1) for i in range(chain)])]
    pallas_call x5 -> x7, Pallas kernels: 40.8 us -> 42.3 us  [run(): pl.pallas_call(kernel, out_shape=outs, in_specs=specs, out_specs=out_spec...]
where the time goes in v4:
time: 120 us; the launch traced here: 119 us
  waiting for transfers between devices  63.9 us (53%)
  Pallas kernels  42.3 us (35%)
  starting transfers between devices  10.1 us (8%)
  other arithmetic  1.68 us (1%)
    ppermute x7, waiting for transfers between devices, swapped(): return lax.ppermute(value, 'chain', [(i, i ^ 1) for i in range(chain)])  63.1 us
    pallas_call x7, Pallas kernels, run(): pl.pallas_call(kernel, out_shape=outs, in_specs=specs, out_specs=out_spec...  42.3 us
    ppermute x7, starting transfers between devices, swapped(): return lax.ppermute(value, 'chain', [(i, i ^ 1) for i in range(chain)])  8.86 us
  transfers between devices with their start and end apart: 8, of which 4 were waited for; matrix products, arithmetic and copies ran while one was open for 1% of the time, Pallas kernels for 35%

profile of v4, /device:TPU:1, one launch (start us, length us, event | category | flops | bytes accessed | tf_op | source)
XLA Modules:
  0.0 119.1 jit_solution(5442861487227269203)
XLA Ops:
  0.0 0.8 bitcast_select_fusion
  0.8 1.3 %collective-permute-start = (f32[16,256]{1,0:T(8,128)S(1)}, f32[16,256]{1,0:T(8,128)S(1)}, u32[]{:S(2)}, u32[]{:S(2)}) collective-permute-start(f32[16,256]{1,0:T(8,128)S(1)} %bitcast_select_fusion), channel_id=1, source_target_pairs={{4,8},{12,16},{20,24},{28,32},{36,40},{44,48},{52,56},{60,64},{68,... | collective-permute-start | bytes 49160 | tf_op jit(solution)/shard_map/ppermute | solution.py:622
  2.1 0.0 copy-start.3
  2.1 0.0 copy-start.4
  2.1 0.0 copy-start.2
  2.1 0.0 copy-start
  2.1 0.0 copy-start.1
  2.2 1.2 shard_map.74
  3.3 4.8 %collective-permute-start.3 = (bf16[3,1024,128]{2,1,0:T(8,128)(2,1)S(1)}, bf16[3,1024,128]{2,1,0:T(8,128)(2,1)S(1)}, u32[]{:S(2)}, u32[]{:S(2)}) collective-permute-start(bf16[3,1024,128]{2,1,0:T(8,128)(2,1)S(1)} %shard_map.74), channel_id=1, source_target_pairs={{0,4},{4,0},{8,12},{12,8},{16,20},{20,16},{24,28},{28,24},{32,36},... | collective-permute-start | bytes 2359304 | tf_op jit(solution)/shard_map/ppermute | solution.py:615
  8.1 2.2 %shard_map.73 = (bf16[1,1024,128]{2,1,0:T(8,128)(2,1)}, bf16[1,1024,128]{2,1,0:T(8,128)(2,1)}, bf16[3,1024,128]{2,1,0:T(8,128)(2,1)S(1)}) custom-call(s32[1]{0:T(128)} %bitcast.1.role, bf16[16,1024,128]{2,1,0:T(8,128)(2,1)} %bitcast.35), custom_call_target="tpu_custom_call" | custom-call | flops 1000000000 | bytes 8000000 | tf_op jit(solution)/shard_map/pallas_call | solution.py:407
  10.3 0.1 collective-permute-start.2
  10.4 1.4 %collective-permute-start.4 = (bf16[1,1024,128]{2,1,0:T(8,128)(2,1)}, bf16[1,1024,128]{2,1,0:T(8,128)(2,1)}, u32[]{:S(2)}, u32[]{:S(2)}) collective-permute-start(bf16[1,1024,128]{2,1,0:T(8,128)(2,1)} %get-tuple-element.22), channel_id=1, source_target_pairs={{0,4},{4,0},{8,12},{12,8},{16,20},{20,16},{24,28},{28,24},{32,36},... | collective-permute-start | bytes 786440 | tf_op jit(solution)/shard_map/ppermute | solution.py:615
  11.9 0.1 collective-permute-start.5
  12.0 0.0 copy-done.3
  12.0 0.0 copy-done.4
  12.0 0.1 pad_add_fusion
  12.1 0.6 slice.18
  12.7 0.8 collective-permute-done
  13.5 0.6 collective-permute-start.1
  14.2 0.0 copy-done.2
  14.2 0.7 pad_maximum_fusion.gates
  14.9 39.2 %collective-permute-done.1 = f32[40,256]{1,0:T(8,128)S(1)} collective-permute-done((f32[40,256]{1,0:T(8,128)S(1)}, f32[40,256]{1,0:T(8,128)S(1)}, u32[]{:S(2)}, u32[]{:S(2)}) %collective-permute-start.1) | collective-permute-done | bytes 40992 | tf_op jit(solution)/shard_map/ppermute | solution.py:615
  54.0 0.0 copy-done
  54.0 0.0 copy-done.1
  54.1 0.1 select_bitcast_fusion.1
  54.1 0.1 broadcast_in_dim.8.scale
  54.2 0.0 collective-permute-done.4.got
  54.2 0.0 collective-permute-done.3.got_0
  54.2 5.8 %shard_map.75 = (bf16[3,512,512]{2,1,0:T(8,128)(2,1)S(1)}, bf16[3,2,512,256]{3,2,1,0:T(8,128)(2,1)S(1)}, f32[3,256,256]{2,1,0:T(8,128)S(1)}, bf16[8,256,256]{2,1,0:T(8,128)(2,1)S(1)}, bf16[1024,128]{1,0:T(8,128)(2,1)S(1)}) custom-call(s32[2]{0:T(128)S(1)} %get-tuple-element.41.role, f32[5]{0:T(128)S(1)} %pad_maximum_fusion.gates, s32[16]{0:T(128)S(1)} %fusion.2.kept, ...), custom_call_target="tpu_custom_call" | custom-call | flops 10000000000 | bytes 8000000 | tf_op jit(solution)/shard_map/pallas_call | solution.py:407
  60.0 0.0 collective-permute-done.2.got
  60.1 14.4 %shard_map.76 = (bf16[3584,128]{1,0:T(8,128)(2,1)S(1)}, bf16[16,1024,128]{2,1,0:T(8,128)(2,1)}, bf16[5,256,256]{2,1,0:T(8,128)(2,1)S(1)}, bf16[4,1024,128]{2,1,0:T(8,128)(2,1)S(1)}, bf16[4,512,256]{2,1,0:T(8,128)(2,1)S(1)}) custom-call(s32[2]{0:T(128)S(1)} %get-tuple-element.41.role, f32[5]{0:T(128)S(1)} %pad_maximum_fusion.gates, s32[16]{0:T(128)S(1)} %fusion.2.kept, ...), custom_call_target="tpu_custom_call" | custom-call | flops 10000000000 | bytes 8000000 | tf_op jit(solution)/shard_map/pallas_call | solution.py:407
  74.5 1.4 %collective-permute-start.7 = (bf16[3584,128]{1,0:T(8,128)(2,1)S(1)}, bf16[3584,128]{1,0:T(8,128)(2,1)S(1)}, u32[]{:S(2)}, u32[]{:S(2)}) collective-permute-start(bf16[3584,128]{1,0:T(8,128)(2,1)S(1)} %get-tuple-element.34), channel_id=1, source_target_pairs={{0,4},{4,0},{8,12},{12,8},{16,20},{20,16},{24,28},{28,24},{32,36},... | collective-permute-start | bytes 2752520 | tf_op jit(solution)/shard_map/ppermute | solution.py:615
  75.9 0.0 collective-permute-done.5.got
  76.0 16.7 %shard_map.77 = (bf16[4,1024,128]{2,1,0:T(8,128)(2,1)S(1)}, bf16[16,1024,128]{2,1,0:T(8,128)(2,1)}, bf16[1024,128]{1,0:T(8,128)(2,1)S(1)}) custom-call(s32[2]{0:T(128)S(1)} %get-tuple-element.40.role, f32[5]{0:T(128)S(1)} %pad_maximum_fusion.gates, s32[16]{0:T(128)S(1)} %fusion.2.kept, ...), custom_call_target="tpu_custom_call", output_to_operand_aliasing={{1}: (9, {})} | custom-call | flops 10000000000 | bytes 8000000 | tf_op jit(solution)/shard_map/pallas_call | solution.py:407
  92.7 0.4 collective-permute-start.6
  93.0 2.1 %collective-permute-done.7.block = bf16[3584,128]{1,0:T(8,128)(2,1)S(1)} collective-permute-done((bf16[3584,128]{1,0:T(8,128)(2,1)S(1)}, bf16[3584,128]{1,0:T(8,128)(2,1)S(1)}, u32[]{:S(2)}, u32[]{:S(2)}) %collective-permute-start.7) | collective-permute-done | bytes 917536 | tf_op jit(solution)/shard_map/ppermute | solution.py:615
  95.1 1.0 shard_map.78._
  96.2 21.8 %collective-permute-done.6.block = bf16[4,1024,128]{2,1,0:T(8,128)(2,1)S(1)} collective-permute-done((bf16[4,1024,128]{2,1,0:T(8,128)(2,1)S(1)}, bf16[4,1024,128]{2,1,0:T(8,128)(2,1)S(1)}, u32[]{:S(2)}, u32[]{:S(2)}) %collective-permute-start.6) | collective-permute-done | bytes 1048608 | tf_op jit(solution)/shard_map/ppermute | solution.py:615
  117.9 1.0 shard_map.79
  (6 shorter events, 0.0 us)
Async XLA Ops:
  0.8 12.7 %collective-permute-start = (f32[16,256]{1,0:T(8,128)S(1)}, f32[16,256]{1,0:T(8,128)S(1)}, u32[]{:S(2)}, u32[]{:S(2)}) collective-permute-start(f32[16,256]{1,0:T(8,128)S(1)} %bitcast_select_fusion), channel_id=1, source_target_pairs={{4,8},{12,16},{20,24},{28,32},{36,40},{44,48},{52,56},{60,64},{68,... | collective-permute-start | bytes 49160 | tf_op jit(solution)/shard_map/ppermute | solution.py:622
  2.1 9.9 %copy-start.3 = (s32[1,1,16]{2,1,0:T(1,128)S(1)}, s32[1,1,16]{2,1,0:T(1,128)}, u32[]{:S(2)}) copy-start(s32[1,1,16]{2,1,0:T(1,128)} %param.10) | copy-start | bytes 196
  2.1 9.9 %copy-start.4 = (f32[3]{0:T(128)S(1)}, f32[3]{0:T(128)}, u32[]{:S(2)}) copy-start(f32[3]{0:T(128)} %param.13) | copy-start | bytes 40
  2.1 12.0 %copy-start.2 = (f32[2]{0:T(128)S(1)}, f32[2]{0:T(128)}, u32[]{:S(2)}) copy-start(f32[2]{0:T(128)} %param.12) | copy-start | bytes 28
  2.1 51.9 %copy-start = (f32[1,1,16,256]{3,2,1,0:T(8,128)S(1)}, f32[1,1,16,256]{3,2,1,0:T(8,128)}, u32[]{:S(2)}) copy-start(f32[1,1,16,256]{3,2,1,0:T(8,128)} %param.8) | copy-start | bytes 49156
  2.1 51.9 %copy-start.1 = (s32[1,1,16]{2,1,0:T(1,128)S(1)}, s32[1,1,16]{2,1,0:T(1,128)}, u32[]{:S(2)}) copy-start(s32[1,1,16]{2,1,0:T(1,128)} %param.9) | copy-start | bytes 196
  3.3 50.9 %collective-permute-start.3 = (bf16[3,1024,128]{2,1,0:T(8,128)(2,1)S(1)}, bf16[3,1024,128]{2,1,0:T(8,128)(2,1)S(1)}, u32[]{:S(2)}, u32[]{:S(2)}) collective-permute-start(bf16[3,1024,128]{2,1,0:T(8,128)(2,1)S(1)} %shard_map.74), channel_id=1, source_target_pairs={{0,4},{4,0},{8,12},{12,8},{16,20},{20,16},{24,28},{28,24},{32,36},... | collective-permute-start | bytes 2359304 | tf_op jit(solution)/shard_map/ppermute | solution.py:615
  10.3 49.7 %collective-permute-start.2 = (bf16[1,1024,128]{2,1,0:T(8,128)(2,1)}, bf16[1,1024,128]{2,1,0:T(8,128)(2,1)S(1)}, u32[]{:S(2)}, u32[]{:S(2)}) collective-permute-start(bf16[1,1024,128]{2,1,0:T(8,128)(2,1)} %get-tuple-element.21), channel_id=1, source_target_pairs={{0,4},{4,0},{8,12},{12,8},{16,20},{20,16},{24,28},{28,24},{32,36},... | collective-permute-start | bytes 786440 | tf_op jit(solution)/shard_map/ppermute | solution.py:615
  10.4 43.8 %collective-permute-start.4 = (bf16[1,1024,128]{2,1,0:T(8,128)(2,1)}, bf16[1,1024,128]{2,1,0:T(8,128)(2,1)}, u32[]{:S(2)}, u32[]{:S(2)}) collective-permute-start(bf16[1,1024,128]{2,1,0:T(8,128)(2,1)} %get-tuple-element.22), channel_id=1, source_target_pairs={{0,4},{4,0},{8,12},{12,8},{16,20},{20,16},{24,28},{28,24},{32,36},... | collective-permute-start | bytes 786440 | tf_op jit(solution)/shard_map/ppermute | solution.py:615
  11.9 64.1 %collective-permute-start.5 = (bf16[3,1024,128]{2,1,0:T(8,128)(2,1)S(1)}, bf16[3,1024,128]{2,1,0:T(8,128)(2,1)S(1)}, u32[]{:S(2)}, u32[]{:S(2)}) collective-permute-start(bf16[3,1024,128]{2,1,0:T(8,128)(2,1)S(1)} %get-tuple-element.29), channel_id=1, source_target_pairs={{0,4},{4,0},{8,12},{12,8},{16,20},{20,16},{24,28},{28,24},{32,36},... | collective-permute-start | bytes 2359304 | tf_op jit(solution)/shard_map/ppermute | solution.py:615
  13.5 40.5 %collective-permute-start.1 = (f32[40,256]{1,0:T(8,128)S(1)}, f32[40,256]{1,0:T(8,128)S(1)}, u32[]{:S(2)}, u32[]{:S(2)}) collective-permute-start(f32[40,256]{1,0:T(8,128)S(1)} %select_maximum_fusion.2), channel_id=1, source_target_pairs={{0,4},{4,0},{8,12},{12,8},{16,20},{20,16},{24,28},{28,24},{32,36},... | collective-permute-start | bytes 122888 | tf_op jit(solution)/shard_map/ppermute | solution.py:615
  74.5 20.6 %collective-permute-start.7 = (bf16[3584,128]{1,0:T(8,128)(2,1)S(1)}, bf16[3584,128]{1,0:T(8,128)(2,1)S(1)}, u32[]{:S(2)}, u32[]{:S(2)}) collective-permute-start(bf16[3584,128]{1,0:T(8,128)(2,1)S(1)} %get-tuple-element.34), channel_id=1, source_target_pairs={{0,4},{4,0},{8,12},{12,8},{16,20},{20,16},{24,28},{28,24},{32,36},... | collective-permute-start | bytes 2752520 | tf_op jit(solution)/shard_map/ppermute | solution.py:615
  92.7 25.3 %collective-permute-start.6 = (bf16[4,1024,128]{2,1,0:T(8,128)(2,1)S(1)}, bf16[4,1024,128]{2,1,0:T(8,128)(2,1)S(1)}, u32[]{:S(2)}, u32[]{:S(2)}) collective-permute-start(bf16[4,1024,128]{2,1,0:T(8,128)(2,1)S(1)} %get-tuple-element.33), channel_id=1, source_target_pairs={{0,4},{4,0},{8,12},{12,8},{16,20},{20,16},{24,28},{28,24},{32,36},... | collective-permute-start | bytes 3145736 | tf_op jit(solution)/shard_map/ppermute | solution.py:615

commit v5 on v4

--- a/solution.py
+++ b/solution.py
@@ -258,21 +258,15 @@
     return own_copy, sketch_copy
 
 
-def early_kernel(role, gates, kept, own, got_0, got, scale, sketches, *refs):
-    mixed, samp, gram, edge, own_low, left_w, right_w, wide, own_win, sketch, sems = refs
-    own_copy, sketch_copy = windows(role[1], own, sketches, own_win, sketch, sems)
-    for t in (1, 2, 3, 4, 5, 0):
-        own_copy(t).start()
-    sketch_copy.start()
+def early_kernel(role, gates, kept, own, got_0, got, scale, sketch, *refs):
+    mixed, samp, gram, edge, left_w, right_w, wide = refs
 
     def step(t, loop):
-        own_copy(t).wait()
-        weigh(t, role, own_win.at[t], got.at[0], scale, left_w.at[t], right_w.at[t], wide)
+        weigh(t, role, own.at[t], got.at[0], scale, left_w.at[t], right_w.at[t], wide)
         return loop
 
     def step_0(t, loop):
-        own_copy(t).wait()
-        weigh(t, role, own_win.at[t], got_0.at[t - 1], scale, left_w.at[t], right_w.at[t], wide)
+        weigh(t, role, own.at[t], got_0.at[t - 1], scale, left_w.at[t], right_w.at[t], wide)
         return loop
 
     lax.fori_loop(1, 4, step_0, 0)
@@ -288,11 +282,6 @@
     for jb in range(2):
         lanes = lanes_of(jb)
         edge[5, :, lanes] = ((wide[0, lines_of(jb, 1), :] * rows) * col[:, lanes]).astype(bf16)
-    own_copy(0).wait()
-    own_low[...] = own_win[0]
-    sketch_copy.wait()
-    edge[6] = sketch[0, UPPER]
-    edge[7] = sketch[0, LOWER]
     for b in range(1, BATCH):
         t = b + 1
         sample(
@@ -310,22 +299,15 @@
         )
 
 
-def first_kernel(role, gates, kept, got, scale, all_own, sketches, *refs):
-    (mixed_e, samp_e, gram_e, edge, own), refs = refs[:5], refs[5:]
-    (msg, out, carry, own_next, sketch_next), refs = refs[:5], refs[5:]
-    mixed, samp, gram, scaled, a_ref, x_ref, wide, ready, sems, next_sems = refs
-    own_copy, sketch_copy = windows(
-        role[1] - BATCH, all_own, sketches, own_next, sketch_next, next_sems
-    )
-    for t in range(4):
-        own_copy(t).start()
-    sketch_copy.start()
+def first_kernel(role, gates, kept, own, got, scale, sketch, *refs):
+    (mixed_e, samp_e, gram_e, edge, msg, out, carry), refs = refs[:7], refs[7:]
+    mixed, samp, gram, scaled, a_ref, x_ref, wide, ready, sems = refs
     left, right = carry.at[pl.ds(1, 2)], carry.at[pl.ds(3, 2)]
-    weigh(0, role, own, got.at[0], scale, left, right, wide)
+    weigh(0, role, own.at[0], got.at[0], scale, left, right, wide)
     sample(
         gates,
         kept[role[1]],
-        jnp.concatenate([edge[6], edge[7]], axis=0),
+        sketch[0],
         (edge[0], edge[1]),
         (left[0], left[1]),
         (edge[2], edge[3]),
@@ -343,9 +325,6 @@
     carry[0] = scaled[0, LOWER, :]
     for copy in deliver(role, scaled, mixed, wide, ready, msg, out, sems, True):
         copy.wait()
-    for t in range(4):
-        own_copy(t).wait()
-    sketch_copy.wait()
 
 
 def second_kernel(role, gates, kept, own, got, scale, sketch, *refs):
@@ -441,50 +420,31 @@
     ]
 
 
-def window_scratch(count):
-    return [
-        pltpu.VMEM((count, *SECTOR), bf16),
-        pltpu.VMEM((BATCH, 2 * SIZE, SIZE), bf16),
-        pltpu.SemaphoreType.DMA((count + 1,)),
-    ]
-
-
-def early(role, gates, kept, own, got_0, got, scale, sketches):
+def early(role, gates, kept, own, got_0, got, scale, sketch):
     return run(
         early_kernel,
-        (role, gates, kept, in_hbm(own), got_0, got, scale, in_hbm(sketches)),
-        [SMEM] * 3 + [HBM, VMEM, VMEM, VMEM, HBM],
-        sample_shapes(jax.ShapeDtypeStruct, BATCH - 1) + [shaped(8, SIZE, SIZE), shaped(*SECTOR)],
-        [VMEM] * 5,
+        (role, gates, kept, own, got_0, got, scale, sketch),
+        [SMEM] * 3 + [VMEM] * 5,
+        sample_shapes(jax.ShapeDtypeStruct, BATCH - 1) + [shaped(6, SIZE, SIZE)],
+        [VMEM] * 4,
         [
             pltpu.VMEM((6, 2, SIZE, SIZE), bf16),
             pltpu.VMEM((6, 2, SIZE, SIZE), bf16),
             pltpu.VMEM((2, *SECTOR), f32),
-        ]
-        + window_scratch(6),
-    )
-
-
-def first_half(role, gates, kept, got, scale, own, sketches, parts):
+        ],
+    )
+
+
+def first_half(role, gates, kept, own, got, scale, sketch, parts):
     return run(
         first_kernel,
-        (role, gates, kept, got, scale, in_hbm(own), in_hbm(sketches), *parts),
-        [SMEM] * 3 + [VMEM, VMEM, HBM, HBM] + [VMEM] * 5,
-        [
-            shaped(14 * SIZE, LANES),
-            pltpu.HBM((16, *SECTOR), bf16),
-            shaped(5, SIZE, SIZE),
-            shaped(4, *SECTOR),
-            shaped(BATCH, 2 * SIZE, SIZE),
-        ],
-        [VMEM, HBM, VMEM, VMEM, VMEM],
+        (role, gates, kept, own, got, scale, sketch, *parts),
+        [SMEM] * 3 + [VMEM] * 8,
+        [shaped(14 * SIZE, LANES), pltpu.HBM((16, *SECTOR), bf16), shaped(5, SIZE, SIZE)],
+        [VMEM, HBM, VMEM],
         sample_shapes(pltpu.VMEM)
         + factor_scratch()
-        + [
-            pltpu.VMEM((BATCH, *SECTOR), bf16),
-            pltpu.SemaphoreType.DMA((BATCH,)),
-            pltpu.SemaphoreType.DMA((5,)),
-        ],
+        + [pltpu.VMEM((BATCH, *SECTOR), bf16), pltpu.SemaphoreType.DMA((BATCH,))],
     )
 
 
@@ -524,7 +484,8 @@
     )[0]
 
 
-def pack_kernel(role, own, out, low, rest, both, sems):
+def pack_kernel(role, own, sketches, out, low, rest, *refs):
+    own_a, sketch_a, own_b, sketch_b, both, sems, sems_a, sems_b = refs
     flag = role[0]
     copies = [
         pltpu.make_async_copy(own.at[7 + 8 * flag], both.at[0], sems.at[0]),
@@ -532,24 +493,38 @@
         pltpu.make_async_copy(own.at[3 + 8 * flag], low.at[0], sems.at[2]),
         pltpu.make_async_copy(own.at[pl.ds(8 * flag, 3)], rest, sems.at[3]),
     ]
+    first = 12 - 8 * flag
+    for start, own_win, sketch, win_sems in (
+        (first, own_a, sketch_a, sems_a),
+        (first - BATCH, own_b, sketch_b, sems_b),
+    ):
+        own_copy, sketch_copy = windows(start, own, sketches, own_win, sketch, win_sems)
+        copies += [own_copy(t) for t in range(own_win.shape[0])] + [sketch_copy]
     for copy in copies:
         copy.start()
     copies[0].wait()
     copies[1].wait()
     is_odd = lax.broadcasted_iota(jnp.int32, SECTOR, 0) % 2 == 1
     out[0] = jnp.where(is_odd, both[1].astype(f32), both[0].astype(f32)).astype(bf16)
-    copies[2].wait()
-    copies[3].wait()
-
-
-def pack(role, own):
+    for copy in copies[2:]:
+        copy.wait()
+
+
+def pack(role, own, sketches):
+    sketch = shaped(BATCH, 2 * SIZE, SIZE)
     return run(
         pack_kernel,
-        (role, in_hbm(own)),
-        [SMEM, HBM],
-        [shaped(1, *SECTOR), shaped(1, *SECTOR), shaped(3, *SECTOR)],
-        [VMEM] * 3,
-        [pltpu.VMEM((2, *SECTOR), bf16), pltpu.SemaphoreType.DMA((4,))],
+        (role, in_hbm(own), in_hbm(sketches)),
+        [SMEM, HBM, HBM],
+        [shaped(count, *SECTOR) for count in (1, 1, 3)]
+        + [shaped(6, *SECTOR), sketch, shaped(4, *SECTOR), sketch],
+        [VMEM] * 7,
+        [
+            pltpu.VMEM((2, *SECTOR), bf16),
+            pltpu.SemaphoreType.DMA((4,)),
+            pltpu.SemaphoreType.DMA((7,)),
+            pltpu.SemaphoreType.DMA((5,)),
+        ],
         mib=2,
     )
 
@@ -633,7 +608,9 @@
     kept_line = jnp.pad(kept_ranks[0, 0].astype(f32)[None, :], ((0, 7), (0, SIZE - sectors)))
     packed = jnp.concatenate([lam, before, kept_line], axis=0)
     other = swapped(packed)
-    outgoing, outgoing_low, outgoing_b = pack(jnp.reshape(flag, (1,)), own)
+    outgoing, outgoing_low, outgoing_b, own_a, sketch_a, own_b, sketch_b = pack(
+        jnp.reshape(flag, (1,)), own, sketches
+    )
     got_a = swapped(outgoing)
     got_low = swapped(outgoing_low)
     lam_prev = jnp.where(is_right, other[sectors : 2 * sectors], before)
@@ -650,10 +627,8 @@
     role_a = jnp.stack([flag, first_a])
     role_b = jnp.stack([flag, first_b])
 
-    parts = early(role_a, gates, kept, own, got_0, got_a, scale, sketches)
-    msg_a, out, carry, own_b, sketch_b = first_half(
-        role_a, gates, kept, got_low, scale, own, sketches, parts
-    )
+    parts = early(role_a, gates, kept, own_a, got_0, got_a, scale, sketch_a)
+    msg_a, out, carry = first_half(role_a, gates, kept, own_a, got_low, scale, sketch_a, parts)
     back_a = swapped(msg_a)
     msg_b, out, merge = second_half(
         role_b, gates, kept, own_b, got_b, scale, sketch_b, parts[3], carry, out

time: 120 us -> 120 us (level)
  waiting for transfers between devices: 63.9 us -> 59.3 us
  local copies, waits for them, and re-layouts: 0.72 us -> 3.81 us
  Pallas kernels: 42.3 us -> 43.5 us
    ppermute x7, waiting for transfers between devices: 63.1 us -> 59.3 us  [swapped(): return lax.ppermute(value, 'chain', [(i, i ^ 1) for i in range(chain)])]
    unnamed x10 -> x20, local copies, waits for them, and re-layouts: 0.03 us -> 3.21 us
    pallas_call x7, Pallas kernels: 42.3 us -> 43.5 us  [run(): pl.pallas_call(kernel, out_shape=outs, in_specs=specs, out_specs=out_spec...]
  transfers between devices with their start and end apart: 8 -> 8, of which waited for: 4 -> 3; matrix products, arithmetic and copies ran while one was open for 1% -> 1% of each run, Pallas kernels for 35% -> 36%
where the time goes in v5:
time: 120 us
  waiting for transfers between devices  59.3 us (49%)
  Pallas kernels  43.5 us (36%)
  starting transfers between devices  10.9 us (9%)
  local copies, waits for them, and re-layouts  3.81 us (3%)
  other arithmetic  1.61 us (1%)
    ppermute x7, waiting for transfers between devices, swapped(): return lax.ppermute(value, 'chain', [(i, i ^ 1) for i in range(chain)])  59.3 us
    pallas_call x7, Pallas kernels, run(): pl.pallas_call(kernel, out_shape=outs, in_specs=specs, out_specs=out_spec...  43.5 us
    ppermute x7, starting transfers between devices, swapped(): return lax.ppermute(value, 'chain', [(i, i ^ 1) for i in range(chain)])  9.6 us
    unnamed x20, local copies, waits for them, and re-layouts  3.21 us
  transfers between devices with their start and end apart: 8, of which 3 were waited for; matrix products, arithmetic and copies ran while one was open for 1% of the time, Pallas kernels for 36%

profile of v5, /device:TPU:1, one launch (start us, length us, event | category | flops | bytes accessed | tf_op | source)
XLA Modules:
  0.0 119.5 jit_solution(12942003537683755037)
XLA Ops:
  0.0 0.8 bitcast_select_fusion
  0.8 1.3 %collective-permute-start = (f32[16,256]{1,0:T(8,128)S(1)}, f32[16,256]{1,0:T(8,128)S(1)}, u32[]{:S(2)}, u32[]{:S(2)}) collective-permute-start(f32[16,256]{1,0:T(8,128)S(1)} %bitcast_select_fusion), channel_id=1, source_target_pairs={{4,8},{12,16},{20,24},{28,32},{36,40},{44,48},{52,56},{60,64},{68,... | collective-permute-start | bytes 49160 | tf_op jit(solution)/shard_map/ppermute | solution.py:597
  2.1 1.1 shard_map.74
  3.3 4.8 %collective-permute-start.3 = (bf16[3,1024,128]{2,1,0:T(8,128)(2,1)S(1)}, bf16[3,1024,128]{2,1,0:T(8,128)(2,1)}, u32[]{:S(2)}, u32[]{:S(2)}) collective-permute-start(bf16[3,1024,128]{2,1,0:T(8,128)(2,1)S(1)} %shard_map.74), channel_id=1, source_target_pairs={{0,4},{4,0},{8,12},{12,8},{16,20},{20,16},{24,28},{28,24},{32,36},... | collective-permute-start | bytes 2359304 | tf_op jit(solution)/shard_map/ppermute | solution.py:590
  8.0 0.0 copy-start.8
  8.0 0.0 copy-start.9
  8.0 0.0 copy-start.7
  8.0 0.0 copy-start.5
  8.0 0.0 copy-start.6
  8.1 4.1 %shard_map.73 = (bf16[1,1024,128]{2,1,0:T(8,128)(2,1)}, bf16[1,1024,128]{2,1,0:T(8,128)(2,1)}, bf16[3,1024,128]{2,1,0:T(8,128)(2,1)}, bf16[6,1024,128]{2,1,0:T(8...) custom-call(s32[1]{0:T(128)} %bitcast.1.role, ...), custom_call_target="tpu_custom_call" | custom-call | flops 1000000000 | bytes 8000000 | tf_op jit(solution)/shard_map/pallas_call | solution.py:386
  12.2 0.0 copy-start
  12.2 1.0 copy-done
  13.2 0.0 copy-start.2
  13.2 1.0 copy-done.2
  14.1 0.0 collective-permute-start.4
  14.1 1.5 %collective-permute-start.5 = (bf16[1,1024,128]{2,1,0:T(8,128)(2,1)}, bf16[1,1024,128]{2,1,0:T(8,128)(2,1)}, u32[]{:S(2)}, u32[]{:S(2)}) collective-permute-start(bf16[1,1024,128]{2,1,0:T(8,128)(2,1)} %get-tuple-element.29), channel_id=1, source_target_pairs={{0,4},{4,0},{8,12},{12,8},{16,20},{20,16},{24,28},{28,24},{32,36},... | collective-permute-start | bytes 786440 | tf_op jit(solution)/shard_map/ppermute | solution.py:590
  15.6 0.0 collective-permute-start.2
  15.6 0.0 copy-done.8
  15.6 0.0 copy-done.9
  15.6 0.1 pad_add_fusion
  15.7 0.6 slice.18
  16.3 0.0 collective-permute-done
  16.3 1.5 %collective-permute-start.1 = (f32[40,256]{1,0:T(8,128)S(1)}, f32[40,256]{1,0:T(8,128)S(1)}, u32[]{:S(2)}, u32[]{:S(2)}) collective-permute-start(f32[40,256]{1,0:T(8,128)S(1)} %select_maximum_fusion.2), channel_id=1, source_target_pairs={{0,4},{4,0},{8,12},{12,8},{16,20},{20,16},{24,28},{28,24},{32,36},... | collective-permute-start | bytes 122888 | tf_op jit(solution)/shard_map/ppermute | solution.py:590
  17.8 0.0 copy-done.7
  17.8 0.6 pad_maximum_fusion.gates
  18.4 35.6 %collective-permute-done.1 = f32[40,256]{1,0:T(8,128)S(1)} collective-permute-done((f32[40,256]{1,0:T(8,128)S(1)}, f32[40,256]{1,0:T(8,128)S(1)}, u32[]{:S(2)}, u32[]{:S(2)}) %collective-permute-start.1) | collective-permute-done | bytes 40992 | tf_op jit(solution)/shard_map/ppermute | solution.py:590
  54.1 0.0 copy-done.5
  54.1 0.0 copy-done.6
  54.1 0.1 select_bitcast_fusion.1
  54.2 0.1 broadcast_in_dim.8.scale
  54.3 0.0 collective-permute-done.4.got
  54.3 0.0 collective-permute-done.3.got_0
  54.3 0.0 copy-start.3
  54.3 1.2 %copy-done.3 = bf16[4,512,256]{2,1,0:T(8,128)(2,1)S(1)} copy-done((bf16[4,512,256]{2,1,0:T(8,128)(2,1)S(1)}, bf16[4,512,256]{2,1,0:T(8,128)(2,1)}, u32[]{:S(2)}) %copy-start.3) | copy-done | bytes 1048600
  55.5 0.0 copy-start.4
  55.5 5.0 %shard_map.75 = (bf16[3,512,512]{2,1,0:T(8,128)(2,1)S(1)}, bf16[3,2,512,256]{3,2,1,0:T(8,128)(2,1)S(1)}, f32[3,256,256]{2,1,0:T(8,128)S(1)}, bf16[6,256,256]{2,1,0:T(8,128)(2,1)S(1)}) custom-call(s32[2]{0:T(128)S(1)} %get-tuple-element.43.role, f32[5]{0:T(128)S(1)} %pad_maximum_fusion.gates, s32[16]{0:T(128)S(1)} %fusion.2.kept, ...), custom_call_target="tpu_custom_call" | custom-call | flops 10000000000 | bytes 8000000 | tf_op jit(solution)/shard_map/pallas_call | solution.py:386
  60.5 0.0 collective-permute-done.5.got
  60.5 0.0 copy-done.4
  60.5 0.0 copy-start.1
  60.5 14.1 %shard_map.76 = (bf16[3584,128]{1,0:T(8,128)(2,1)S(1)}, bf16[16,1024,128]{2,1,0:T(8,128)(2,1)}, bf16[5,256,256]{2,1,0:T(8,128)(2,1)S(1)}) custom-call(s32[2]{0:T(128)S(1)} %get-tuple-element.43.role, f32[5]{0:T(128)S(1)} %pad_maximum_fusion.gates, s32[16]{0:T(128)S(1)} %fusion.2.kept, bf16[6,1024,128]{2,1,0:T(8,128)(2,1)S(1)} %get-tuple-element.25.own, ...), custom_call_target="tpu_custom_call" | custom-call | flops 10000000000 | bytes 8000000 | tf_op jit(solution)/shard_map/pallas_call | solution.py:386
  74.6 1.4 %collective-permute-start.7 = (bf16[3584,128]{1,0:T(8,128)(2,1)S(1)}, bf16[3584,128]{1,0:T(8,128)(2,1)S(1)}, u32[]{:S(2)}, u32[]{:S(2)}) collective-permute-start(bf16[3584,128]{1,0:T(8,128)(2,1)S(1)} %get-tuple-element.36), channel_id=1, source_target_pairs={{0,4},{4,0},{8,12},{12,8},{16,20},{20,16},{24,28},{28,24},{32,36},... | collective-permute-start | bytes 2752520 | tf_op jit(solution)/shard_map/ppermute | solution.py:590
  76.0 0.0 collective-permute-done.2.got
  76.0 0.0 copy-done.1
  76.0 17.3 %shard_map.77 = (bf16[4,1024,128]{2,1,0:T(8,128)(2,1)S(1)}, bf16[16,1024,128]{2,1,0:T(8,128)(2,1)}, bf16[1024,128]{1,0:T(8,128)(2,1)S(1)}) custom-call(s32[2]{0:T(128)S(1)} %get-tuple-element.42.role, f32[5]{0:T(128)S(1)} %pad_maximum_fusion.gates, s32[16]{0:T(128)S(1)} %fusion.2.kept, ...), custom_call_target="tpu_custom_call", output_to_operand_aliasing={{1}: (9, {})} | custom-call | flops 10000000000 | bytes 8000000 | tf_op jit(solution)/shard_map/pallas_call | solution.py:386
  93.3 0.4 collective-permute-start.6
  93.7 1.7 %collective-permute-done.7.block = bf16[3584,128]{1,0:T(8,128)(2,1)S(1)} collective-permute-done((bf16[3584,128]{1,0:T(8,128)(2,1)S(1)}, bf16[3584,128]{1,0:T(8,128)(2,1)S(1)}, u32[]{:S(2)}, u32[]{:S(2)}) %collective-permute-start.7) | collective-permute-done | bytes 917536 | tf_op jit(solution)/shard_map/ppermute | solution.py:590
  95.3 1.0 shard_map.78._
  96.3 22.0 %collective-permute-done.6.block = bf16[4,1024,128]{2,1,0:T(8,128)(2,1)S(1)} collective-permute-done((bf16[4,1024,128]{2,1,0:T(8,128)(2,1)S(1)}, bf16[4,1024,128]{2,1,0:T(8,128)(2,1)S(1)}, u32[]{:S(2)}, u32[]{:S(2)}) %collective-permute-start.6) | collective-permute-done | bytes 1048608 | tf_op jit(solution)/shard_map/ppermute | solution.py:590
  118.4 1.0 shard_map.79
  (6 shorter events, 0.0 us)
Async XLA Ops:
  0.8 15.5 %collective-permute-start = (f32[16,256]{1,0:T(8,128)S(1)}, f32[16,256]{1,0:T(8,128)S(1)}, u32[]{:S(2)}, u32[]{:S(2)}) collective-permute-start(f32[16,256]{1,0:T(8,128)S(1)} %bitcast_select_fusion), channel_id=1, source_target_pairs={{4,8},{12,16},{20,24},{28,32},{36,40},{44,48},{52,56},{60,64},{68,... | collective-permute-start | bytes 49160 | tf_op jit(solution)/shard_map/ppermute | solution.py:597
  3.3 51.0 %collective-permute-start.3 = (bf16[3,1024,128]{2,1,0:T(8,128)(2,1)S(1)}, bf16[3,1024,128]{2,1,0:T(8,128)(2,1)}, u32[]{:S(2)}, u32[]{:S(2)}) collective-permute-start(bf16[3,1024,128]{2,1,0:T(8,128)(2,1)S(1)} %shard_map.74), channel_id=1, source_target_pairs={{0,4},{4,0},{8,12},{12,8},{16,20},{20,16},{24,28},{28,24},{32,36},... | collective-permute-start | bytes 2359304 | tf_op jit(solution)/shard_map/ppermute | solution.py:590
  8.0 7.6 %copy-start.8 = (s32[1,1,16]{2,1,0:T(1,128)S(1)}, s32[1,1,16]{2,1,0:T(1,128)}, u32[]{:S(2)}) copy-start(s32[1,1,16]{2,1,0:T(1,128)} %param.10) | copy-start | bytes 196
  8.0 7.6 %copy-start.9 = (f32[3]{0:T(128)S(1)}, f32[3]{0:T(128)}, u32[]{:S(2)}) copy-start(f32[3]{0:T(128)} %param.13) | copy-start | bytes 40
  8.0 9.8 %copy-start.7 = (f32[2]{0:T(128)S(1)}, f32[2]{0:T(128)}, u32[]{:S(2)}) copy-start(f32[2]{0:T(128)} %param.12) | copy-start | bytes 28
  8.0 46.0 %copy-start.5 = (f32[1,1,16,256]{3,2,1,0:T(8,128)S(1)}, f32[1,1,16,256]{3,2,1,0:T(8,128)}, u32[]{:S(2)}) copy-start(f32[1,1,16,256]{3,2,1,0:T(8,128)} %param.8) | copy-start | bytes 49156
  8.0 46.0 %copy-start.6 = (s32[1,1,16]{2,1,0:T(1,128)S(1)}, s32[1,1,16]{2,1,0:T(1,128)}, u32[]{:S(2)}) copy-start(s32[1,1,16]{2,1,0:T(1,128)} %param.9) | copy-start | bytes 196
  12.2 1.0 copy-start
  13.2 1.0 copy-start.2
  14.1 40.1 %collective-permute-start.4 = (bf16[1,1024,128]{2,1,0:T(8,128)(2,1)}, bf16[1,1024,128]{2,1,0:T(8,128)(2,1)}, u32[]{:S(2)}, u32[]{:S(2)}) collective-permute-start(bf16[1,1024,128]{2,1,0:T(8,128)(2,1)} %get-tuple-element.26), channel_id=1, source_target_pairs={{0,4},{4,0},{8,12},{12,8},{16,20},{20,16},{24,28},{28,24},{32,36},... | collective-permute-start | bytes 786440 | tf_op jit(solution)/shard_map/ppermute | solution.py:590
  14.1 46.4 %collective-permute-start.5 = (bf16[1,1024,128]{2,1,0:T(8,128)(2,1)}, bf16[1,1024,128]{2,1,0:T(8,128)(2,1)}, u32[]{:S(2)}, u32[]{:S(2)}) collective-permute-start(bf16[1,1024,128]{2,1,0:T(8,128)(2,1)} %get-tuple-element.29), channel_id=1, source_target_pairs={{0,4},{4,0},{8,12},{12,8},{16,20},{20,16},{24,28},{28,24},{32,36},... | collective-permute-start | bytes 786440 | tf_op jit(solution)/shard_map/ppermute | solution.py:590
  15.6 60.4 %collective-permute-start.2 = (bf16[3,1024,128]{2,1,0:T(8,128)(2,1)}, bf16[3,1024,128]{2,1,0:T(8,128)(2,1)}, u32[]{:S(2)}, u32[]{:S(2)}) collective-permute-start(bf16[3,1024,128]{2,1,0:T(8,128)(2,1)} %get-tuple-element.23), channel_id=1, source_target_pairs={{0,4},{4,0},{8,12},{12,8},{16,20},{20,16},{24,28},{28,24},{32,36},... | collective-permute-start | bytes 2359304 | tf_op jit(solution)/shard_map/ppermute | solution.py:590
  16.3 37.8 %collective-permute-start.1 = (f32[40,256]{1,0:T(8,128)S(1)}, f32[40,256]{1,0:T(8,128)S(1)}, u32[]{:S(2)}, u32[]{:S(2)}) collective-permute-start(f32[40,256]{1,0:T(8,128)S(1)} %select_maximum_fusion.2), channel_id=1, source_target_pairs={{0,4},{4,0},{8,12},{12,8},{16,20},{20,16},{24,28},{28,24},{32,36},... | collective-permute-start | bytes 122888 | tf_op jit(solution)/shard_map/ppermute | solution.py:590
  54.3 1.2 %copy-start.3 = (bf16[4,512,256]{2,1,0:T(8,128)(2,1)S(1)}, bf16[4,512,256]{2,1,0:T(8,128)(2,1)}, u32[]{:S(2)}) copy-start(bf16[4,512,256]{2,1,0:T(8,128)(2,1)} %copy-done.2) | copy-start | bytes 3145732
  55.5 5.0 %copy-start.4 = (bf16[4,512,256]{2,1,0:T(8,128)(2,1)S(1)}, bf16[4,512,256]{2,1,0:T(8,128)(2,1)}, u32[]{:S(2)}) copy-start(bf16[4,512,256]{2,1,0:T(8,128)(2,1)} %copy-done.2) | copy-start | bytes 3145732
  60.5 15.5 %copy-start.1 = (bf16[4,512,256]{2,1,0:T(8,128)(2,1)S(1)}, bf16[4,512,256]{2,1,0:T(8,128)(2,1)}, u32[]{:S(2)}) copy-start(bf16[4,512,256]{2,1,0:T(8,128)(2,1)} %copy-done) | copy-start | bytes 3145732
  74.6 20.7 %collective-permute-start.7 = (bf16[3584,128]{1,0:T(8,128)(2,1)S(1)}, bf16[3584,128]{1,0:T(8,128)(2,1)S(1)}, u32[]{:S(2)}, u32[]{:S(2)}) collective-permute-start(bf16[3584,128]{1,0:T(8,128)(2,1)S(1)} %get-tuple-element.36), channel_id=1, source_target_pairs={{0,4},{4,0},{8,12},{12,8},{16,20},{20,16},{24,28},{28,24},{32,36},... | collective-permute-start | bytes 2752520 | tf_op jit(solution)/shard_map/ppermute | solution.py:590
  93.3 25.1 %collective-permute-start.6 = (bf16[4,1024,128]{2,1,0:T(8,128)(2,1)S(1)}, bf16[4,1024,128]{2,1,0:T(8,128)(2,1)S(1)}, u32[]{:S(2)}, u32[]{:S(2)}) collective-permute-start(bf16[4,1024,128]{2,1,0:T(8,128)(2,1)S(1)} %get-tuple-element.35), channel_id=1, source_target_pairs={{0,4},{4,0},{8,12},{12,8},{16,20},{20,16},{24,28},{28,24},{32,36},... | collective-permute-start | bytes 3145736 | tf_op jit(solution)/shard_map/ppermute | solution.py:590

commit v6 on v5

--- a/solution.py
+++ b/solution.py
@@ -232,7 +232,8 @@
         left_site = left_wide[...]
         right_site = right_wide[...]
         if not halved:
-            msg[b] = jnp.where(is_right, left_site, right_site).astype(bf16)
+            target = msg[0].at[b] if b + 1 < BATCH else msg[1].at[0]
+            target[...] = jnp.where(is_right, left_site, right_site).astype(bf16)
         elif b + 1 < BATCH:
             lines = slice(b * 4 * SIZE, (b + 1) * 4 * SIZE)
             msg[lines, :] = jnp.where(is_right, left_site, right_site).astype(bf16)
@@ -328,7 +329,7 @@
 
 
 def second_kernel(role, gates, kept, own, got, scale, sketch, *refs):
-    (edge, carry, _, msg, out, merge), refs = refs[:6], refs[6:]
+    (edge, carry, _, msg, msg_last, out, merge), refs = refs[:7], refs[7:]
     left_w, right_w, mixed, samp, gram, scaled, a_ref, x_ref, wide = refs[:9]
     ready, sems = refs[9:]
 
@@ -362,7 +363,15 @@
     solve([gram.at[b] for b in every], [samp.at[b] for b in every], scaled, a_ref, x_ref)
     scaled[BATCH, LOWER, :] = carry[0]
     copies = deliver(
-        role, scaled, [mixed.at[b] for b in every], wide, ready, msg, out, sems, False
+        role,
+        scaled,
+        [mixed.at[b] for b in every],
+        wide,
+        ready,
+        (msg, msg_last),
+        out,
+        sems,
+        False,
     )
     used = jnp.where(role[0] == 1, 0.0, 1.0)
     for jb in range(2):
@@ -453,8 +462,13 @@
         second_kernel,
         (role, gates, kept, own, got, scale, sketch, edge, carry, out),
         [SMEM] * 3 + [VMEM] * 6 + [HBM],
-        [shaped(BATCH, *SECTOR), pltpu.HBM((16, *SECTOR), bf16), shaped(*SECTOR)],
-        [VMEM, HBM, VMEM],
+        [
+            shaped(BATCH - 1, *SECTOR),
+            shaped(1, *SECTOR),
+            pltpu.HBM((16, *SECTOR), bf16),
+            shaped(*SECTOR),
+        ],
+        [VMEM, VMEM, HBM, VMEM],
         [pltpu.VMEM((6, 2, SIZE, SIZE), bf16), pltpu.VMEM((6, 2, SIZE, SIZE), bf16)]
         + sample_shapes(pltpu.VMEM, BATCH)
         + factor_scratch()
@@ -462,7 +476,7 @@
             pltpu.VMEM((BATCH, *SECTOR), bf16),
             pltpu.SemaphoreType.DMA((BATCH,)),
         ],
-        aliases={9: 1},
+        aliases={9: 2},
     )
 
 
@@ -630,14 +644,16 @@
     parts = early(role_a, gates, kept, own_a, got_0, got_a, scale, sketch_a)
     msg_a, out, carry = first_half(role_a, gates, kept, own_a, got_low, scale, sketch_a, parts)
     back_a = swapped(msg_a)
-    msg_b, out, merge = second_half(
+    msg_b, msg_last, out, merge = second_half(
         role_b, gates, kept, own_b, got_b, scale, sketch_b, parts[3], carry, out
     )
     back_b = swapped(msg_b)
+    back_last = swapped(msg_last)
 
     back_at = 8 * flag
     out = place(out, back_a, back_at + 4, merge)
     out = place(out, back_b, back_at)
+    out = place(out, back_last, back_at + BATCH - 1)
     return from_lines(out)[None, None]
 
 

time: 120 us -> 122 us (1.017)
  Pallas kernels: 43.5 us -> 44.8 us
    ppermute x7 -> x8, waiting for transfers between devices: 59.3 us -> 52 us  [swapped(): return lax.ppermute(value, 'chain', [(i, i ^ 1) for i in range(chain)])]
    ppermute x1, waiting for transfers between devices: 0.01 us -> 6.31 us  [onward(): return lax.ppermute(value, ('chain', 'group'), pairs)]
    pallas_call x7 -> x8, Pallas kernels: 43.5 us -> 44.8 us  [run(): pl.pallas_call(kernel, out_shape=outs, in_specs=specs, out_specs=out_spec...]
    unnamed x20 -> x24, local copies, waits for them, and re-layouts: 3.21 us -> 4.2 us
    ppermute x7 -> x8, starting transfers between devices: 9.6 us -> 9.63 us  [swapped(): return lax.ppermute(value, 'chain', [(i, i ^ 1) for i in range(chain)])]
  transfers between devices with their start and end apart: 8 -> 9, of which waited for: 3 -> 4; matrix products, arithmetic and copies ran while one was open for 1% -> 1% of each run, Pallas kernels for 36% -> 33%
where the time goes in v6:
time: 122 us; the launch traced here: 120 us
  waiting for transfers between devices  58.3 us (48%)
  Pallas kernels  44.8 us (37%)
  starting transfers between devices  10.9 us (9%)
  local copies, waits for them, and re-layouts  4.9 us (4%)
    ppermute x8, waiting for transfers between devices, swapped(): return lax.ppermute(value, 'chain', [(i, i ^ 1) for i in range(chain)])  52 us
    pallas_call x8, Pallas kernels, run(): pl.pallas_call(kernel, out_shape=outs, in_specs=specs, out_specs=out_spec...  44.8 us
    ppermute x8, starting transfers between devices, swapped(): return lax.ppermute(value, 'chain', [(i, i ^ 1) for i in range(chain)])  9.63 us
    ppermute x1, waiting for transfers between devices, onward(): return lax.ppermute(value, ('chain', 'group'), pairs)  6.31 us
    unnamed x24, local copies, waits for them, and re-layouts  4.2 us
  transfers between devices with their start and end apart: 9, of which 4 were waited for; matrix products, arithmetic and copies ran while one was open for 1% of the time, Pallas kernels for 33%

profile of v6, /device:TPU:1, one launch (start us, length us, event | category | flops | bytes accessed | tf_op | source)
XLA Modules:
  0.0 120.3 jit_solution(1571334521093831526)
XLA Ops:
  0.0 4.1 %shard_map.73 = (bf16[1,1024,128]{2,1,0:T(8,128)(2,1)}, bf16[1,1024,128]{2,1,0:T(8,128)(2,1)}, bf16[3,1024,128]{2,1,0:T(8,128)(2,1)}, bf16[6,1024,128]{2,1,0:T(8...) custom-call(s32[1]{0:T(128)} %bitcast.1.role, ...), custom_call_target="tpu_custom_call" | custom-call | flops 1000000000 | bytes 8000000 | tf_op jit(solution)/shard_map/pallas_call | solution.py:395
  4.1 0.0 copy-start
  4.1 1.0 copy-done
  5.1 0.0 copy-start.2
  5.1 1.0 copy-done.2
  6.1 0.0 copy-start.4
  6.1 1.0 copy-done.4
  7.0 0.0 copy-start.7
  7.0 0.0 copy-start.8
  7.0 0.0 copy-start.10
  7.0 0.0 copy-start.11
  7.0 0.0 copy-start.9
  7.1 2.5 %collective-permute-start.4 = (bf16[1,1024,128]{2,1,0:T(8,128)(2,1)}, bf16[1,1024,128]{2,1,0:T(8,128)(2,1)}, u32[]{:S(2)}, u32[]{:S(2)}) collective-permute-start(bf16[1,1024,128]{2,1,0:T(8,128)(2,1)} %get-tuple-element.27), channel_id=1, source_target_pairs={{0,4},{4,0},{8,12},{12,8},{16,20},{20,16},{24,28},{28,24},{32,36},... | collective-permute-start | bytes 786440 | tf_op jit(solution)/shard_map/ppermute | solution.py:604
  9.5 1.1 shard_map.74
  10.7 0.1 collective-permute-start.3
  10.8 0.0 copy-done.7
  10.8 0.0 copy-done.8
  10.8 0.1 bitcast_select_fusion
  10.9 1.3 %collective-permute-start = (f32[16,256]{1,0:T(8,128)S(1)}, f32[16,256]{1,0:T(8,128)S(1)}, u32[]{:S(2)}, u32[]{:S(2)}) collective-permute-start(f32[16,256]{1,0:T(8,128)S(1)} %bitcast_select_fusion), channel_id=1, source_target_pairs={{4,8},{12,16},{20,24},{28,32},{36,40},{44,48},{52,56},{60,64},{68,... | collective-permute-start | bytes 49160 | tf_op jit(solution)/shard_map/ppermute | solution.py:611
  12.2 3.8 %collective-permute-start.5 = (bf16[1,1024,128]{2,1,0:T(8,128)(2,1)}, bf16[1,1024,128]{2,1,0:T(8,128)(2,1)}, u32[]{:S(2)}, u32[]{:S(2)}) collective-permute-start(bf16[1,1024,128]{2,1,0:T(8,128)(2,1)} %get-tuple-element.30), channel_id=1, source_target_pairs={{0,4},{4,0},{8,12},{12,8},{16,20},{20,16},{24,28},{28,24},{32,36},... | collective-permute-start | bytes 786440 | tf_op jit(solution)/shard_map/ppermute | solution.py:604
  16.0 0.1 collective-permute-start.2
  16.1 0.0 copy-done.10
  16.1 0.0 copy-done.11
  16.1 0.1 pad_add_fusion
  16.2 0.7 slice.18
  16.8 6.3 %collective-permute-done = f32[16,256]{1,0:T(8,128)S(1)} collective-permute-done((f32[16,256]{1,0:T(8,128)S(1)}, f32[16,256]{1,0:T(8,128)S(1)}, u32[]{:S(2)}, u32[]{:S(2)}) %collective-permute-start) | collective-permute-done | bytes 16416 | tf_op jit(solution)/shard_map/ppermute | solution.py:611
  23.2 0.1 collective-permute-start.1
  23.2 0.0 copy-done.9
  23.3 0.7 pad_maximum_fusion.gates
  24.0 32.0 %collective-permute-done.1 = f32[40,256]{1,0:T(8,128)S(1)} collective-permute-done((f32[40,256]{1,0:T(8,128)S(1)}, f32[40,256]{1,0:T(8,128)S(1)}, u32[]{:S(2)}, u32[]{:S(2)}) %collective-permute-start.1) | collective-permute-done | bytes 40992 | tf_op jit(solution)/shard_map/ppermute | solution.py:604
  56.0 0.1 select_bitcast_fusion.1
  56.1 0.1 broadcast_in_dim.8.scale
  56.2 0.0 collective-permute-done.4.got
  56.2 0.0 collective-permute-done.3.got_0
  56.2 0.0 copy-start.5
  56.2 1.2 %copy-done.5 = bf16[4,512,256]{2,1,0:T(8,128)(2,1)S(1)} copy-done((bf16[4,512,256]{2,1,0:T(8,128)(2,1)S(1)}, bf16[4,512,256]{2,1,0:T(8,128)(2,1)}, u32[]{:S(2)}) %copy-start.5) | copy-done | bytes 1048600
  57.4 0.0 copy-start.6
  57.4 4.8 %shard_map.75 = (bf16[3,512,512]{2,1,0:T(8,128)(2,1)S(1)}, bf16[3,2,512,256]{3,2,1,0:T(8,128)(2,1)S(1)}, f32[3,256,256]{2,1,0:T(8,128)S(1)}, bf16[6,256,256]{2,1,0:T(8,128)(2,1)S(1)}) custom-call(s32[2]{0:T(128)S(1)} %get-tuple-element.45.role, f32[5]{0:T(128)S(1)} %pad_maximum_fusion.gates, s32[16]{0:T(128)S(1)} %fusion.2.kept, ...), custom_call_target="tpu_custom_call" | custom-call | flops 10000000000 | bytes 8000000 | tf_op jit(solution)/shard_map/pallas_call | solution.py:395
  62.2 0.0 collective-permute-done.5.got
  62.2 0.0 copy-done.6
  62.2 0.0 copy-start.1
  62.2 0.0 copy-start.3
  62.2 14.1 %shard_map.76 = (bf16[3584,128]{1,0:T(8,128)(2,1)S(1)}, bf16[16,1024,128]{2,1,0:T(8,128)(2,1)}, bf16[5,256,256]{2,1,0:T(8,128)(2,1)S(1)}) custom-call(s32[2]{0:T(128)S(1)} %get-tuple-element.45.role, f32[5]{0:T(128)S(1)} %pad_maximum_fusion.gates, s32[16]{0:T(128)S(1)} %fusion.2.kept, bf16[6,1024,128]{2,1,0:T(8,128)(2,1)S(1)} %get-tuple-element.26.own, ...), custom_call_target="tpu_custom_call" | custom-call | flops 10000000000 | bytes 8000000 | tf_op jit(solution)/shard_map/pallas_call | solution.py:395
  76.3 1.5 %collective-permute-start.8 = (bf16[3584,128]{1,0:T(8,128)(2,1)S(1)}, bf16[3584,128]{1,0:T(8,128)(2,1)S(1)}, u32[]{:S(2)}, u32[]{:S(2)}) collective-permute-start(bf16[3584,128]{1,0:T(8,128)(2,1)S(1)} %get-tuple-element.38), channel_id=1, source_target_pairs={{0,4},{4,0},{8,12},{12,8},{16,20},{20,16},{24,28},{28,24},{32,36},... | collective-permute-start | bytes 2752520 | tf_op jit(solution)/shard_map/ppermute | solution.py:604
  77.8 0.0 collective-permute-done.2.got
  77.8 0.0 copy-done.1
  77.8 0.0 copy-done.3
  77.8 18.2 %shard_map.77 = (bf16[3,1024,128]{2,1,0:T(8,128)(2,1)}, bf16[1,1024,128]{2,1,0:T(8,128)(2,1)S(1)}, bf16[16,1024,128]{2,1,0:T(8,128)(2,1)}, bf16[1024,128]{1,0:T(8,128)(2,1)S(1)}) custom-call(s32[2]{0:T(128)S(1)} %get-tuple-element.44.role, f32[5]{0:T(128)S(1)} %pad_maximum_fusion.gates, s32[16]{0:T(128)S(1)} %fusion.2.kept, ...), custom_call_target="tpu_custom_call", output_to_operand_aliasing={{2}: (9, {})} | custom-call | flops 10000000000 | bytes 8000000 | tf_op jit(solution)/shard_map/pallas_call | solution.py:395
  96.0 0.3 collective-permute-start.7
  96.3 1.2 %collective-permute-start.6 = (bf16[1,1024,128]{2,1,0:T(8,128)(2,1)S(1)}, bf16[1,1024,128]{2,1,0:T(8,128)(2,1)S(1)}, u32[]{:S(2)}, u32[]{:S(2)}) collective-permute-start(bf16[1,1024,128]{2,1,0:T(8,128)(2,1)S(1)} %get-tuple-element.36), channel_id=1, source_target_pairs={{0,4},{4,0},{8,12},{12,8},{16,20},{20,16},{24,28},{28,24},{32,36},... | collective-permute-start | bytes 786440 | tf_op jit(solution)/shard_map/ppermute | solution.py:604
  97.5 0.0 collective-permute-done.8.block
  97.5 1.0 shard_map.78._
  98.5 15.4 %collective-permute-done.7.block = bf16[3,1024,128]{2,1,0:T(8,128)(2,1)S(1)} collective-permute-done((bf16[3,1024,128]{2,1,0:T(8,128)(2,1)}, bf16[3,1024,128]{2,1,0:T(8,128)(2,1)S(1)}, u32[]{:S(2)}, u32[]{:S(2)}) %collective-permute-start.7) | collective-permute-done | bytes 786464 | tf_op jit(solution)/shard_map/ppermute | solution.py:604
  113.9 0.9 shard_map.79._
  114.8 4.6 %collective-permute-done.6.block = bf16[1,1024,128]{2,1,0:T(8,128)(2,1)S(1)} collective-permute-done((bf16[1,1024,128]{2,1,0:T(8,128)(2,1)S(1)}, bf16[1,1024,128]{2,1,0:T(8,128)(2,1)S(1)}, u32[]{:S(2)}, u32[]{:S(2)}) %collective-permute-start.6) | collective-permute-done | bytes 262176 | tf_op jit(solution)/shard_map/ppermute | solution.py:604
  119.4 0.7 shard_map.80
  (6 shorter events, 0.0 us)
Async XLA Ops:
  4.1 1.0 copy-start
  5.1 1.0 copy-start.2
  6.1 1.0 copy-start.4
  7.0 3.7 %copy-start.7 = (f32[1,1,16,256]{3,2,1,0:T(8,128)S(1)}, f32[1,1,16,256]{3,2,1,0:T(8,128)}, u32[]{:S(2)}) copy-start(f32[1,1,16,256]{3,2,1,0:T(8,128)} %param.8) | copy-start | bytes 49156
  7.0 3.7 %copy-start.8 = (s32[1,1,16]{2,1,0:T(1,128)S(1)}, s32[1,1,16]{2,1,0:T(1,128)}, u32[]{:S(2)}) copy-start(s32[1,1,16]{2,1,0:T(1,128)} %param.9) | copy-start | bytes 196
  7.0 9.0 %copy-start.10 = (s32[1,1,16]{2,1,0:T(1,128)S(1)}, s32[1,1,16]{2,1,0:T(1,128)}, u32[]{:S(2)}) copy-start(s32[1,1,16]{2,1,0:T(1,128)} %param.10) | copy-start | bytes 196
  7.0 9.0 %copy-start.11 = (f32[3]{0:T(128)S(1)}, f32[3]{0:T(128)}, u32[]{:S(2)}) copy-start(f32[3]{0:T(128)} %param.13) | copy-start | bytes 40
  7.0 16.2 %copy-start.9 = (f32[2]{0:T(128)S(1)}, f32[2]{0:T(128)}, u32[]{:S(2)}) copy-start(f32[2]{0:T(128)} %param.12) | copy-start | bytes 28
  7.1 49.1 %collective-permute-start.4 = (bf16[1,1024,128]{2,1,0:T(8,128)(2,1)}, bf16[1,1024,128]{2,1,0:T(8,128)(2,1)}, u32[]{:S(2)}, u32[]{:S(2)}) collective-permute-start(bf16[1,1024,128]{2,1,0:T(8,128)(2,1)} %get-tuple-element.27), channel_id=1, source_target_pairs={{0,4},{4,0},{8,12},{12,8},{16,20},{20,16},{24,28},{28,24},{32,36},... | collective-permute-start | bytes 786440 | tf_op jit(solution)/shard_map/ppermute | solution.py:604
  10.7 45.5 %collective-permute-start.3 = (bf16[3,1024,128]{2,1,0:T(8,128)(2,1)S(1)}, bf16[3,1024,128]{2,1,0:T(8,128)(2,1)S(1)}, u32[]{:S(2)}, u32[]{:S(2)}) collective-permute-start(bf16[3,1024,128]{2,1,0:T(8,128)(2,1)S(1)} %shard_map.74), channel_id=1, source_target_pairs={{0,4},{4,0},{8,12},{12,8},{16,20},{20,16},{24,28},{28,24},{32,36},... | collective-permute-start | bytes 2359304 | tf_op jit(solution)/shard_map/ppermute | solution.py:604
  10.9 12.3 %collective-permute-start = (f32[16,256]{1,0:T(8,128)S(1)}, f32[16,256]{1,0:T(8,128)S(1)}, u32[]{:S(2)}, u32[]{:S(2)}) collective-permute-start(f32[16,256]{1,0:T(8,128)S(1)} %bitcast_select_fusion), channel_id=1, source_target_pairs={{4,8},{12,16},{20,24},{28,32},{36,40},{44,48},{52,56},{60,64},{68,... | collective-permute-start | bytes 49160 | tf_op jit(solution)/shard_map/ppermute | solution.py:611
  12.2 50.0 %collective-permute-start.5 = (bf16[1,1024,128]{2,1,0:T(8,128)(2,1)}, bf16[1,1024,128]{2,1,0:T(8,128)(2,1)}, u32[]{:S(2)}, u32[]{:S(2)}) collective-permute-start(bf16[1,1024,128]{2,1,0:T(8,128)(2,1)} %get-tuple-element.30), channel_id=1, source_target_pairs={{0,4},{4,0},{8,12},{12,8},{16,20},{20,16},{24,28},{28,24},{32,36},... | collective-permute-start | bytes 786440 | tf_op jit(solution)/shard_map/ppermute | solution.py:604
  16.0 61.8 %collective-permute-start.2 = (bf16[3,1024,128]{2,1,0:T(8,128)(2,1)}, bf16[3,1024,128]{2,1,0:T(8,128)(2,1)}, u32[]{:S(2)}, u32[]{:S(2)}) collective-permute-start(bf16[3,1024,128]{2,1,0:T(8,128)(2,1)} %get-tuple-element.24), channel_id=1, source_target_pairs={{0,4},{4,0},{8,12},{12,8},{16,20},{20,16},{24,28},{28,24},{32,36},... | collective-permute-start | bytes 2359304 | tf_op jit(solution)/shard_map/ppermute | solution.py:604
  23.2 32.8 %collective-permute-start.1 = (f32[40,256]{1,0:T(8,128)S(1)}, f32[40,256]{1,0:T(8,128)S(1)}, u32[]{:S(2)}, u32[]{:S(2)}) collective-permute-start(f32[40,256]{1,0:T(8,128)S(1)} %select_maximum_fusion.2), channel_id=1, source_target_pairs={{0,4},{4,0},{8,12},{12,8},{16,20},{20,16},{24,28},{28,24},{32,36},... | collective-permute-start | bytes 122888 | tf_op jit(solution)/shard_map/ppermute | solution.py:604
  56.2 1.2 %copy-start.5 = (bf16[4,512,256]{2,1,0:T(8,128)(2,1)S(1)}, bf16[4,512,256]{2,1,0:T(8,128)(2,1)}, u32[]{:S(2)}) copy-start(bf16[4,512,256]{2,1,0:T(8,128)(2,1)} %copy-done.4) | copy-start | bytes 3145732
  57.4 4.8 %copy-start.6 = (bf16[4,512,256]{2,1,0:T(8,128)(2,1)S(1)}, bf16[4,512,256]{2,1,0:T(8,128)(2,1)}, u32[]{:S(2)}) copy-start(bf16[4,512,256]{2,1,0:T(8,128)(2,1)} %copy-done.4) | copy-start | bytes 3145732
  62.2 15.6 %copy-start.1 = (bf16[4,1024,128]{2,1,0:T(8,128)(2,1)S(1)}, bf16[4,1024,128]{2,1,0:T(8,128)(2,1)}, u32[]{:S(2)}) copy-start(bf16[4,1024,128]{2,1,0:T(8,128)(2,1)} %copy-done) | copy-start | bytes 3145732
  62.2 15.6 %copy-start.3 = (bf16[4,512,256]{2,1,0:T(8,128)(2,1)S(1)}, bf16[4,512,256]{2,1,0:T(8,128)(2,1)}, u32[]{:S(2)}) copy-start(bf16[4,512,256]{2,1,0:T(8,128)(2,1)} %copy-done.2) | copy-start | bytes 3145732
  76.3 21.2 %collective-permute-start.8 = (bf16[3584,128]{1,0:T(8,128)(2,1)S(1)}, bf16[3584,128]{1,0:T(8,128)(2,1)S(1)}, u32[]{:S(2)}, u32[]{:S(2)}) collective-permute-start(bf16[3584,128]{1,0:T(8,128)(2,1)S(1)} %get-tuple-element.38), channel_id=1, source_target_pairs={{0,4},{4,0},{8,12},{12,8},{16,20},{20,16},{24,28},{28,24},{32,36},... | collective-permute-start | bytes 2752520 | tf_op jit(solution)/shard_map/ppermute | solution.py:604
  96.0 17.9 %collective-permute-start.7 = (bf16[3,1024,128]{2,1,0:T(8,128)(2,1)}, bf16[3,1024,128]{2,1,0:T(8,128)(2,1)S(1)}, u32[]{:S(2)}, u32[]{:S(2)}) collective-permute-start(bf16[3,1024,128]{2,1,0:T(8,128)(2,1)} %get-tuple-element.37), channel_id=1, source_target_pairs={{0,4},{4,0},{8,12},{12,8},{16,20},{20,16},{24,28},{28,24},{32,36},... | collective-permute-start | bytes 2359304 | tf_op jit(solution)/shard_map/ppermute | solution.py:604
  96.3 23.2 %collective-permute-start.6 = (bf16[1,1024,128]{2,1,0:T(8,128)(2,1)S(1)}, bf16[1,1024,128]{2,1,0:T(8,128)(2,1)S(1)}, u32[]{:S(2)}, u32[]{:S(2)}) collective-permute-start(bf16[1,1024,128]{2,1,0:T(8,128)(2,1)S(1)} %get-tuple-element.36), channel_id=1, source_target_pairs={{0,4},{4,0},{8,12},{12,8},{16,20},{20,16},{24,28},{28,24},{32,36},... | collective-permute-start | bytes 786440 | tf_op jit(solution)/shard_map/ppermute | solution.py:604
